TPU v7x, 32 devices: a whole 2x2x4 slice. The times are simulated.
32 devices in a mesh: ctx: 8 (over y, x, core), fsdp: 4 (over z).
Axes of the slice: x: 2, y: 2, z: 4, core: 2. Of those that a mesh axis runs over, the one named last changes fastest.
Arguments:
- hidden_in: bfloat16 [4, 2048, 768], P('fsdp', 'ctx'), may hold values from -6 to 6
- norm1_gain: bfloat16 [768], P('fsdp'), may hold values from 0.099609375 to 1.8984375
- attention_norm_bias: bfloat16 [768], P('fsdp'), may hold values from -1.5 to 1.5
- qkv_weight: bfloat16 [768, 2304], P('fsdp'), as said below
- qkv_bias: bfloat16 [2304], P('fsdp'), may hold values from -0.29882812 to 0.29882812
- out_weight: bfloat16 [768, 768], P('fsdp'), may hold values from -1.75 to 1.75
- out_bias: bfloat16 [768], P('fsdp'), may hold values from -1.5 to 1.5
- norm2_gain: bfloat16 [768], P('fsdp'), may hold values from 0.099609375 to 1.8984375
- feedforward_norm_bias: bfloat16 [768], P('fsdp'), may hold values from -1.5 to 1.5
- up_weight: bfloat16 [768, 3072], P('fsdp'), may hold values from -0.21875 to 0.21875
- up_bias: bfloat16 [3072], P('fsdp'), may hold values from -2.5 to 2.5
- down_weight: bfloat16 [3072, 768], P('fsdp'), may hold values from -0.109375 to 0.109375
- down_bias: bfloat16 [768], P('fsdp'), may hold values from -1.5 to 1.5
- cotangent: bfloat16 [4, 2048, 768], P('fsdp', 'ctx'), may hold values from -6 to 6
- block_order: int32 [16], replicated, may hold values from 0 to 15, as said below
Outputs:
- hidden_out: bfloat16 [4, 2048, 768], P('fsdp', 'ctx')
- hidden_grad: float32 [4, 2048, 768], P('fsdp', 'ctx')
- grad_norm1_gain: float32 [768], P('fsdp')
- grad_norm1_shift: float32 [768], P('fsdp')
- grad_qkv_weight: float32 [768, 2304], P('fsdp')
- grad_qkv_bias: float32 [2304], P('fsdp')
- grad_out_weight: float32 [768, 768], P('fsdp')
- grad_out_bias: float32 [768], P('fsdp')
- grad_norm2_gain: float32 [768], P('fsdp')
- grad_norm2_shift: float32 [768], P('fsdp')
- grad_up_weight: float32 [768, 3072], P('fsdp')
- grad_up_bias: float32 [3072], P('fsdp')
- grad_down_weight: float32 [3072, 768], P('fsdp')
- grad_down_bias: float32 [768], P('fsdp')
Inputs may be any that keep to these rules, and one draw needn't show every extreme that they name: `qkv_weight`: the query, key and value projections side by side. `block_order`: each block number appears once; entries 2 j and 2 j + 1 are b and 15 - b.
All inputs are finite; a program needn't handle non-finite values.
Results may differ from a plain program's by a relative error of at most 0.014.
Values may be sent and summed in bfloat16 or wider, within the bound.
A program may use at most 192 MiB of HBM per device.

v0:
```python
import math

import jax
import jax.numpy as jnp
from jax import lax
from jax.sharding import PartitionSpec as P

H = 12
HD = 64
ROT = 16
BLK = 128


EPS = 1e-05
NEG = -1e30
SQRT_HALF = 0.7071067811865476
INV_ROOT_TWO_PI = 0.3989422804014327


def apply_layer_norm(values_in, norm_gain, norm_bias):
    centre = jnp.mean(values_in, axis=-1, keepdims=True)
    mean_removed = values_in - centre
    inverse_deviation = lax.rsqrt(
        jnp.mean(mean_removed * mean_removed, axis=-1, keepdims=True) + EPS
    )
    standardized = mean_removed * inverse_deviation
    return (standardized * norm_gain + norm_bias, standardized, inverse_deviation)


def layer_norm_backward(output_gradient, standardized, inverse_deviation, norm_gain):
    gain_scaled = output_gradient * norm_gain
    return inverse_deviation * (
        gain_scaled
        - jnp.mean(gain_scaled, axis=-1, keepdims=True)
        - standardized * jnp.mean(gain_scaled * standardized, axis=-1, keepdims=True)
    )


def gelu_exact(values_in):
    return 0.5 * values_in * (1.0 + lax.erf(values_in * SQRT_HALF))


def gelu_slope(values_in):
    return (
        0.5 * (1.0 + lax.erf(values_in * SQRT_HALF))
        + values_in * jnp.exp(-0.5 * values_in * values_in) * INV_ROOT_TWO_PI
    )


def rotary_tables(position_list):
    half_rot = ROT // 2
    inverse = jnp.power(jnp.float32(10000.0), -2.0 * jnp.arange(half_rot, dtype=jnp.float32) / ROT)
    angle = position_list.astype(jnp.float32)[:, None] * inverse[None, :]
    return (jnp.cos(angle)[:, None, :], jnp.sin(angle)[:, None, :])


def rotate(tensor, cosine, sine):
    half_rot = ROT // 2
    first_half = tensor[..., :half_rot]
    second_half = tensor[..., half_rot:ROT]
    return jnp.concatenate(
        [
            first_half * cosine - second_half * sine,
            second_half * cosine + first_half * sine,
            tensor[..., ROT:],
        ],
        axis=-1,
    )


def rotate_back(tensor, cosine, sine):
    half_rot = ROT // 2
    first_half = tensor[..., :half_rot]
    second_half = tensor[..., half_rot:ROT]
    return jnp.concatenate(
        [
            first_half * cosine + second_half * sine,
            second_half * cosine - first_half * sine,
            tensor[..., ROT:],
        ],
        axis=-1,
    )


def masked_logits(query_block, key_block, query_pos, key_pos):
    logits = jnp.einsum(
        "qhd,khd->hqk", query_block, key_block, preferred_element_type=jnp.float32
    ) * (1.0 / math.sqrt(HD))
    return jnp.where(key_pos[None, None, :] <= query_pos[None, :, None], logits, NEG)


def block_terms(
    query_block, dout_block, total_t, delta_t, query_pos, key_block, value_block, key_pos
):
    logits = masked_logits(query_block, key_block, query_pos, key_pos)
    probs_wide = jnp.exp(logits - total_t[:, :, None])
    dprobs = jnp.einsum("qhd,khd->hqk", dout_block, value_block, preferred_element_type=jnp.float32)
    d_logits = (probs_wide * (dprobs - delta_t[:, :, None]) * (1.0 / math.sqrt(HD))).astype(
        jnp.bfloat16
    )
    return (probs_wide.astype(jnp.bfloat16), d_logits)


def keep_state(state_in):
    return state_in


def forward_attention(query, keys_all, values_all, own_pos, all_pos):
    local_rows = query.shape[0]
    seq_rows = keys_all.shape[0]
    qstep = min(512, local_rows)
    kstep = min(512, seq_rows)
    latest = jnp.max(own_pos)

    def stats_step(number, state_in):
        key_block = lax.dynamic_slice_in_dim(keys_all, number * kstep, kstep, 0)
        key_pos = lax.dynamic_slice_in_dim(all_pos, number * kstep, kstep, 0)

        def stats_live(state_now):
            running_max, running_sum = state_now
            logits = masked_logits(query, key_block, own_pos, key_pos)
            new_max = jnp.maximum(running_max, jnp.max(logits, axis=-1))
            running_sum = running_sum * jnp.exp(running_max - new_max) + jnp.sum(
                jnp.exp(logits - new_max[:, :, None]), axis=-1
            )
            return (new_max, running_sum)

        return lax.cond(jnp.min(key_pos) <= latest, stats_live, keep_state, state_in)

    start_state = (jnp.full((H, qstep), NEG, jnp.float32), jnp.zeros((H, qstep), jnp.float32))
    running_max, running_sum = lax.fori_loop(0, seq_rows // kstep, stats_step, start_state)
    total_t = running_max + jnp.log(running_sum)

    def value_step(number, state_in):
        key_block = lax.dynamic_slice_in_dim(keys_all, number * kstep, kstep, 0)
        value_block = lax.dynamic_slice_in_dim(values_all, number * kstep, kstep, 0)
        key_pos = lax.dynamic_slice_in_dim(all_pos, number * kstep, kstep, 0)

        def value_live(state_now):
            logits = masked_logits(query, key_block, own_pos, key_pos)
            attn_probs = jnp.exp(logits - total_t[:, :, None]).astype(jnp.bfloat16)
            return state_now + jnp.einsum(
                "hqk,khd->qhd", attn_probs, value_block, preferred_element_type=jnp.float32
            )

        return lax.cond(jnp.min(key_pos) <= latest, value_live, keep_state, state_in)

    weighted = lax.fori_loop(
        0, seq_rows // kstep, value_step, jnp.zeros((qstep, H, HD), jnp.float32)
    )
    totals = total_t.T
    return (weighted, totals)


def query_grads(query, d_att, log_total, delta, own_pos, keys_all, values_all, all_pos):
    local_rows = query.shape[0]
    seq_rows = keys_all.shape[0]
    qstep = min(512, local_rows)
    kstep = min(512, seq_rows)
    key_grads = jnp.zeros((seq_rows, H, HD), jnp.float32)
    value_grads = jnp.zeros((seq_rows, H, HD), jnp.float32)
    total_t = log_total.T
    delta_t = delta.T
    latest = jnp.max(own_pos)

    def key_step(number, state_in):
        offset = number * kstep
        key_block = lax.dynamic_slice_in_dim(keys_all, offset, kstep, 0)
        value_block = lax.dynamic_slice_in_dim(values_all, offset, kstep, 0)
        key_pos = lax.dynamic_slice_in_dim(all_pos, offset, kstep, 0)

        def key_live(state_now):
            attn_probs, d_logits = block_terms(
                query, d_att, total_t, delta_t, own_pos, key_block, value_block, key_pos
            )
            d_query = state_now[0] + jnp.einsum(
                "hqk,khd->qhd", d_logits, key_block, preferred_element_type=jnp.float32
            )
            key_acc = state_now[1]
            value_acc = state_now[2]
            key_part = jnp.einsum(
                "hqk,qhd->khd", d_logits, query, preferred_element_type=jnp.float32
            )
            value_part = jnp.einsum(
                "hqk,qhd->khd", attn_probs, d_att, preferred_element_type=jnp.float32
            )
            key_acc = lax.dynamic_update_slice_in_dim(
                key_acc, lax.dynamic_slice_in_dim(key_acc, offset, kstep, 0) + key_part, offset, 0
            )
            value_acc = lax.dynamic_update_slice_in_dim(
                value_acc,
                lax.dynamic_slice_in_dim(value_acc, offset, kstep, 0) + value_part,
                offset,
                0,
            )
            return (d_query, key_acc, value_acc)

        return lax.cond(jnp.min(key_pos) <= latest, key_live, keep_state, state_in)

    start_state = (jnp.zeros((qstep, H, HD), jnp.float32),) + (key_grads, value_grads)
    result = lax.fori_loop(0, seq_rows // kstep, key_step, start_state)
    pieces = result[0]
    key_grads = result[1]
    value_grads = result[2]
    return (pieces, key_grads, value_grads)


def local(
    hidden_in,
    norm1_gain,
    attention_norm_bias,
    qkv_weight,
    qkv_bias,
    out_weight,
    out_bias,
    norm2_gain,
    feedforward_norm_bias,
    up_weight,
    up_bias,
    down_weight,
    down_bias,
    cotangent,
    block_order,
):
    (
        attention_norm_gain,
        attention_bias_term,
        wqkv,
        bqkv,
        wout,
        bout,
        feedforward_norm_gain,
        feedforward_bias_term,
        wup,
        bup,
        wdown,
        bdown,
    ) = (
        lax.all_gather(norm1_gain, "fsdp", axis=0, tiled=True),
        lax.all_gather(attention_norm_bias, "fsdp", axis=0, tiled=True),
        lax.all_gather(qkv_weight, "fsdp", axis=0, tiled=True),
        lax.all_gather(qkv_bias, "fsdp", axis=0, tiled=True),
        lax.all_gather(out_weight, "fsdp", axis=0, tiled=True),
        lax.all_gather(out_bias, "fsdp", axis=0, tiled=True),
        lax.all_gather(norm2_gain, "fsdp", axis=0, tiled=True),
        lax.all_gather(feedforward_norm_bias, "fsdp", axis=0, tiled=True),
        lax.all_gather(up_weight, "fsdp", axis=0, tiled=True),
        lax.all_gather(up_bias, "fsdp", axis=0, tiled=True),
        lax.all_gather(down_weight, "fsdp", axis=0, tiled=True),
        lax.all_gather(down_bias, "fsdp", axis=0, tiled=True),
    )
    width = H * HD
    hidden_rows = hidden_in[0]
    cotan_rows = cotangent[0]
    local_rows = hidden_rows.shape[0]
    ctx_count = lax.axis_size("ctx")
    ctx_rank = lax.axis_index("ctx")
    seq_rows = local_rows * ctx_count
    all_pos = (block_order[:, None] * BLK + jnp.arange(BLK, dtype=jnp.int32)[None, :]).reshape(
        seq_rows
    )
    own_pos = lax.dynamic_slice_in_dim(all_pos, ctx_rank * local_rows, local_rows, 0)
    cosine, sine = rotary_tables(own_pos)
    attention_norm_gain = attention_norm_gain.astype(jnp.float32)
    feedforward_norm_gain = feedforward_norm_gain.astype(jnp.float32)
    residual_stream = hidden_rows.astype(jnp.float32)
    attention_normed, attention_standardized, attention_inverse_deviation = apply_layer_norm(
        residual_stream, attention_norm_gain, attention_bias_term.astype(jnp.float32)
    )
    normed1_b = attention_normed.astype(jnp.bfloat16)
    projected = jnp.dot(normed1_b, wqkv, preferred_element_type=jnp.float32) + bqkv.astype(
        jnp.float32
    )
    query = rotate(projected[:, :width].reshape(local_rows, H, HD), cosine, sine).astype(
        jnp.bfloat16
    )
    key_rows = rotate(
        projected[:, width : 2 * width].reshape(local_rows, H, HD), cosine, sine
    ).astype(jnp.bfloat16)
    value_rows = projected[:, 2 * width :].astype(jnp.bfloat16)
    keys_all, values_all = (
        lax.all_gather(key_rows.reshape(local_rows, width), "ctx", axis=0, tiled=True),
        lax.all_gather(value_rows, "ctx", axis=0, tiled=True),
    )
    keys_all = keys_all.reshape(seq_rows, H, HD)
    values_all = values_all.reshape(seq_rows, H, HD)
    attended, log_total = forward_attention(query, keys_all, values_all, own_pos, all_pos)
    attended_b = attended.reshape(local_rows, width).astype(jnp.bfloat16)
    attn_out = jnp.dot(attended_b, wout, preferred_element_type=jnp.float32) + bout.astype(
        jnp.float32
    )
    feedforward_normed, feedforward_standardized, feedforward_inverse_deviation = apply_layer_norm(
        residual_stream, feedforward_norm_gain, feedforward_bias_term.astype(jnp.float32)
    )
    normed2_b = feedforward_normed.astype(jnp.bfloat16)
    up_rows = jnp.dot(normed2_b, wup, preferred_element_type=jnp.float32) + bup.astype(jnp.float32)
    act_b = gelu_exact(up_rows).astype(jnp.bfloat16)
    mlp_out = jnp.dot(act_b, wdown, preferred_element_type=jnp.float32) + bdown.astype(jnp.float32)
    hidden_out = (residual_stream + attn_out + mlp_out).astype(jnp.bfloat16)
    cotan_wide = cotan_rows.astype(jnp.float32)
    grad_wdown = jnp.einsum("tk,tn->kn", act_b, cotan_rows, preferred_element_type=jnp.float32)
    grad_bdown = jnp.sum(cotan_wide, axis=0)
    d_up = jnp.einsum(
        "tn,kn->tk", cotan_rows, wdown, preferred_element_type=jnp.float32
    ) * gelu_slope(up_rows)
    d_up16 = d_up.astype(jnp.bfloat16)
    grad_wup = jnp.einsum("tk,tn->kn", normed2_b, d_up16, preferred_element_type=jnp.float32)
    grad_bup = jnp.sum(d_up, axis=0)
    grad_feedforward_normed = jnp.einsum(
        "tn,kn->tk", d_up16, wup, preferred_element_type=jnp.float32
    )
    grad_feedforward_gain = jnp.sum(grad_feedforward_normed * feedforward_standardized, axis=0)
    grad_shift2 = jnp.sum(grad_feedforward_normed, axis=0)
    feedforward_branch_grad = layer_norm_backward(
        grad_feedforward_normed,
        feedforward_standardized,
        feedforward_inverse_deviation,
        feedforward_norm_gain,
    )
    grad_wout = jnp.einsum("tk,tn->kn", attended_b, cotan_rows, preferred_element_type=jnp.float32)
    d_att = jnp.einsum("tn,kn->tk", cotan_rows, wout, preferred_element_type=jnp.float32).astype(
        jnp.bfloat16
    )
    delta = jnp.sum(
        d_att.reshape(local_rows, H, HD).astype(jnp.float32)
        * attended_b.reshape(local_rows, H, HD).astype(jnp.float32),
        axis=-1,
    )
    d_att3 = d_att.reshape(local_rows, H, HD)
    d_query, key_grads, value_grads = query_grads(
        query, d_att3, log_total, delta, own_pos, keys_all, values_all, all_pos
    )
    d_key, d_value = (
        lax.psum_scatter(
            key_grads.reshape(seq_rows, width), "ctx", scatter_dimension=0, tiled=True
        ),
        lax.psum_scatter(
            value_grads.reshape(seq_rows, width), "ctx", scatter_dimension=0, tiled=True
        ),
    )
    d_query = rotate_back(d_query, cosine, sine)
    d_key = rotate_back(d_key.reshape(local_rows, H, HD), cosine, sine)
    d_qkv = jnp.concatenate(
        [d_query.reshape(local_rows, width), d_key.reshape(local_rows, width), d_value], axis=1
    )
    d_qkv16 = d_qkv.astype(jnp.bfloat16)
    grad_wqkv = jnp.einsum("tk,tn->kn", normed1_b, d_qkv16, preferred_element_type=jnp.float32)
    grad_bqkv = jnp.sum(d_qkv, axis=0)
    grad_attention_normed = jnp.einsum(
        "tn,kn->tk", d_qkv16, wqkv, preferred_element_type=jnp.float32
    )
    grad_attention_gain = jnp.sum(grad_attention_normed * attention_standardized, axis=0)
    grad_shift1 = jnp.sum(grad_attention_normed, axis=0)
    attention_branch_grad = layer_norm_backward(
        grad_attention_normed,
        attention_standardized,
        attention_inverse_deviation,
        attention_norm_gain,
    )
    hidden_grad = cotan_wide + attention_branch_grad + feedforward_branch_grad
    terms = (
        grad_attention_gain,
        grad_shift1,
        grad_wqkv,
        grad_bqkv,
        grad_wout,
        grad_bdown,
        grad_feedforward_gain,
        grad_shift2,
        grad_wup,
        grad_bup,
        grad_wdown,
        grad_bdown,
    )
    shares = (
        lax.psum_scatter(terms[0], "fsdp", scatter_dimension=0, tiled=True),
        lax.psum_scatter(terms[1], "fsdp", scatter_dimension=0, tiled=True),
        lax.psum_scatter(terms[2], "fsdp", scatter_dimension=0, tiled=True),
        lax.psum_scatter(terms[3], "fsdp", scatter_dimension=0, tiled=True),
        lax.psum_scatter(terms[4], "fsdp", scatter_dimension=0, tiled=True),
        lax.psum_scatter(terms[5], "fsdp", scatter_dimension=0, tiled=True),
        lax.psum_scatter(terms[6], "fsdp", scatter_dimension=0, tiled=True),
        lax.psum_scatter(terms[7], "fsdp", scatter_dimension=0, tiled=True),
        lax.psum_scatter(terms[8], "fsdp", scatter_dimension=0, tiled=True),
        lax.psum_scatter(terms[9], "fsdp", scatter_dimension=0, tiled=True),
        lax.psum_scatter(terms[10], "fsdp", scatter_dimension=0, tiled=True),
        lax.psum_scatter(terms[11], "fsdp", scatter_dimension=0, tiled=True),
    )
    shares = lax.psum(
        (
            shares[0],
            shares[1],
            shares[2],
            shares[3],
            shares[4],
            shares[5],
            shares[6],
            shares[7],
            shares[8],
            shares[9],
            shares[10],
            shares[11],
        ),
        "ctx",
    )
    return (
        hidden_out[None],
        hidden_grad[None],
        shares[0],
        shares[1],
        shares[2],
        shares[3],
        shares[4],
        shares[5],
        shares[6],
        shares[7],
        shares[8],
        shares[9],
        shares[10],
        shares[11],
    )


def solution(mesh):
    in_specs = (
        P("fsdp", "ctx", None),
        P("fsdp"),
        P("fsdp"),
        P("fsdp", None),
        P("fsdp"),
        P("fsdp", None),
        P("fsdp"),
        P("fsdp"),
        P("fsdp"),
        P("fsdp", None),
        P("fsdp"),
        P("fsdp", None),
        P("fsdp"),
        P("fsdp", "ctx", None),
        P(),
    )
    out_specs = (
        P("fsdp", "ctx", None),
        P("fsdp", "ctx", None),
        P("fsdp"),
        P("fsdp"),
        P("fsdp", None),
        P("fsdp"),
        P("fsdp", None),
        P("fsdp"),
        P("fsdp"),
        P("fsdp"),
        P("fsdp", None),
        P("fsdp"),
        P("fsdp", None),
        P("fsdp"),
    )
    return jax.shard_map(local, mesh=mesh, in_specs=in_specs, out_specs=out_specs, check_vma=False)
```

profile of v0, /device:TPU:1, one launch (start us, length us, event | category | flops | bytes accessed | tf_op | source)
XLA Modules:
  0.0 1125.9 jit_solution(13537540870815105237)
XLA Ops:
  17.2 18.7 %all-reduce.17 = (bf16[768]{0:T(1024)(128)(2,1)}, bf16[768]{0:T(1024)(128)(2,1)}, bf16[768]{0:T(1024)(128)(2,1)}, bf16[2304]{0:T(1024)(128)(2,1)S(1)}, bf16[768]...) all-reduce(bf16[768]{0:T(1024)(128)(2,1)S(1)} %dynamic-update-slice, ...), channel_id=1, replica_groups=mesh['ctx'=8,'fsdp'=4] {'fsdp'}, use_global_device_ids=true, to_apply=%add.5 | all-reduce | flops 6912 | bytes 27648
  38.4 44.2 %all-gather.8.cloned.1.call-done = bf16[768,2304]{1,0:T(8,128)(2,1)} async-done(((bf16[192,2304]{1,0:T(8,128)(2,1)}), bf16[768,2304]{1,0:T(8,128)(2,1)}) %all-gather.8.cloned.1.call-update) | async-done | bytes 3538960 | tf_op jit(solution)/shard_map/all_gather | solution.py:241
  93.3 18.9 %all-gather.14.cloned.1.call-done = bf16[768,768]{1,0:T(8,128)(2,1)} async-done(((bf16[192,768]{1,0:T(8,128)(2,1)}), bf16[768,768]{1,0:T(8,128)(2,1)}) %all-gather.14.cloned.1.call-update) | async-done | bytes 1179664 | tf_op jit(solution)/shard_map/all_gather | solution.py:243
  115.0 32.2 %all-gather.12.cloned.1.call-done = bf16[2048,768]{1,0:T(8,128)(2,1)} async-done(((bf16[256,768]{1,0:T(8,128)(2,1)}), bf16[2048,768]{1,0:T(8,128)(2,1)}) %all-gather.12.cloned.1.call-update) | async-done | bytes 3145744 | tf_op jit(solution)/shard_map/all_gather | solution.py:283
  147.2 4.7 copy.61
  151.8 30.4 %all-gather.10.cloned.1.call-done = bf16[2048,768]{0,1:T(8,128)(2,1)} async-done(((bf16[256,768]{0,1:T(8,128)(2,1)}), bf16[2048,768]{0,1:T(8,128)(2,1)}) %all-gather.10.cloned.1.call-update) | async-done | bytes 3145744 | tf_op jit(solution)/shard_map/all_gather | solution.py:282
  182.3 23.4 %while.48 = (s32[]{:T(128)}, f32[12,256]{1,0:T(8,128)S(1)}, f32[12,256]{1,0:T(8,128)S(1)}, s32[2048]{0:T(1024)S(1)}, s32[]{:T(128)}, /*index=5*/s32[256]{0:T(256...) while((s32[]{:T(128)}, f32[12,256]{1,0:T(8,128)S(1)}, ...), condition=%wide.region_9.10_spmd, body=%wide.region_3.9_spmd.sunk | while | flops 212474368 | bytes 14323481 | solution.py:131
  206.3 23.0 %while.49 = (s32[]{:T(128)}, f32[256,12,64]{0,2,1:T(8,128)S(1)}, s32[2048]{0:T(1024)S(1)}, s32[]{:T(128)}, s32[256]{0:T(256)S(1)}, /*index=5*/bf16[2048,12,64]{0...) while((s32[]{:T(128)}, f32[256,12,64]{0,2,1:T(8,128)S(1)}, ...), condition=%wide.region_14.15_spmd, body=%wide.region_10.14_spmd.sunk | while | flops 409272832 | bytes 3825929 | solution.py:148
  239.6 80.6 %while.50 = (s32[]{:T(128)}, f32[256,12,64]{0,2,1:T(8,128)}, f32[2048,12,64]{0,2,1:T(8,128)}, f32[2048,12,64]{0,2,1:T(8,128)}, s32[2048]{0:T(1024)S(1)}, /*index...) while((s32[]{:T(128)}, f32[256,12,64]{0,2,1:T(8,128)}, ...), condition=%wide.region_20.21_spmd, body=%wide.region_16.20_spmd.sunk | while | flops 1025049088 | bytes 91984960 | solution.py:201
  241.6 18.2 %conditional.8 = ((f32[256,12,64]{0,2,1:T(8,128)}, f32[2048,12,64]{0,2,1:T(8,128)}, f32[2048,12,64]{0,2,1:T(8,128)})) conditional(s32[]{:T(128)} %convert_element_type.249, (f32[256,12,64]{0,2,1:T(8,128)}, f32[2048,12,64]{0,2,1:T(8,128)}, f32[2048,12,64]{0,2,1:T(8,128)}) %tuple.162, (s32[512]{0:T(512)S(1)}, s32[256]{0:T(256)S(1)}, ...), branch_computations={%region_18.18_spmd, %region_19.19_spmd} | conditional | flops 1025048576 | bytes 91980512 | solution.py:198
  252.4 4.5 fusion.36
  261.8 18.1 %conditional.8 = ((f32[256,12,64]{0,2,1:T(8,128)}, f32[2048,12,64]{0,2,1:T(8,128)}, f32[2048,12,64]{0,2,1:T(8,128)})) conditional(s32[]{:T(128)} %convert_element_type.249, (f32[256,12,64]{0,2,1:T(8,128)}, f32[2048,12,64]{0,2,1:T(8,128)}, f32[2048,12,64]{0,2,1:T(8,128)}) %tuple.162, (s32[512]{0:T(512)S(1)}, s32[256]{0:T(256)S(1)}, ...), branch_computations={%region_18.18_spmd, %region_19.19_spmd} | conditional | flops 1025048576 | bytes 91980512 | solution.py:198
  272.5 4.5 fusion.36
  281.9 18.1 %conditional.8 = ((f32[256,12,64]{0,2,1:T(8,128)}, f32[2048,12,64]{0,2,1:T(8,128)}, f32[2048,12,64]{0,2,1:T(8,128)})) conditional(s32[]{:T(128)} %convert_element_type.249, (f32[256,12,64]{0,2,1:T(8,128)}, f32[2048,12,64]{0,2,1:T(8,128)}, f32[2048,12,64]{0,2,1:T(8,128)}) %tuple.162, (s32[512]{0:T(512)S(1)}, s32[256]{0:T(256)S(1)}, ...), branch_computations={%region_18.18_spmd, %region_19.19_spmd} | conditional | flops 1025048576 | bytes 91980512 | solution.py:198
  302.1 18.1 %conditional.8 = ((f32[256,12,64]{0,2,1:T(8,128)}, f32[2048,12,64]{0,2,1:T(8,128)}, f32[2048,12,64]{0,2,1:T(8,128)})) conditional(s32[]{:T(128)} %convert_element_type.249, (f32[256,12,64]{0,2,1:T(8,128)}, f32[2048,12,64]{0,2,1:T(8,128)}, f32[2048,12,64]{0,2,1:T(8,128)}) %tuple.162, (s32[512]{0:T(512)S(1)}, s32[256]{0:T(256)S(1)}, ...), branch_computations={%region_18.18_spmd, %region_19.19_spmd} | conditional | flops 1025048576 | bytes 91980512 | solution.py:198
  312.8 4.5 fusion.36
  323.4 13.6 %all-gather = bf16[4,1,768]{2,1,0:T(2,128)(2,1)S(1)} all-gather(bf16[1,1,768]{2,1,0:T(2,128)(2,1)S(1)} %reshape.290), channel_id=1, replica_groups=mesh['ctx'=8,'fsdp'=4] {'fsdp'}, dimensions={0}, use_global_device_ids=true | all-gather | bytes 7680 | tf_op jit(solution)/shard_map/all_gather | solution.py:248
  337.1 5.8 multiply_convert_fusion
  342.9 19.1 %all-gather.18.cloned.1.call-done = bf16[3072,768]{1,0:T(8,128)(2,1)} async-done(((bf16[768,768]{1,0:T(8,128)(2,1)}), bf16[3072,768]{1,0:T(8,128)(2,1)}) %all-gather.18.cloned.1.call-update) | async-done | bytes 4718608 | tf_op jit(solution)/shard_map/all_gather | solution.py:249
  362.0 6.3 fusion.110
  369.5 6.2 fusion.86
  376.0 5.1 fusion.90
  382.4 43.0 %reduce-scatter.7.cloned.1.call-done = f32[256,768]{0,1:T(8,128)} async-done(((f32[2048,768]{0,1:T(8,128)}), f32[256,768]{0,1:T(8,128)}) %reduce-scatter.7.cloned.1.call-update) | async-done | bytes 786448 | tf_op jit(solution)/shard_map/reduce_scatter | solution.py:334
  427.7 62.7 %reduce-scatter.9.cloned.1.call-done = f32[256,768]{0,1:T(8,128)} async-done(((f32[2048,768]{0,1:T(8,128)}), f32[256,768]{0,1:T(8,128)}) %reduce-scatter.9.cloned.1.call-update) | async-done | bytes 786448 | tf_op jit(solution)/shard_map/reduce_scatter | solution.py:337
  490.4 5.4 fusion.96
  495.8 45.0 %reduce-scatter.13.cloned.1.call-done = f32[192,768]{1,0:T(8,128)} async-done(((f32[768,768]{1,0:T(8,128)}), f32[192,768]{1,0:T(8,128)}) %reduce-scatter.13.cloned.1.call-update) | async-done | bytes 589840 | tf_op jit(solution)/shard_map/reduce_scatter | solution.py:380
  540.8 162.8 %reduce-scatter.15.cloned.1.call-done = f32[192,3072]{1,0:T(8,128)} async-done(((f32[768,3072]{1,0:T(8,128)}), f32[192,3072]{1,0:T(8,128)}) %reduce-scatter.15.cloned.1.call-update) | async-done | bytes 2359312 | tf_op jit(solution)/shard_map/reduce_scatter | solution.py:384
  703.5 164.5 %reduce-scatter.17.cloned.1.call-done = f32[768,768]{1,0:T(8,128)} async-done(((f32[3072,768]{1,0:T(8,128)}), f32[768,768]{1,0:T(8,128)}) %reduce-scatter.17.cloned.1.call-update) | async-done | bytes 2359312 | tf_op jit(solution)/shard_map/reduce_scatter | solution.py:386
  868.1 127.0 %reduce-scatter.11.cloned.1.call-done = f32[192,2304]{1,0:T(8,128)} async-done(((f32[768,2304]{1,0:T(8,128)}), f32[192,2304]{1,0:T(8,128)}) %reduce-scatter.11.cloned.1.call-update) | async-done | bytes 1769488 | tf_op jit(solution)/shard_map/reduce_scatter | solution.py:378
  1011.3 15.7 %all-reduce.16 = (f32[768]{0:T(1024)S(1)}, f32[768]{0:T(1024)S(1)}, f32[2304]{0:T(1024)S(1)}, f32[768]{0:T(1024)S(1)}, f32[768]{0:T(1024)S(1)}, /*index=5*/f32[768]{0:T(1024)S(1)}, f32[3072]{0:T(1024)S(1)}) all-reduce(f32[768]{0:T(1024)S(1)} %get-tuple-element.798, ...), channel_id=4, replica_groups=mesh['ctx'=8,'fsdp'=4] {'fsdp'}, use_global_device_ids=true, to_apply=%region_28.0.clone | all-reduce | flops 9216 | bytes 73728
  1027.5 23.7 %all-reduce.14 = (f32[192]{0:T(256)}, f32[192]{0:T(256)}, f32[576]{0:T(1024)}, f32[192]{0:T(256)S(1)}, f32[192]{0:T(256)}, /*index=5*/f32[192]{0:T(256)}, f32[768]{0:T(1024)}) all-reduce(f32[192]{0:T(256)S(1)} %dynamic-slice.8, f32[192]{0:T(256)S(1)} %dynamic-slice.10, ...), channel_id=1, replica_groups=mesh['ctx'=8,'fsdp'=4] {'ctx'}, use_global_device_ids=true, to_apply=%region_29.30 | all-reduce | flops 2304 | bytes 18432 | tf_op jit(solution)/shard_map/psum | solution.py:389
  1051.2 60.8 %all-reduce.20.cloned.1.call-done = (f32[192,2304]{1,0:T(8,128)}, f32[192,768]{1,0:T(8,128)}, f32[192,3072]{1,0:T(8,128)}, f32[768,768]{1,0:T(8,128)}) async-done(((f32[192,2304]{1,0:T(8,128)}, f32[192,768]{1,0:T(8,128)}, f32[192,3072]{1,0:T(8,128)}, f32[768,768]{1,0:T(8,128)}), (f32[192,2304]{1,0:T(8,128)}, f32[192,768]{1,0:T(8,128)}, f32[192,3072]{1,0:T(8,128)}, ...) | async-done | bytes 7077904 | tf_op jit(solution)/shard_map/psum | solution.py:389
  (287 shorter events, 192.4 us)
Async XLA Ops:
  7.2 75.3 %all-gather.8.cloned.1.call-start = ((), (), s32[]{:S(2)}) async-start(), calls=%async_computation.6 | async-start | bytes 4423680 | tf_op jit(solution)/shard_map/all_gather | solution.py:241
  7.9 104.3 %all-gather.14.cloned.1.call-start = ((), (), s32[]{:S(2)}) async-start(), calls=%async_computation.9 | async-start | bytes 1474560 | tf_op jit(solution)/shard_map/all_gather | solution.py:243
  8.7 138.5 %all-gather.12.cloned.1.call-start = ((), (), s32[]{:S(2)}) async-start(), calls=%async_computation.8 | async-start | bytes 3538944 | tf_op jit(solution)/shard_map/all_gather | solution.py:283
  35.9 49.9 %copy-start.17 = (f32[768]{0:T(1024)}, f32[768]{0:T(1024)S(1)}, u32[]{:S(2)}) copy-start(f32[768]{0:T(1024)S(1)} %convert_element_type.116) | copy-start | bytes 9220
  35.9 49.9 %copy-start.19 = (f32[768]{0:T(1024)}, f32[768]{0:T(1024)S(1)}, u32[]{:S(2)}) copy-start(f32[768]{0:T(1024)S(1)} %convert_element_type.117) | copy-start | bytes 9220
  37.1 48.8 %copy-start.25 = (f32[256]{0:T(256)}, f32[256]{0:T(256)S(1)}, u32[]{:S(2)}) copy-start(f32[256]{0:T(256)S(1)} %broadcast_multiply_fusion.4) | copy-start | bytes 3076
  38.3 47.5 %copy-start.27 = (f32[256]{0:T(256)}, f32[256]{0:T(256)S(1)}, u32[]{:S(2)}) copy-start(f32[256]{0:T(256)S(1)} %add_rsqrt_fusion) | copy-start | bytes 3076
  38.3 49.8 %copy-start.37 = (s32[16]{0:T(128)S(1)}, s32[16]{0:T(128)}, u32[]{:S(2)}) copy-start(s32[16]{0:T(128)} %param.41) | copy-start | bytes 196
  88.1 94.2 %all-gather.10.cloned.1.call-start = ((), (), s32[]{:S(2)}) async-start(), calls=%async_computation.7 | async-start | bytes 3538944 | tf_op jit(solution)/shard_map/all_gather | solution.py:282
  90.3 22.0 %copy-start.3 = (bf16[1,256,768]{2,1,0:T(8,128)(2,1)S(1)}, bf16[1,256,768]{2,1,0:T(8,128)(2,1)}, u32[]{:S(2)}) copy-start(bf16[1,256,768]{2,1,0:T(8,128)(2,1)} %param.40) | copy-start | bytes 1179652
  91.5 245.5 %all-gather.16.cloned.1.call-start = ((), (), s32[]{:S(2)}) async-start(), calls=%async_computation.10 | async-start | bytes 5898240 | tf_op jit(solution)/shard_map/all_gather | solution.py:247
  92.1 269.9 %all-gather.18.cloned.1.call-start = ((), (), s32[]{:S(2)}) async-start(), calls=%async_computation.11 | async-start | bytes 5898240 | tf_op jit(solution)/shard_map/all_gather | solution.py:249
  92.7 332.7 %reduce-scatter.7.cloned.1.call-start = ((), (), s32[]{:S(2)}) async-start(), calls=%async_computation.12 | async-start | bytes 7077888 | tf_op jit(solution)/shard_map/reduce_scatter | solution.py:334
  243.8 4.6 copy-start
  264.0 4.6 copy-start
  284.2 4.6 copy-start
  304.3 4.6 copy-start
  320.2 170.1 %reduce-scatter.9.cloned.1.call-start = ((), (), s32[]{:S(2)}) async-start(), calls=%async_computation.13 | async-start | bytes 7077888 | tf_op jit(solution)/shard_map/reduce_scatter | solution.py:337
  321.0 16.1 %copy-start.2 = (bf16[1,256,768]{2,1,0:T(8,128)(2,1)S(1)}, bf16[1,256,768]{2,1,0:T(8,128)(2,1)}, u32[]{:S(2)}) copy-start(bf16[1,256,768]{2,1,0:T(8,128)(2,1)} %param.27) | copy-start | bytes 1179652
  321.0 16.1 %copy-start.26 = (f32[256]{0:T(256)S(1)}, f32[256]{0:T(256)}, u32[]{:S(2)}) copy-start(f32[256]{0:T(256)} %copy-done.25) | copy-start | bytes 3076
  321.0 16.1 %copy-start.28 = (f32[256]{0:T(256)S(1)}, f32[256]{0:T(256)}, u32[]{:S(2)}) copy-start(f32[256]{0:T(256)} %copy-done.27) | copy-start | bytes 3076
  321.0 219.7 %reduce-scatter.13.cloned.1.call-start = ((), (), s32[]{:S(2)}) async-start(), calls=%async_computation.15 | async-start | bytes 2949120 | tf_op jit(solution)/shard_map/reduce_scatter | solution.py:380
  323.3 380.3 %reduce-scatter.15.cloned.1.call-start = ((), (), s32[]{:S(2)}) async-start(), calls=%async_computation.16 | async-start | bytes 11796480 | tf_op jit(solution)/shard_map/reduce_scatter | solution.py:384
  342.9 33.1 %copy-start.10 = (bf16[256,3072]{1,0:T(8,128)(2,1)}, bf16[256,3072]{1,0:T(8,128)(2,1)S(1)}, u32[]{:S(2)}) copy-start(bf16[256,3072]{1,0:T(8,128)(2,1)S(1)} %get-tuple-element.925) | copy-start | bytes 4718596
  375.7 492.4 %reduce-scatter.17.cloned.1.call-start = ((), (), s32[]{:S(2)}) async-start(), calls=%async_computation.17 | async-start | bytes 11796480 | tf_op jit(solution)/shard_map/reduce_scatter | solution.py:386
  381.1 45.3 %copy-start.22 = (f32[256,8]{0,1:T(8,128)S(1)}, f32[256,8]{0,1:T(8,128)}, u32[]{:S(2)}) copy-start(f32[256,8]{0,1:T(8,128)} %copy-done.21) | copy-start | bytes 24580
  381.1 45.3 %copy-start.24 = (f32[256,8]{0,1:T(8,128)S(1)}, f32[256,8]{0,1:T(8,128)}, u32[]{:S(2)}) copy-start(f32[256,8]{0,1:T(8,128)} %copy-done.23) | copy-start | bytes 24580
  381.2 614.0 %reduce-scatter.11.cloned.1.call-start = ((), (), s32[]{:S(2)}) async-start(), calls=%async_computation.14 | async-start | bytes 8847360 | tf_op jit(solution)/shard_map/reduce_scatter | solution.py:378
  381.2 109.1 %copy-start.18 = (f32[768]{0:T(1024)S(1)}, f32[768]{0:T(1024)}, u32[]{:S(2)}) copy-start(f32[768]{0:T(1024)} %copy-done.17) | copy-start | bytes 9220
  381.2 109.1 %copy-start.20 = (f32[768]{0:T(1024)S(1)}, f32[768]{0:T(1024)}, u32[]{:S(2)}) copy-start(f32[768]{0:T(1024)} %copy-done.19) | copy-start | bytes 9220
  495.8 616.3 %all-reduce.20.cloned.1.call-start = ((), (), s32[]{:S(2)}) async-start(), calls=%async_computation.18 | async-start | bytes 14155776 | tf_op jit(solution)/shard_map/psum | solution.py:389
  1051.2 66.7 %copy-start.35 = (f32[192]{0:T(256)}, f32[192]{0:T(256)S(1)}, u32[]{:S(2)}) copy-start(f32[192]{0:T(256)S(1)} %get-tuple-element.1310) | copy-start | bytes 2308
  (34 other events, 101.4 us)
Sparse Core Ops, SparseCore 0:
  9.6 72.9 all-gather.7
  84.1 28.1 all-gather.13
  114.7 32.4 all-gather.11
  149.5 32.7 all-gather.9
  183.7 88.8 all-gather.15
  274.0 87.9 all-gather.17
  365.4 59.9 reduce-scatter.6
  428.7 61.5 reduce-scatter.8
  493.2 47.4 reduce-scatter.12
  543.0 160.5 reduce-scatter.14
  705.9 162.1 reduce-scatter.16
  870.3 124.8 reduce-scatter.10
  998.8 113.1 all-reduce.19
where the time goes:
time: 1130 us
  waiting for transfers between devices  814 us (72%)
  matrix products  142 us (13%)
  blocking collectives  71.7 us (6%)
  local copies, waits for them, and re-layouts  37.9 us (3%)
  other arithmetic  25.6 us (2%)
  between operations  17.8 us (2%)
  loops' own time  16.6 us (1%)
    reduce_scatter x1, waiting for transfers between devices, local(): lax.psum_scatter(terms[10], 'fsdp', scatter_dimension=0, tiled=True)  165 us
    reduce_scatter x1, waiting for transfers between devices, local(): lax.psum_scatter(terms[8], 'fsdp', scatter_dimension=0, tiled=True)  163 us
    reduce_scatter x1, waiting for transfers between devices, local(): lax.psum_scatter(terms[2], 'fsdp', scatter_dimension=0, tiled=True)  127 us
    reduce_scatter x1, waiting for transfers between devices, local(): lax.psum_scatter(value_grads.reshape(seq_rows, width), 'ctx', scatter_dim...  62.7 us
    psum x1, waiting for transfers between devices, local(): lax.psum((shares[0], shares[1], shares[2], shares[3], shares[4], shares[5...  60.8 us
    reduce_scatter x1, waiting for transfers between devices, local(): lax.psum_scatter(terms[4], 'fsdp', scatter_dimension=0, tiled=True)  45 us
    all_gather x1, waiting for transfers between devices, local(): lax.all_gather(qkv_weight, 'fsdp', axis=0, tiled=True)  44.2 us
    reduce_scatter x1, waiting for transfers between devices, local(): lax.psum_scatter(key_grads.reshape(seq_rows, width), 'ctx', scatter_dimen...  43 us
  transfers between devices with their start and end apart: 13, of which 12 were waited for; matrix products, arithmetic and copies ran while one was open for 17% of the time, Pallas kernels for 0%

commit v1 on v0

--- a/solution.py
+++ b/solution.py
@@ -1,8 +1,11 @@
+import functools
 import math
 
 import jax
 import jax.numpy as jnp
 from jax import lax
+from jax.experimental import pallas as pl
+from jax.experimental.pallas import tpu as pltpu
 from jax.sharding import PartitionSpec as P
 
 H = 12
@@ -205,7 +208,7 @@
     return (pieces, key_grads, value_grads)
 
 
-def local(
+def whole_parameter_layer(
     hidden_in,
     norm1_gain,
     attention_norm_bias,
@@ -421,6 +424,1151 @@
     )
 
 
+MESH_IDS = pl.DeviceIdType.MESH
+
+
+def flip(index, bit):
+    return index + bit - 2 * bit * ((index // bit) % 2)
+
+
+class Copies:
+    def __init__(self, send_sems, recv_sems):
+        self.send_sems, self.recv_sems = send_sems, recv_sems
+        self.count, self.started, self.numbers = 0, [], {}
+
+    def make(self, source, target, device, when=None, like=None):
+        if like is None:
+            number = self.count
+            self.count += 1
+        else:
+            number = self.numbers[id(like)]
+        copy = pltpu.make_async_remote_copy(
+            src_ref=source,
+            dst_ref=target,
+            send_sem=self.send_sems.at[number],
+            recv_sem=self.recv_sems.at[number],
+            device_id=device,
+            device_id_type=MESH_IDS,
+        )
+        self.started.append((copy, when))
+        self.numbers[id(copy)] = number
+        return copy
+
+    def finish(self):
+        for copy, when in self.started:
+            run_when(when, copy.wait_send)
+
+
+def run_when(condition, action):
+    if condition is None:
+        action()
+    else:
+        pl.when(condition)(action)
+
+
+def greet(peers):
+    barrier = pltpu.get_barrier_semaphore()
+    total = 0
+    for device, condition in peers:
+        run_when(
+            condition,
+            functools.partial(
+                pl.semaphore_signal, barrier, inc=1, device_id=device, device_id_type=MESH_IDS
+            ),
+        )
+        total = total + (1 if condition is None else condition.astype(jnp.int32))
+    pl.semaphore_wait(barrier, total)
+
+
+def plane_gather(copies, source, same, other, slot, chip_of, rows, ids):
+    c, z, xn, yn, pn = ids
+    half = rows // 2
+    top, bottom = pl.ds(0, half), pl.ds(half, half)
+    t = chip_of
+    to_x = copies.make(source, same.at[slot(t)], (xn, z))
+    to_y = copies.make(source, same.at[slot(t)], (yn, z))
+    to_x.start()
+    to_y.start()
+    swaps = []
+
+    def swap(tt, part=None):
+        if other is None:
+            return
+        here, there = same.at[slot(tt)], other.at[slot(tt)]
+        if part is not None:
+            here, there = here.at[part], there.at[part]
+        copy = copies.make(here, there, (pn, z))
+        copy.start()
+        swaps.append(copy)
+
+    if other is not None:
+        copy = copies.make(source, other.at[slot(t)], (pn, z))
+        copy.start()
+        swaps.append(copy)
+    tx, ty, td = flip(t, 1), flip(t, 2), flip(flip(t, 1), 2)
+
+    def on_x():
+        to_x.wait_recv()
+        forward = copies.make(same.at[slot(tx)].at[top], same.at[slot(tx)].at[top], (yn, z))
+        forward.start()
+        swap(tx)
+        return forward
+
+    def on_y():
+        to_y.wait_recv()
+        forward = copies.make(same.at[slot(ty)].at[bottom], same.at[slot(ty)].at[bottom], (xn, z))
+        forward.start()
+        swap(ty)
+        return forward
+
+    def on_diagonal(from_y, from_x):
+        from_y.wait_recv()
+        swap(td, top)
+        from_x.wait_recv()
+        swap(td, bottom)
+
+    return on_x, on_y, on_diagonal, swaps
+
+
+def line_gather(copies, source, gathered, nz, ids, half_of):
+    c, z, xn, yn, pn = ids
+    steps = []
+    rows = gathered.shape[1] // 2
+    mine = pl.ds(half_of * rows, rows)
+    forwards = {}
+    for step in range(nz - 1):
+        for sign in (1, -1):
+            shard = z - sign * step
+            target = z + sign
+            ok = (shard >= 0) & (shard < nz) & (target >= 0) & (target < nz)
+            from_here = source.at[mine] if step == 0 else gathered.at[jnp.clip(shard, 0, nz - 1), mine]
+            place = gathered.at[jnp.clip(shard, 0, nz - 1), mine]
+            copy = copies.make(from_here, place, (c, jnp.clip(target, 0, nz - 1)), when=ok)
+            forwards[step, sign] = (copy, ok)
+    for sign in (1, -1):
+        copy, ok = forwards[0, sign]
+        run_when(ok, copy.start)
+    swaps = []
+
+    def advance(step):
+        for sign in (1, -1):
+            arrived = z - sign * (step + 1)
+            ok = (arrived >= 0) & (arrived < nz)
+            copy, _ = forwards[step, sign]
+            run_when(ok, copy.wait_recv)
+            if step + 1 < nz - 1:
+                following, following_ok = forwards[step + 1, sign]
+                run_when(following_ok, following.start)
+            place = gathered.at[jnp.clip(arrived, 0, nz - 1), mine]
+            swap = copies.make(place, place, (pn, z), when=ok)
+            run_when(ok, swap.start)
+            swaps.append((swap, ok))
+
+    return advance, swaps
+
+
+def gather_kernel(
+    nz,
+    h_ref,
+    g_ref,
+    wq_ref,
+    wu_ref,
+    wd_ref,
+    wo_ref,
+    sm_ref,
+    hall_ref,
+    gall_ref,
+    wq4_ref,
+    wu4_ref,
+    wd4_ref,
+    wo1_ref,
+    sm4_ref,
+    send_sems,
+    recv_sems,
+    local_sems,
+):
+    c, z = lax.axis_index("ctx"), lax.axis_index("fsdp")
+    k, t = c % 2, c // 2
+    xn, yn, pn = flip(c, 2), flip(c, 4), flip(c, 1)
+    ids = (c, z, xn, yn, pn)
+    others = [(z + d) % nz for d in range(1, nz)]
+    greet(
+        [((xn, z), None), ((yn, z), None), ((pn, z), None)] + [((c, other), None) for other in others]
+    )
+    copies = Copies(send_sems, recv_sems)
+    local_copies = []
+
+    def keep(source, target):
+        copy = pltpu.make_async_copy(source, target, local_sems.at[len(local_copies)])
+        copy.start()
+        local_copies.append(copy)
+
+    rows = h_ref.shape[0]
+    shard = wq_ref.shape[0]
+    wd_own = wd_ref.at[pl.ds(t * shard, shard)]
+    small = [copies.make(sm_ref, sm4_ref.at[z], (c, other)) for other in others]
+    for copy in small:
+        copy.start()
+    wq_step, wq_swaps = line_gather(copies, wq_ref, wq4_ref, nz, ids, k)
+    h_x, h_y, h_d, h_swaps = plane_gather(
+        copies, h_ref, hall_ref.at[0], hall_ref.at[1], lambda i: i, t, rows, ids
+    )
+    wu_step, wu_swaps = line_gather(copies, wu_ref, wu4_ref, nz, ids, k)
+    wd_step, wd_swaps = line_gather(copies, wd_own, wd4_ref, nz, ids, k)
+    g_x, g_y, g_d, _ = plane_gather(copies, g_ref, gall_ref, None, lambda i: i, t, rows, ids)
+    keep(h_ref, hall_ref.at[0, t])
+    keep(g_ref, gall_ref.at[t])
+    keep(wq_ref, wq4_ref.at[z])
+    keep(wu_ref, wu4_ref.at[z])
+    keep(wd_own, wd4_ref.at[z])
+    keep(sm_ref, sm4_ref.at[z])
+    own_slice = z == t
+    half = shard // 2
+    mine = pl.ds(k * half, half)
+    whole = pltpu.make_async_copy(wo_ref, wo1_ref, local_sems.at[len(local_copies)])
+    pl.when(own_slice)(whole.start)
+    wo_up = copies.make(
+        wo_ref.at[mine], wo1_ref.at[mine], (c, jnp.minimum(z + 1, nz - 1)), when=own_slice & (z < nz - 1)
+    )
+    wo_down = copies.make(
+        wo_ref.at[mine], wo1_ref.at[mine], (c, jnp.maximum(z - 1, 0)), when=own_slice & (z > 0)
+    )
+    pl.when(own_slice & (z < nz - 1))(wo_up.start)
+    pl.when(own_slice & (z > 0))(wo_down.start)
+
+    from_x = h_x()
+    from_y = h_y()
+    wq_step(0)
+    h_d(from_x, from_y)
+    wq_step(1)
+    wu_step(0)
+    g_from_x = g_x()
+    g_from_y = g_y()
+    wq_step(2)
+    wd_step(0)
+    wu_step(1)
+    above, below = z > t, z < t
+    relay_up, relay_down = above & (z < nz - 1), below & (z > 0)
+    pl.when(above)(wo_up.wait_recv)
+    pl.when(below)(wo_down.wait_recv)
+    wo_on_up = copies.make(
+        wo1_ref.at[mine], wo1_ref.at[mine], (c, jnp.minimum(z + 1, nz - 1)), when=relay_up, like=wo_up
+    )
+    wo_on_down = copies.make(
+        wo1_ref.at[mine], wo1_ref.at[mine], (c, jnp.maximum(z - 1, 0)), when=relay_down, like=wo_down
+    )
+    pl.when(relay_up)(wo_on_up.start)
+    pl.when(relay_down)(wo_on_down.start)
+    wo_swap = copies.make(wo1_ref.at[mine], wo1_ref.at[mine], (pn, z), when=above | below)
+    pl.when(above | below)(wo_swap.start)
+    wd_step(1)
+    wu_step(2)
+    wd_step(2)
+    g_from_x.wait_recv()
+    g_from_y.wait_recv()
+    for copy in small:
+        copy.wait_recv()
+    for copy in h_swaps:
+        copy.wait_recv()
+    for swaps in (wq_swaps, wu_swaps, wd_swaps):
+        for swap, ok in swaps:
+            run_when(ok, swap.wait_recv)
+    pl.when(above | below)(wo_swap.wait_recv)
+    for copy in local_copies:
+        copy.wait()
+    pl.when(own_slice)(whole.wait)
+    copies.finish()
+
+
+def reduce_kernel(
+    nz,
+    e_ref,
+    o_ref,
+    gq_ref,
+    gu_ref,
+    gd_ref,
+    go_ref,
+    vec_ref,
+    eall_ref,
+    oall_ref,
+    fq_ref,
+    fu_ref,
+    fd_ref,
+    fo_ref,
+    vsum_ref,
+    rq_ref,
+    ru_ref,
+    rd_ref,
+    ro_ref,
+    uq_ref,
+    uu_ref,
+    ud_ref,
+    uo_ref,
+    dq_ref,
+    du_ref,
+    dd_ref,
+    do_ref,
+    vz_ref,
+    vs_ref,
+    vp_ref,
+    send_sems,
+    recv_sems,
+    local_sems,
+):
+    c, z = lax.axis_index("ctx"), lax.axis_index("fsdp")
+    k, t = c % 2, c // 2
+    xn, yn, pn = flip(c, 2), flip(c, 4), flip(c, 1)
+    dn = flip(xn, 4)
+    above_id, below_id = jnp.minimum(z + 1, nz - 1), jnp.maximum(z - 1, 0)
+    others = [(z + d) % nz for d in range(1, nz)]
+    plane = [xn, yn, dn, pn, flip(xn, 1), flip(yn, 1), flip(dn, 1)]
+    greet([((peer, z), None) for peer in plane] + [((c, other), None) for other in others])
+    copies = Copies(send_sems, recv_sems)
+    arrays = (
+        (gq_ref, rq_ref, uq_ref, dq_ref, fq_ref),
+        (gu_ref, ru_ref, uu_ref, du_ref, fu_ref),
+        (gd_ref, rd_ref, ud_ref, dd_ref, fd_ref),
+    )
+    half = gq_ref.shape[1] // 2
+    mine = pl.ds(k * half, half)
+    theirs = pl.ds((1 - k) * half, half)
+
+    exchanged = []
+    for source, received, _, _, _ in arrays:
+        copy = copies.make(source.at[:, theirs], received, (pn, z))
+        copy.start()
+        exchanged.append(copy)
+    o_exchanged = copies.make(go_ref.at[theirs], ro_ref, (pn, z))
+    o_exchanged.start()
+    vec_out = [copies.make(vec_ref.at[other], vz_ref.at[z], (c, other)) for other in others]
+    for copy in vec_out:
+        copy.start()
+    scattered = []
+    for source, target in ((o_ref, oall_ref), (e_ref, eall_ref)):
+        for peer in (xn, yn, dn):
+            copy = copies.make(source.at[peer // 2], target.at[t], (peer, z))
+            copy.start()
+            scattered.append(copy)
+    own_e = pltpu.make_async_copy(e_ref.at[t], eall_ref.at[t], local_sems.at[0])
+    own_o = pltpu.make_async_copy(o_ref.at[t], oall_ref.at[t], local_sems.at[1])
+    own_e.start()
+    own_o.start()
+
+    for copy, (source, received, _, _, _) in zip(exchanged, arrays):
+        copy.wait_recv()
+        for zz in range(nz):
+            received[zz] = (
+                received[zz].astype(jnp.float32) + source[zz, mine].astype(jnp.float32)
+            ).astype(jnp.bfloat16)
+    o_exchanged.wait_recv()
+    ro_ref[...] = (ro_ref[...].astype(jnp.float32) + go_ref[mine].astype(jnp.float32)).astype(
+        jnp.bfloat16
+    )
+
+    chains = []
+    for _, total, up, down, _ in arrays:
+        chains.append((total, up, down))
+    up_sends, down_sends = {}, {}
+    for number, (total, up, down) in enumerate(chains):
+        for owner in range(nz):
+            up_sends[number, owner] = copies.make(
+                total.at[owner], up.at[owner], (c, above_id), when=z < owner
+            )
+            down_sends[number, owner] = copies.make(
+                total.at[owner], down.at[owner], (c, below_id), when=z > owner
+            )
+    order = list(range(len(chains)))
+
+    def add_into(total, incoming, owner):
+        total[owner] = (
+            total[owner].astype(jnp.float32) + incoming[owner].astype(jnp.float32)
+        ).astype(jnp.bfloat16)
+
+    for place in range(nz):
+
+        @pl.when(z == place)
+        def _():
+            events = []
+            for owner in range(place, nz):
+                if place > 0 or owner > place:
+                    events.append((nz - 1 - owner + place, 0, owner))
+            for owner in range(place + 1):
+                if place < nz - 1 or owner < place:
+                    events.append((owner + nz - 1 - place, 1, owner))
+            for time, way, owner in sorted(events):
+                for number in order:
+                    total, up, down = chains[number]
+                    if way == 0:
+                        if place > 0:
+                            up_sends[number, owner].wait_recv()
+                            add_into(total, up, owner)
+                        if owner > place:
+                            up_sends[number, owner].start()
+                    else:
+                        if place < nz - 1:
+                            down_sends[number, owner].wait_recv()
+                            add_into(total, down, owner)
+                        if owner < place:
+                            down_sends[number, owner].start()
+
+    o_up = copies.make(ro_ref, uo_ref, (c, above_id), when=z < t)
+    o_down = copies.make(ro_ref, do_ref, (c, below_id), when=z > t)
+
+    def take(incoming):
+        ro_ref[...] = (ro_ref[...].astype(jnp.float32) + incoming[...].astype(jnp.float32)).astype(
+            jnp.bfloat16
+        )
+
+    @pl.when((z <= t) & (z > 0))
+    def _():
+        o_up.wait_recv()
+        take(uo_ref)
+
+    pl.when(z < t)(o_up.start)
+
+    @pl.when((z >= t) & (z < nz - 1))
+    def _():
+        o_down.wait_recv()
+        take(do_ref)
+
+    pl.when(z > t)(o_down.start)
+
+    for copy in vec_out:
+        copy.wait_recv()
+    total = vec_ref[z]
+    for other in others:
+        total = total + vz_ref[other]
+    vs_ref[...] = total
+    vec_plane = [copies.make(vs_ref, vp_ref.at[c], (peer, z)) for peer in plane]
+    for copy in vec_plane:
+        copy.start()
+
+    ids = (c, z, xn, yn, pn)
+    kept = 2
+    stages = []
+    for total, (_, _, _, _, final) in zip((rq_ref, ru_ref, rd_ref), arrays):
+        own = total.at[z]
+        copy = pltpu.make_async_copy(own, final.at[k, t], local_sems.at[kept])
+        copy.start()
+        kept += 1
+        stages.append((plane_share(copies, own, final, ids, k, t, half), copy))
+    source_here = t == z
+    source_x, source_y, source_d = flip(t, 1) == z, flip(t, 2) == z, flip(flip(t, 1), 2) == z
+    o_own = pltpu.make_async_copy(ro_ref, fo_ref.at[k], local_sems.at[kept])
+    top, bottom = pl.ds(0, half // 2), pl.ds(half // 2, half // 2)
+    o_x = copies.make(ro_ref, fo_ref.at[k], (xn, z), when=source_here)
+    o_y = copies.make(ro_ref, fo_ref.at[k], (yn, z), when=source_here)
+
+    @pl.when(source_here)
+    def _():
+        o_own.start()
+        o_x.start()
+        o_y.start()
+
+    o_fx = copies.make(fo_ref.at[k, top], fo_ref.at[k, top], (yn, z), when=source_x)
+    o_fy = copies.make(fo_ref.at[k, bottom], fo_ref.at[k, bottom], (xn, z), when=source_y)
+    o_swap = copies.make(fo_ref.at[k], fo_ref.at[k], (pn, z))
+
+    for (on_x, _, _, _), _ in stages:
+        on_x()
+    for (_, on_y, _, _), _ in stages:
+        on_y()
+
+    @pl.when(source_x)
+    def _():
+        o_x.wait_recv()
+        o_fx.start()
+
+    @pl.when(source_y)
+    def _():
+        o_y.wait_recv()
+        o_fy.start()
+
+    pl.when(source_here)(o_own.wait)
+
+    @pl.when(source_d)
+    def _():
+        o_fx.wait_recv()
+        o_fy.wait_recv()
+
+    o_swap.start()
+    for (_, _, on_diagonal, _), _ in stages:
+        on_diagonal()
+    for copy in vec_plane:
+        copy.wait_recv()
+    vsum = vs_ref[...]
+    for peer in plane:
+        vsum = vsum + vp_ref[peer]
+    vsum_ref[...] = vsum
+    for (_, _, _, swaps), copy in stages:
+        for swap in swaps:
+            swap.wait_recv()
+        copy.wait()
+    o_swap.wait_recv()
+    for copy in scattered:
+        copy.wait_recv()
+    own_e.wait()
+    own_o.wait()
+    copies.finish()
+
+
+def plane_share(copies, own, final, ids, k, t, rows):
+    c, z, xn, yn, pn = ids
+    top, bottom = pl.ds(0, rows // 2), pl.ds(rows // 2, rows // 2)
+    tx, ty, td = flip(t, 1), flip(t, 2), flip(flip(t, 1), 2)
+    to_x = copies.make(own, final.at[k, t], (xn, z))
+    to_y = copies.make(own, final.at[k, t], (yn, z))
+    to_p = copies.make(own, final.at[k, t], (pn, z))
+    to_x.start()
+    to_y.start()
+    to_p.start()
+    swaps = [to_p]
+    hop_y = copies.make(final.at[k, tx, top], final.at[k, tx, top], (yn, z))
+    hop_x = copies.make(final.at[k, ty, bottom], final.at[k, ty, bottom], (xn, z))
+
+    def swap(place):
+        copy = copies.make(place, place, (pn, z))
+        copy.start()
+        swaps.append(copy)
+
+    def on_x():
+        to_x.wait_recv()
+        hop_y.start()
+        swap(final.at[k, tx])
+
+    def on_y():
+        to_y.wait_recv()
+        hop_x.start()
+        swap(final.at[k, ty])
+
+    def on_diagonal():
+        hop_y.wait_recv()
+        swap(final.at[k, td, top])
+        hop_x.wait_recv()
+        swap(final.at[k, td, bottom])
+
+    return on_x, on_y, on_diagonal, swaps
+
+
+NN = (((1,), (0,)), ((), ()))
+NT = (((1,), (1,)), ((), ()))
+TN = (((0,), (0,)), ((), ()))
+
+
+def mm(left, right, dims=NN):
+    return lax.dot_general(left, right, dims, preferred_element_type=jnp.float32)
+
+
+def norm_rows(values_in):
+    centre = jnp.mean(values_in, axis=-1, keepdims=True)
+    mean_removed = values_in - centre
+    inverse_deviation = lax.rsqrt(
+        jnp.mean(mean_removed * mean_removed, axis=-1, keepdims=True) + EPS
+    )
+    return mean_removed * inverse_deviation, inverse_deviation
+
+
+def slice_kernel(wqkv_ref, wup_ref, wq_ref, wu_ref):
+    t = lax.axis_index("ctx") // 2
+    part = wq_ref.shape[1] // 3
+    chips = wqkv_ref.shape[1] // wq_ref.shape[1]
+    for chip in range(chips):
+
+        @pl.when(t == chip)
+        def _():
+            for source, target in ((wqkv_ref, wq_ref), (wup_ref, wu_ref)):
+                for piece in range(target.shape[1] // part):
+                    first = (piece * chips + chip) * part
+                    target[:, piece * part : (piece + 1) * part] = source[:, first : first + part]
+
+
+def qkv_kernel(pos_ref, h_ref, w_ref, b_ref, gain_ref, shift_ref, rope_ref, q_ref, k_ref, v_ref, kt_ref, vt_ref):
+    step = pl.program_id(0)
+    part = q_ref.shape[1]
+    standardized, _ = norm_rows(h_ref[0].astype(jnp.float32))
+    normed = (standardized * gain_ref[...] + shift_ref[...]).astype(jnp.bfloat16)
+    projected = mm(normed, w_ref[...]) + b_ref[...]
+    both = projected[:, : 2 * part]
+    wide = both.shape[1]
+    tables = [
+        jnp.concatenate([rope_ref[:, 128 * n : 128 * n + 128]] * (wide // 128), axis=1)
+        for n in range(3)
+    ]
+    turned = (
+        both * tables[0]
+        + pltpu.roll(both, wide - ROT // 2, 1) * tables[1]
+        + pltpu.roll(both, ROT // 2, 1) * tables[2]
+    )
+    blocks = both.shape[0] // BLK
+    for block in range(blocks):
+        place = pl.ds(pl.multiple_of(pos_ref[step * blocks + block] * BLK, BLK), BLK)
+        rows = slice(block * BLK, (block + 1) * BLK)
+        q_ref[place, :] = (turned[rows, :part].astype(jnp.bfloat16) * (HD**-0.5)).astype(jnp.bfloat16)
+        key_rows = turned[rows, part:]
+        value_rows = projected[rows, 2 * part :]
+        k_ref[place, :] = key_rows.astype(jnp.bfloat16)
+        v_ref[place, :] = value_rows.astype(jnp.bfloat16)
+        kt_ref[:, place] = key_rows.T.astype(jnp.bfloat16)
+        vt_ref[:, place] = value_rows.T.astype(jnp.bfloat16)
+
+
+def head_rows(rows, head):
+    lanes = lax.broadcasted_iota(jnp.int32, rows.shape, 1)
+    inside = (lanes >= head * HD) & (lanes < (head + 1) * HD)
+    return jnp.where(inside, rows, jnp.zeros_like(rows))
+
+
+def attention_kernel(pos_ref, q_ref, k_ref, vt_ref, o_ref, lse_ref):
+    step = pl.program_id(0)
+    part = k_ref.shape[1]
+    heads = part // HD
+    kstep = 2 * BLK
+    position = pos_ref[step]
+    query = q_ref[pl.ds(pl.multiple_of(position * BLK, BLK), BLK), :]
+    per_head = [head_rows(query, head) for head in range(heads)]
+
+    def visit(number, state, masked):
+        place = pl.ds(pl.multiple_of(number * kstep, kstep), kstep)
+        keys = k_ref[place, :]
+        result = []
+        for head in range(heads):
+            top, total, acc = state[head]
+            logits = mm(keys, per_head[head], NT)
+            if masked:
+                key_pos = number * kstep + lax.broadcasted_iota(jnp.int32, logits.shape, 0)
+                query_pos = position * BLK + lax.broadcasted_iota(jnp.int32, logits.shape, 1)
+                logits = jnp.where(key_pos <= query_pos, logits, NEG)
+            new_top = jnp.maximum(top, jnp.max(logits, axis=0, keepdims=True))
+            fade = jnp.exp(top - new_top)
+            probs = jnp.exp(logits - new_top)
+            total = total * fade + jnp.sum(probs, axis=0, keepdims=True)
+            values = vt_ref[head * HD : (head + 1) * HD, place]
+            acc = acc * fade + mm(values, probs.astype(jnp.bfloat16))
+            result.append((new_top, total, acc))
+        return tuple(result)
+
+    start = tuple(
+        (
+            jnp.full((1, BLK), NEG, jnp.float32),
+            jnp.zeros((1, BLK), jnp.float32),
+            jnp.zeros((HD, BLK), jnp.float32),
+        )
+        for _ in range(heads)
+    )
+    last = position // 2
+    state = lax.fori_loop(0, last, lambda n, s: visit(n, s, False), start)
+    state = visit(last, state, True)
+    rows = jnp.concatenate([acc / total for _, total, acc in state], axis=0)
+    o_ref[...] = rows.T.astype(jnp.bfloat16)
+    for head in range(heads):
+        lse_ref[0, head : head + 1, :] = state[head][0] + jnp.log(state[head][1])
+
+
+def attention_grad_kernel(
+    pos_ref, order_ref, q_ref, k_ref, v_ref, kt_ref, do_ref, o_ref, lse_ref, dq_ref, own_ref, sent_ref, dk_ref, dv_ref
+):
+    step = pl.program_id(0)
+    part = k_ref.shape[1]
+    heads = part // HD
+    kstep = 2 * BLK
+    position = pos_ref[step]
+
+    @pl.when(step == 0)
+    def _():
+        dk_ref[...] = jnp.zeros_like(dk_ref)
+        dv_ref[...] = jnp.zeros_like(dv_ref)
+
+    query = q_ref[pl.ds(pl.multiple_of(position * BLK, BLK), BLK), :]
+    d_out = do_ref[...]
+    queries = jnp.concatenate([head_rows(query, head) for head in range(heads)], axis=0)
+    d_outs = jnp.concatenate([head_rows(d_out, head) for head in range(heads)], axis=0)
+    product = d_out.astype(jnp.float32) * o_ref[...].astype(jnp.float32)
+    head_of = lax.broadcasted_iota(jnp.int32, (8, part), 1) // HD
+    pick = (head_of == lax.broadcasted_iota(jnp.int32, (8, part), 0)).astype(jnp.float32)
+    delta = lax.dot_general(
+        pick, product, NT, precision=lax.Precision.HIGHEST, preferred_element_type=jnp.float32
+    )
+    log_total = lse_ref[0]
+
+    def visit(number, state, masked):
+        place = pl.ds(pl.multiple_of(number * kstep, kstep), kstep)
+        keys, values = k_ref[place, :], v_ref[place, :]
+        probs_all, d_logits_all, result = [], [], []
+        for head in range(heads):
+            rows = slice(head * BLK, (head + 1) * BLK)
+            logits = mm(keys, queries[rows], NT)
+            probs = jnp.exp(logits - log_total[head : head + 1, :])
+            if masked:
+                key_pos = number * kstep + lax.broadcasted_iota(jnp.int32, logits.shape, 0)
+                query_pos = position * BLK + lax.broadcasted_iota(jnp.int32, logits.shape, 1)
+                probs = jnp.where(key_pos <= query_pos, probs, 0.0)
+            d_probs = mm(values, d_outs[rows], NT)
+            d_logits = (probs * (d_probs - delta[head : head + 1, :])).astype(jnp.bfloat16)
+            probs_all.append(probs.astype(jnp.bfloat16))
+            d_logits_all.append(d_logits)
+            result.append(state[head] + mm(kt_ref[head * HD : (head + 1) * HD, place], d_logits))
+        dv_ref[place, :] += mm(jnp.concatenate(probs_all, axis=1), d_outs)
+        dk_ref[place, :] += mm(jnp.concatenate(d_logits_all, axis=1), queries)
+        return tuple(result)
+
+    start = tuple(jnp.zeros((HD, BLK), jnp.float32) for _ in range(heads))
+    last = position // 2
+    state = lax.fori_loop(0, last, lambda n, s: visit(n, s, False), start)
+    state = visit(last, state, True)
+    dq_ref[...] = jnp.concatenate(state, axis=0).T * (HD**-0.5)
+
+    @pl.when(step == pl.num_programs(0) - 1)
+    def _():
+        blocks = own_ref.shape[0] // BLK
+        for block in range(2 * blocks):
+            place = pl.ds(pl.multiple_of(order_ref[block] * BLK, BLK), BLK)
+            if block < blocks:
+                rows = slice(block * BLK, (block + 1) * BLK)
+                own_ref[rows, :part] = dk_ref[place, :]
+                own_ref[rows, part:] = dv_ref[place, :]
+            else:
+                rows = slice((block - blocks) * BLK, (block - blocks + 1) * BLK)
+                sent_ref[rows, :part] = dk_ref[place, :].astype(jnp.bfloat16)
+                sent_ref[rows, part:] = dv_ref[place, :].astype(jnp.bfloat16)
+
+
+def swap_kernel(source_ref, target_ref, send_sem, recv_sem):
+    c, z = lax.axis_index("ctx"), lax.axis_index("fsdp")
+    partner = (flip(c, 1), z)
+    greet([(partner, None)])
+    copy = pltpu.make_async_remote_copy(
+        src_ref=source_ref,
+        dst_ref=target_ref,
+        send_sem=send_sem,
+        recv_sem=recv_sem,
+        device_id=partner,
+        device_id_type=MESH_IDS,
+    )
+    copy.start()
+    copy.wait()
+
+
+def qkv_grad_kernel(
+    h_ref, dq_ref, own_ref, got_ref, rope_ref, w_ref, gain_ref, shift_ref, gain2_ref, d2_ref,
+    gq_ref, e_ref, bias_ref, norm_ref, acc_ref,
+):
+    step = pl.program_id(0)
+    part = dq_ref.shape[1]
+
+    @pl.when(step == 0)
+    def _():
+        acc_ref[...] = jnp.zeros_like(acc_ref)
+        bias_ref[...] = jnp.zeros_like(bias_ref)
+        norm_ref[...] = jnp.zeros_like(norm_ref)
+
+    standardized, _ = norm_rows(h_ref[0].astype(jnp.float32))
+    normed = (standardized * gain_ref[...] + shift_ref[...]).astype(jnp.bfloat16)
+    key_value = own_ref[...] + got_ref[...].astype(jnp.float32)
+    both = jnp.concatenate([dq_ref[...], key_value[:, :part]], axis=1)
+    wide = both.shape[1]
+    tables = [
+        jnp.concatenate([rope_ref[:, 128 * n : 128 * n + 128]] * (wide // 128), axis=1)
+        for n in range(3)
+    ]
+    turned = (
+        both * tables[0]
+        - pltpu.roll(both, wide - ROT // 2, 1) * tables[1]
+        - pltpu.roll(both, ROT // 2, 1) * tables[2]
+    )
+    d_qkv = jnp.concatenate([turned, key_value[:, part:]], axis=1)
+    d_qkv16 = d_qkv.astype(jnp.bfloat16)
+    bias_ref[...] += jnp.sum(d_qkv, axis=0, keepdims=True)
+    acc_ref[...] += mm(normed, d_qkv16, TN)
+    d_normed = mm(d_qkv16, w_ref[...], NT)
+    norm_ref[0:1, :] += jnp.sum(d_normed * standardized, axis=0, keepdims=True)
+    norm_ref[1:2, :] += jnp.sum(d_normed, axis=0, keepdims=True)
+    e_ref[...] = (d_normed * gain_ref[...] + d2_ref[...] * gain2_ref[...]).astype(jnp.bfloat16)
+
+    @pl.when(step == pl.num_programs(0) - 1)
+    def _():
+        gq_ref[...] = acc_ref[...].astype(jnp.bfloat16)
+
+
+def assemble_kernel(fq_ref, fu_ref, fd_ref, fo_ref, gq_ref, gu_ref, gd_ref, go_ref):
+    cores, chips, half, _ = fq_ref.shape
+    part = fq_ref.shape[3] // 3
+    for core in range(cores):
+        rows = slice(core * half, (core + 1) * half)
+        go_ref[rows, :] = fo_ref[core].astype(jnp.float32)
+        for chip in range(chips):
+            for source, target in ((fq_ref, gq_ref), (fu_ref, gu_ref)):
+                for piece in range(source.shape[3] // part):
+                    first = (piece * chips + chip) * part
+                    target[rows, first : first + part] = source[
+                        core, chip, :, piece * part : (piece + 1) * part
+                    ].astype(jnp.float32)
+            first = chip * cores * half + core * half
+            gd_ref[first : first + half, :] = fd_ref[core, chip].astype(jnp.float32)
+
+
+def rotary_lanes(position_list):
+    half_rot = ROT // 2
+    inverse = jnp.power(jnp.float32(10000.0), -2.0 * jnp.arange(half_rot, dtype=jnp.float32) / ROT)
+    angle = position_list.astype(jnp.float32)[:, None] * inverse[None, :]
+    cosine, sine = jnp.cos(angle), jnp.sin(angle)
+    rest = jnp.zeros((position_list.shape[0], HD - ROT), jnp.float32)
+    nothing = jnp.zeros_like(sine)
+    one = [cosine, cosine, rest + 1.0]
+    upper = [-sine, nothing, rest]
+    lower = [nothing, sine, rest]
+    return jnp.concatenate((one + one) + (upper + upper) + (lower + lower), axis=1)
+
+
+VMEM_SPEC = pl.BlockSpec(memory_space=pltpu.VMEM)
+ANY_SPEC = pl.BlockSpec(memory_space=pl.ANY)
+VMEM_LIMIT = 56 * 1024 * 1024
+
+
+def shape_of(shape, kind=jnp.bfloat16):
+    return jax.ShapeDtypeStruct(shape, kind)
+
+
+def sliced_layer(
+    nz,
+    hidden_in,
+    norm1_gain,
+    attention_norm_bias,
+    qkv_weight,
+    qkv_bias,
+    out_weight,
+    out_bias,
+    norm2_gain,
+    feedforward_norm_bias,
+    up_weight,
+    up_bias,
+    down_weight,
+    down_bias,
+    cotangent,
+    block_order,
+):
+    f32, b16 = jnp.float32, jnp.bfloat16
+    h, g = hidden_in[0], cotangent[0]
+    local_rows, width = h.shape
+    chips = lax.axis_size("ctx") // 2
+    c, z = lax.axis_index("ctx"), lax.axis_index("fsdp")
+    k, t = c % 2, c // 2
+    shard = qkv_weight.shape[0]
+    part = width // chips
+    heads = part // HD
+    hidden = up_weight.shape[1] // chips
+    rows = chips * local_rows
+    all_rows = 2 * rows
+    sides = local_rows // BLK
+
+    order = block_order.reshape(chips, 2, sides)
+    order = jnp.stack([order[:, k], order[:, 1 - k]]).reshape(2 * chips * sides)
+    own_order = order[: chips * sides]
+    positions = (order[:, None] * BLK + jnp.arange(BLK, dtype=jnp.int32)[None, :]).reshape(all_rows)
+    rope = rotary_lanes(positions)
+
+    small = [norm1_gain, attention_norm_bias, norm2_gain, feedforward_norm_bias, out_bias, down_bias, qkv_bias, up_bias]
+    cuts = [0]
+    for vector in small:
+        cuts.append(cuts[-1] + vector.shape[0])
+    small_rows = -(-cuts[-1] // (16 * 128)) * 16
+    sm = jnp.pad(jnp.concatenate(small), (0, small_rows * 128 - cuts[-1])).reshape(small_rows, 128)
+
+    wq, wu = pl.pallas_call(
+        slice_kernel,
+        out_shape=(shape_of((shard, 3 * part)), shape_of((shard, hidden))),
+        in_specs=[VMEM_SPEC] * 2,
+        out_specs=(VMEM_SPEC,) * 2,
+        name="slice_weights",
+    )(qkv_weight, up_weight)
+
+    hall, gall, wq4, wu4, wd4, wo1, sm4 = pl.pallas_call(
+        functools.partial(gather_kernel, nz),
+        out_shape=(
+            shape_of((2, chips, local_rows, width)),
+            shape_of((chips, local_rows, width)),
+            shape_of((nz, shard, 3 * part)),
+            shape_of((nz, shard, hidden)),
+            shape_of((nz, shard, width)),
+            shape_of((part, width)),
+            shape_of((nz, small_rows, 128)),
+        ),
+        in_specs=[VMEM_SPEC] * 7,
+        out_specs=(ANY_SPEC,) * 7,
+        scratch_shapes=[
+            pltpu.SemaphoreType.DMA((96,)),
+            pltpu.SemaphoreType.DMA((96,)),
+            pltpu.SemaphoreType.DMA((8,)),
+        ],
+        compiler_params=pltpu.CompilerParams(collective_id=0, has_side_effects=True),
+        name="gather",
+    )(h, g, wq, wu, down_weight, out_weight, sm)
+
+    flat = sm4.reshape(nz, small_rows * 128).astype(f32)
+    gain1, shift1, gain2, shift2, bout, bdown = (
+        flat[:, cuts[n] : cuts[n + 1]].reshape(1, width) for n in range(6)
+    )
+    bq = lax.dynamic_slice_in_dim(
+        flat[:, cuts[6] : cuts[7]].reshape(3, chips, part), t, 1, 1
+    ).reshape(1, 3 * part)
+    bu = lax.dynamic_slice_in_dim(
+        flat[:, cuts[7] : cuts[8]].reshape(hidden // part, chips, part), t, 1, 1
+    ).reshape(1, hidden)
+    wq_full = wq4.reshape(width, 3 * part)
+    wu_full = wu4.reshape(width, hidden)
+    wd_full = wd4.reshape(hidden, width)
+    h_blocks = hall.reshape(2 * chips, local_rows, width)
+
+    def whole(*shape):
+        return pl.BlockSpec(shape, lambda i, *_: (0,) * len(shape))
+
+    q, key_rows, value_rows, keys_t, values_t = pl.pallas_call(
+        qkv_kernel,
+        grid_spec=pltpu.PrefetchScalarGridSpec(
+            num_scalar_prefetch=1,
+            grid=(2 * chips,),
+            in_specs=[
+                pl.BlockSpec((1, local_rows, width), lambda i, *_: (i, 0, 0)),
+                whole(width, 3 * part),
+                whole(1, 3 * part),
+                whole(1, width),
+                whole(1, width),
+                pl.BlockSpec((local_rows, 384), lambda i, *_: (i, 0)),
+            ],
+            out_specs=(
+                whole(all_rows, part),
+                whole(all_rows, part),
+                whole(all_rows, part),
+                whole(part, all_rows),
+                whole(part, all_rows),
+            ),
+        ),
+        out_shape=(shape_of((all_rows, part)),) * 3 + (shape_of((part, all_rows)),) * 2,
+        compiler_params=pltpu.CompilerParams(vmem_limit_bytes=VMEM_LIMIT),
+        name="qkv",
+    )(order, h_blocks, wq_full, bq, gain1, shift1, rope)
+
+    attended, log_total = pl.pallas_call(
+        attention_kernel,
+        grid_spec=pltpu.PrefetchScalarGridSpec(
+            num_scalar_prefetch=1,
+            grid=(chips * sides,),
+            in_specs=[whole(all_rows, part), whole(all_rows, part), whole(part, all_rows)],
+            out_specs=(
+                pl.BlockSpec((BLK, part), lambda i, *_: (i, 0)),
+                pl.BlockSpec((1, 8, BLK), lambda i, *_: (i, 0, 0)),
+            ),
+        ),
+        out_shape=(shape_of((rows, part)), shape_of((chips * sides, 8, BLK), f32)),
+        compiler_params=pltpu.CompilerParams(vmem_limit_bytes=VMEM_LIMIT),
+        name="attention",
+    )(own_order, q, key_rows, values_t)
+
+    h_own = hall[0].reshape(rows, width).astype(f32)
+    g_own = gall.reshape(rows, width)
+    standardized, _ = norm_rows(h_own)
+    normed2 = (standardized * gain2 + shift2).astype(b16)
+    up = mm(normed2, wu_full) + bu
+    act = gelu_exact(up).astype(b16)
+    d_up = mm(g_own, wd_full, NT) * gelu_slope(up)
+    d_up16 = d_up.astype(b16)
+    out_part = (mm(attended, wo1) + mm(act, wd_full)).astype(b16)
+    grad_d = mm(act, g_own, TN).astype(b16)
+    grad_u = mm(normed2, d_up16, TN).astype(b16)
+    grad_bu = jnp.sum(d_up, axis=0)
+    d_normed2 = mm(d_up16, wu_full, NT)
+    grad_gain2 = jnp.sum(d_normed2 * standardized, axis=0)
+    grad_shift2 = jnp.sum(d_normed2, axis=0)
+    grad_o = mm(attended, g_own, TN).astype(b16)
+    d_att = mm(g_own, wo1, NT).astype(b16)
+
+    d_query, kv_own, kv_sent = pl.pallas_call(
+        attention_grad_kernel,
+        grid_spec=pltpu.PrefetchScalarGridSpec(
+            num_scalar_prefetch=2,
+            grid=(chips * sides,),
+            in_specs=[
+                whole(all_rows, part),
+                whole(all_rows, part),
+                whole(all_rows, part),
+                whole(part, all_rows),
+                pl.BlockSpec((BLK, part), lambda i, *_: (i, 0)),
+                pl.BlockSpec((BLK, part), lambda i, *_: (i, 0)),
+                pl.BlockSpec((1, 8, BLK), lambda i, *_: (i, 0, 0)),
+            ],
+            out_specs=(
+                pl.BlockSpec((BLK, part), lambda i, *_: (i, 0)),
+                whole(rows, 2 * part),
+                whole(rows, 2 * part),
+            ),
+            scratch_shapes=[pltpu.VMEM((all_rows, part), f32), pltpu.VMEM((all_rows, part), f32)],
+        ),
+        out_shape=(
+            shape_of((rows, part), f32),
+            shape_of((rows, 2 * part), f32),
+            shape_of((rows, 2 * part)),
+        ),
+        compiler_params=pltpu.CompilerParams(vmem_limit_bytes=VMEM_LIMIT),
+        name="attention_grad",
+    )(own_order, order, q, key_rows, value_rows, keys_t, d_att, attended, log_total)
+
+    kv_got = pl.pallas_call(
+        swap_kernel,
+        out_shape=shape_of((rows, 2 * part)),
+        in_specs=[ANY_SPEC],
+        out_specs=ANY_SPEC,
+        scratch_shapes=[pltpu.SemaphoreType.DMA, pltpu.SemaphoreType.DMA],
+        compiler_params=pltpu.CompilerParams(collective_id=1, has_side_effects=True),
+        name="swap",
+    )(kv_sent)
+
+    by_rows = lambda cols: pl.BlockSpec((local_rows, cols), lambda i, *_: (i, 0))
+    grad_q, e_part, grad_bq, grad_norm1 = pl.pallas_call(
+        qkv_grad_kernel,
+        grid=(chips,),
+        in_specs=[
+            pl.BlockSpec((1, local_rows, width), lambda i: (i, 0, 0)),
+            by_rows(part),
+            by_rows(2 * part),
+            by_rows(2 * part),
+            by_rows(384),
+            whole(width, 3 * part),
+            whole(1, width),
+            whole(1, width),
+            whole(1, width),
+            by_rows(width),
+        ],
+        out_specs=(
+            whole(width, 3 * part),
+            by_rows(width),
+            whole(1, 3 * part),
+            whole(8, width),
+        ),
+        out_shape=(
+            shape_of((width, 3 * part)),
+            shape_of((rows, width)),
+            shape_of((1, 3 * part), f32),
+            shape_of((8, width), f32),
+        ),
+        scratch_shapes=[pltpu.VMEM((width, 3 * part), f32)],
+        compiler_params=pltpu.CompilerParams(vmem_limit_bytes=VMEM_LIMIT),
+        name="qkv_grad",
+    )(h_blocks, d_query, kv_own, kv_got, rope, wq_full, gain1, shift1, gain2, d_normed2)
+
+    def spread(values, pieces):
+        slots = jnp.arange(chips)[None, :, None] == t
+        return jnp.where(slots, values.reshape(pieces, 1, part), 0.0).reshape(nz, -1)
+
+    vectors = jnp.concatenate(
+        [
+            grad_norm1[0].reshape(nz, -1),
+            grad_norm1[1].reshape(nz, -1),
+            grad_gain2.reshape(nz, -1),
+            grad_shift2.reshape(nz, -1),
+            jnp.sum(g.astype(f32), axis=0).reshape(nz, -1),
+            spread(grad_bq, 3),
+            spread(grad_bu, hidden // part),
+        ],
+        axis=1,
+    )
+    vec_used = vectors.shape[1]
+    vec_rows = -(-vec_used // (8 * 128)) * 8
+    vectors = jnp.pad(vectors, ((0, 0), (0, vec_rows * 128 - vec_used))).reshape(nz, vec_rows, 128)
+
+    half = shard // 2
+    widths = (3 * part, hidden, width)
+    grads = (
+        grad_q.reshape(nz, shard, 3 * part),
+        grad_u.reshape(nz, shard, hidden),
+        grad_d.reshape(nz, shard, width),
+    )
+    eall, oall, fq, fu, fd, fo, vsum = pl.pallas_call(
+        functools.partial(reduce_kernel, nz),
+        out_shape=(
+            shape_of((chips, local_rows, width)),
+            shape_of((chips, local_rows, width)),
+        )
+        + tuple(shape_of((2, chips, half, cols)) for cols in widths)
+        + (shape_of((2, half, width)), shape_of((vec_rows, 128), f32)),
+        in_specs=[VMEM_SPEC] * 7,
+        out_specs=(ANY_SPEC,) * 6 + (VMEM_SPEC,),
+        scratch_shapes=[pltpu.VMEM((nz, half, cols), b16) for cols in widths]
+        + [pltpu.VMEM((half, width), b16)]
+        + [pltpu.VMEM((nz, half, cols), b16) for cols in widths]
+        + [pltpu.VMEM((half, width), b16)]
+        + [pltpu.VMEM((nz, half, cols), b16) for cols in widths]
+        + [pltpu.VMEM((half, width), b16)]
+        + [
+            pltpu.VMEM((nz, vec_rows, 128), f32),
+            pltpu.VMEM((vec_rows, 128), f32),
+            pltpu.VMEM((2 * chips, vec_rows, 128), f32),
+            pltpu.SemaphoreType.DMA((96,)),
+            pltpu.SemaphoreType.DMA((96,)),
+            pltpu.SemaphoreType.DMA((8,)),
+        ],
+        compiler_params=pltpu.CompilerParams(
+            collective_id=2, has_side_effects=True, vmem_limit_bytes=VMEM_LIMIT
+        ),
+        name="reduce",
+    )(
+        e_part.reshape(chips, local_rows, width),
+        out_part.reshape(chips, local_rows, width),
+        *grads,
+        grad_o,
+        vectors,
+    )
+
+    grad_qkv, grad_up, grad_down, grad_out = pl.pallas_call(
+        assemble_kernel,
+        out_shape=(
+            shape_of(qkv_weight.shape, f32),
+            shape_of(up_weight.shape, f32),
+            shape_of(down_weight.shape, f32),
+            shape_of(out_weight.shape, f32),
+        ),
+        in_specs=[VMEM_SPEC] * 4,
+        out_specs=(VMEM_SPEC,) * 4,
+        compiler_params=pltpu.CompilerParams(vmem_limit_bytes=VMEM_LIMIT),
+        name="assemble",
+    )(fq, fu, fd, fo)
+
+    residual = h.astype(f32)
+    own_standardized, own_deviation = norm_rows(residual)
+    hidden_out = (residual + bout + bdown + jnp.sum(oall.astype(f32), axis=0)).astype(b16)
+    e_total = jnp.sum(eall.astype(f32), axis=0)
+    hidden_grad = g.astype(f32) + own_deviation * (
+        e_total
+        - jnp.mean(e_total, axis=-1, keepdims=True)
+        - own_standardized * jnp.mean(e_total * own_standardized, axis=-1, keepdims=True)
+    )
+    final = vsum.reshape(-1)
+    sizes = [shard] * 5 + [qkv_bias.shape[0], up_bias.shape[0]]
+    pieces, first = [], 0
+    for size in sizes:
+        pieces.append(final[first : first + size])
+        first += size
+    g_gain1, g_shift1, g_gain2, g_shift2, g_bias, g_bq, g_bu = pieces
+    return (
+        hidden_out[None],
+        hidden_grad[None],
+        g_gain1,
+        g_shift1,
+        grad_qkv,
+        g_bq,
+        grad_out,
+        g_bias,
+        g_gain2,
+        g_shift2,
+        grad_up,
+        g_bu,
+        grad_down,
+        g_bias,
+    )
+
+
+def sliced_fits(mesh):
+    return mesh.shape["ctx"] == 8 and mesh.shape["fsdp"] == 4
+
+
 def solution(mesh):
     in_specs = (
         P("fsdp", "ctx", None),
@@ -455,4 +1603,7 @@
         P("fsdp", None),
         P("fsdp"),
     )
+    local = whole_parameter_layer
+    if sliced_fits(mesh):
+        local = functools.partial(sliced_layer, mesh.shape["fsdp"])
     return jax.shard_map(local, mesh=mesh, in_specs=in_specs, out_specs=out_specs, check_vma=False)

time: 1130 us -> 314 us (0.28)
  waiting for transfers between devices: 814 us -> 0 us
  Pallas kernels: 0 us -> 229 us
  matrix products: 142 us -> 26 us
  blocking collectives: 71.7 us -> 0 us
  between operations: 17.8 us -> 1.08 us
  loops' own time: 16.6 us -> 0 us
    reduce_scatter x6 -> x0, waiting for transfers between devices: 605 us -> none  [the longest x1 165 us: local(): lax.psum_scatter(terms[10], 'fsdp', scatter_dimension=0, tiled=True)]
    pallas_call x0 -> x9, Pallas kernels: none -> 229 us  [the longest x1 74.5 us: sliced_layer(): pl.pallas_call(functools.partial(reduce_kernel, nz), out_shape=(shape_of(...]
    all_gather x6 -> x0, waiting for transfers between devices: 145 us -> none  [the longest x1 44.2 us: local(): lax.all_gather(qkv_weight, 'fsdp', axis=0, tiled=True)]
    dot_general x40 -> x9, matrix products: 142 us -> 26 us  [mm(): lax.dot_general(left, right, dims, preferred_element_type=jnp.float32)]
    psum x1 -> x0, waiting for transfers between devices: 60.8 us -> none  [local(): lax.psum((shares[0], shares[1], shares[2], shares[3], shares[4], shares[5...]
    unnamed x2 -> x0, blocking collectives: 34.4 us -> none
    psum x1 -> x0, blocking collectives: 23.7 us -> none  [local(): lax.psum((shares[0], shares[1], shares[2], shares[3], shares[4], shares[5...]
    concatenate x0 -> x3, local copies, waits for them, and re-layouts: none -> 17.2 us  [the longest x1 11.7 us: rotary_lanes(): jnp.concatenate(one + one + (upper + upper) + (lower + lower), axis=1)]
  transfers between devices with their start and end apart: 13 -> 0, of which waited for: 12 -> 0; matrix products, arithmetic and copies ran while one was open for 17% -> 0% of each run, Pallas kernels for 0% -> 0%
where the time goes in v1:
time: 314 us; the launch traced here: 312 us
  Pallas kernels  229 us (73%)
  local copies, waits for them, and re-layouts  36.6 us (12%)
  matrix products  26 us (8%)
  other arithmetic  19.5 us (6%)
    pallas_call x1, Pallas kernels, sliced_layer(): pl.pallas_call(functools.partial(reduce_kernel, nz), out_shape=(shape_of(...  74.5 us
    pallas_call x1, Pallas kernels, sliced_layer(): pl.pallas_call(functools.partial(gather_kernel, nz), out_shape=(shape_of(...  49 us
    pallas_call x1, Pallas kernels, sliced_layer(): pl.pallas_call(attention_grad_kernel, grid_spec=pltpu.PrefetchScalarGridS...  42.5 us
    pallas_call x1, Pallas kernels, sliced_layer(): pl.pallas_call(attention_kernel, grid_spec=pltpu.PrefetchScalarGridSpec(n...  29.7 us
    dot_general x9, matrix products, mm(): lax.dot_general(left, right, dims, preferred_element_type=jnp.float32)  26 us
    pallas_call x1, Pallas kernels, sliced_layer(): pl.pallas_call(qkv_kernel, grid_spec=pltpu.PrefetchScalarGridSpec(num_sca...  12.8 us
    concatenate x1, local copies, waits for them, and re-layouts, rotary_lanes(): jnp.concatenate(one + one + (upper + upper) + (lower + lower), axis=1)  11.7 us
    pallas_call x1, Pallas kernels, sliced_layer(): pl.pallas_call(qkv_grad_kernel, grid=(chips,), in_specs=[pl.BlockSpec((1,...  9.87 us

profile of v1, /device:TPU:1, one launch (start us, length us, event | category | flops | bytes accessed | tf_op | source)
XLA Modules:
  0.0 312.1 jit_solution(4364362077068137009)
XLA Ops:
  1.9 1.1 convert_reduce_fusion.4
  3.1 1.2 fusion.8
  4.9 0.7 reshape.309
  7.8 1.1 convert_reduce_fusion.5
  9.6 5.5 %concatenate.9 = bf16[2496]{0:T(1024)(128)(2,1)S(1)} concatenate(bf16[192]{0:T(256)(128)(2,1)} %param.16, bf16[192]{0:T(256)(128)(2,1)} %param.17, bf16[192]{0:T(256)(128)(2,1)} %param.22, bf16[192]{0:T(256)(128)(2,1)} %param.23, bf16[192]{0:T(256)(128)(2,1)} %param.21, bf16[192]{0:T(256)(128)(2,1)} %param.27, bf16[576]{0:T(1024)(128)(2,1)} %param.19, bf16[768]{0:T(1024)(128)(2,1)} %param.25), dimensions={0} | concatenate | bytes 9984 | tf_op jit(solution)/shard_map/concatenate | solution.py:1274
  15.7 2.5 slice_weights.1
  18.2 5.5 %multiply_sine_fusion = (f32[2048,8]{1,0:T(8,128)}, f32[2048,8]{1,0:T(8,128)}, f32[2048,8]{1,0:T(8,128)S(1)}) fusion(f32[2048]{0:T(1024)S(1)} %convert_bitcast_fusion.1, f32[8]{0:T(128)S(1)} %multiply_power_fusion), kind=kLoop, calls=%fused_computation.21 | loop fusion | flops 32768 | bytes 204832 | tf_op jit(solution)/shard_map/sin | solution.py:1213
  23.7 1.0 add.144
  24.9 11.7 %concatenate.10.rope_ref = f32[2048,384]{1,0:T(8,128)} concatenate(f32[2048,8]{1,0:T(8,128)S(1)} %get-tuple-element.106, f32[2048,8]{1,0:T(8,128)S(1)} %get-tuple-element.106, f32[2048,48]{1,0:T(8,128)} %add.144, f32[2048,8]{1,0:T(8,128)S(1)} %get-tuple-element.106, f32[2048,8]{1,0:T(8,128)S(1)} %get-tuple-element.106, f32[2048,48]{1,0:T(8,128)} %add.144, ...), dimensions={1} | concatenate | bytes 6291456 | tf_op jit(solution)/shard_map/concatenate | solution.py:1219
  36.5 49.0 %gather.1 = (bf16[2,4,256,768]{3,2,1,0:T(8,128)(2,1)}, bf16[4,256,768]{2,1,0:T(8,128)(2,1)}, bf16[4,192,576]{2,1,0:T(8,128)(2,1)}, bf16[4,192,768]{2,1,0:T(8,128...) custom-call(bf16[256,768]{1,0:T(8,128)(2,1)} %bitcast.76, ...), custom_call_target="tpu_custom_call" | custom-call | tf_op jit(solution)/shard_map/gather/pallas_call | solution.py:1284
  85.6 1.7 convert_reduce_fusion.3
  87.9 2.1 multiply_reduce_fusion.1
  95.9 2.1 convolution_convert_fusion.2
  98.0 1.0 copy.46.do_ref
  100.3 3.0 multiply_convert_fusion
  103.3 3.7 %fusion.29 = (f32[768]{0:T(1024)S(1)}, bf16[1024,768]{1,0:T(8,128)(2,1)}) fusion(f32[1024,768]{1,0:T(8,128)S(1)} %get-tuple-element.113, f32[768]{0:T(1024)S(1)} %copy-done.19, bf16[1024,768]{1,0:T(8,128)(2,1)S(1)} %bitcast.98, bf16[768,768]{1,0:T(8,128)(2,1)S(1)} %bitcast.102), kind=kOutput, calls=%fused_computation.79 | convolution fusion | flops 1217395968 | bytes 7477248 | tf_op jit(solution)/shard_map/dot_general | solution.py:959
  107.2 4.5 %convolution_convert_fusion = bf16[768,768]{1,0:T(8,128)(2,1)} fusion(bf16[1024,768]{1,0:T(8,128)(2,1)} %get-tuple-element.112, bf16[1024,768]{1,0:T(8,128)(2,1)} %bitcast.97), kind=kOutput, calls=%fused_computation.19 | convolution fusion | flops 1208549376 | bytes 4325376 | tf_op jit(solution)/shard_map/dot_general | solution.py:959
  111.8 3.0 fusion.30
  114.8 3.1 fusion.25
  117.9 2.5 convolution_convert_fusion.1
  120.6 12.8 %qkv.1 = (bf16[2048,192]{1,0:T(8,128)(2,1)}, bf16[2048,192]{1,0:T(8,128)(2,1)}, bf16[2048,192]{1,0:T(8,128)(2,1)}, bf16[192,2048]{1,0:T(8,128)(2,1)}, bf16[192,2048]{1,0:T(8,128)(2,1)}) custom-call(s32[16]{0:T(128)} %copy-done.14, bf16[8,256,768]{2,1,0:T(8,128)(2,1)} %bitcast.74, bf16[768,576]{1,0:T(8,128)(2,1)} %bitcast.78, f32[1,576]{1,0:T(1,128)} %reshape.313.b_ref, ...), custom_call_target="tpu_custom_call" | custom-call | tf_op jit(solution)/shard_map/qkv/pallas_call | solution.py:1324
  133.3 29.7 %attention.1 = (bf16[1024,192]{1,0:T(8,128)(2,1)}, f32[8,8,128]{2,1,0:T(8,128)}) custom-call(s32[8]{0:T(128)} %slice.63.pos_ref, bf16[2048,192]{1,0:T(8,128)(2,1)} %get-tuple-element.53.q_ref, bf16[2048,192]{1,0:T(8,128)(2,1)} %get-tuple-element.54.k_ref, bf16[192,2048]{1,0:T(8,128)(2,1)} %get-tuple-element.59.vt_ref), custom_call_target="tpu_custom_call" | custom-call | tf_op jit(solution)/shard_map/attention/pallas_call | solution.py:1350
  163.1 2.9 add_convert_fusion.1
  166.0 1.2 convolution_convert_fusion.3.go_ref
  167.2 42.5 %attention_grad.1 = (f32[1024,192]{1,0:T(8,128)}, f32[1024,384]{1,0:T(8,128)}, bf16[1024,384]{1,0:T(8,128)(2,1)}) custom-call(s32[8]{0:T(128)} %slice.63.pos_ref, s32[16]{0:T(128)} %copy-done.14, bf16[2048,192]{1,0:T(8,128)(2,1)} %get-tuple-element.53.q_ref, bf16[2048,192]{1,0:T(8,128)(2,1)} %get-tuple-element.54.k_ref, ...), custom_call_target="tpu_custom_call" | custom-call | tf_op jit(solution)/shard_map/attention_grad/pallas_call | solution.py:1384
  209.7 2.6 swap.1.got_ref
  212.4 9.9 %qkv_grad.1 = (bf16[768,576]{1,0:T(8,128)(2,1)}, bf16[1024,768]{1,0:T(8,128)(2,1)}, f32[1,576]{1,0:T(1,128)}, f32[8,768]{1,0:T(8,128)}) custom-call(bf16[8,256,768]{2,1,0:T(8,128)(2,1)} %bitcast.75, f32[1024,192]{1,0:T(8,128)} %get-tuple-element.62.dq_ref, f32[1024,384]{1,0:T(8,128)} %get-tuple-element.63.own_ref, bf16[1024,384]{1,0:T(8,128)(2,1)} %swap.1.got_ref, ...), custom_call_target="tpu_custom_call" | custom-call | tf_op jit(solution)/shard_map/qkv_grad/pallas_call | solution.py:1425
  223.2 0.8 slice_reduce_fusion
  224.9 74.5 %reduce.18 = (bf16[4,256,768]{2,1,0:T(8,128)(2,1)}, bf16[4,256,768]{2,1,0:T(8,128)(2,1)}, bf16[2,4,96,576]{3,2,1,0:T(8,128)(2,1)}, bf16[2,4,96,768]{3,2,1,0:T(8,...) custom-call(bf16[4,256,768]{2,1,0:T(8,128)(2,1)} %bitcast.82, ...), custom_call_target="tpu_custom_call" | custom-call | tf_op jit(solution)/shard_map/reduce/pallas_call | solution.py:1484
  299.5 3.0 convert_reduce_fusion
  302.9 1.3 fusion.18
  306.1 5.4 %assemble.1 = (f32[192,2304]{1,0:T(8,128)}, f32[192,3072]{1,0:T(8,128)}, f32[768,768]{1,0:T(8,128)}, f32[192,768]{1,0:T(8,128)}) custom-call(bf16[2,4,96,576]{3,2,1,0:T(8,128)(2,1)} %get-tuple-element.74.fq_ref, bf16[2,4,96,768]{3,2,1,0:T(8,128)(2,1)} %get-tuple-element.75.fu_ref, bf16[2,4,96,768]{3,2,1,0:T(8,128)(2,1)} %get-tuple-element.76.fd_ref, ...), custom_call_target="tpu_custom_call" | custom-call | tf_op jit(solution)/shard_map/assemble/pallas_call | solution.py:1520
  (125 shorter events, 18.2 us)
Async XLA Ops:
  0.7 0.5 copy-start.20
  3.1 1.3 copy-start.10
  7.8 1.1 copy-start.14
  85.6 5.1 %copy-start.6 = (bf16[4,32,128]{2,1,0:T(8,128)(2,1)S(1)}, bf16[4,32,128]{2,1,0:T(8,128)(2,1)}, u32[]{:S(2)}) copy-start(bf16[4,32,128]{2,1,0:T(8,128)(2,1)} %get-tuple-element.50) | copy-start | bytes 98308
  87.9 11.2 %copy-start = (bf16[2,4,256,768]{3,2,1,0:T(8,128)(2,1)S(1)}, bf16[2,4,256,768]{3,2,1,0:T(8,128)(2,1)}, u32[]{:S(2)}) copy-start(bf16[2,4,256,768]{3,2,1,0:T(8,128)(2,1)} %get-tuple-element.51) | copy-start | bytes 9437188
  99.0 0.7 copy-start.19
  99.0 1.3 copy-start.24
  100.3 3.0 copy-start.22
  100.3 3.0 copy-start.26
  103.3 3.9 %copy-start.15 = (pred[768]{0:T(1024)(128)(4,1)S(1)}, pred[768]{0:T(1024)(128)(4,1)}, u32[]{:S(2)}) copy-start(pred[768]{0:T(1024)(128)(4,1)} %broadcast_in_dim.76) | copy-start | bytes 2308
  107.2 4.5 %copy-start.27 = (bf16[4,192,768]{2,1,0:T(8,128)(2,1)S(1)}, bf16[4,192,768]{2,1,0:T(8,128)(2,1)}, u32[]{:S(2)}) copy-start(bf16[4,192,768]{2,1,0:T(8,128)(2,1)} %get-tuple-element.65) | copy-start | bytes 3538948
  107.2 4.5 %copy-start.28 = (bf16[1024,768]{1,0:T(8,128)(2,1)S(1)}, bf16[1024,768]{1,0:T(8,128)(2,1)}, u32[]{:S(2)}) copy-start(bf16[1024,768]{1,0:T(8,128)(2,1)} %get-tuple-element.112) | copy-start | bytes 4718596
  111.8 3.1 copy-start.17
  111.8 3.1 copy-start.18
  111.8 3.1 copy-start.25
  111.8 3.1 copy-start.29
  120.6 42.5 %copy-start.3 = (f32[1024,768]{1,0:T(8,128)S(1)}, f32[1024,768]{1,0:T(8,128)}, u32[]{:S(2)}) copy-start(f32[1024,768]{1,0:T(8,128)} %fusion.30) | copy-start | bytes 9437188
  133.3 29.7 %copy-start.5 = (bf16[192,768]{1,0:T(8,128)(2,1)S(1)}, bf16[192,768]{1,0:T(8,128)(2,1)}, u32[]{:S(2)}) copy-start(bf16[192,768]{1,0:T(8,128)(2,1)} %get-tuple-element.58) | copy-start | bytes 884740
  163.1 2.9 copy-start.4
  163.1 2.9 copy-start.23
  212.3 10.7 %copy-start.21 = (pred[4]{0:T(512)(128)(4,1)S(1)}, pred[4]{0:T(512)(128)(4,1)}, u32[]{:S(2)}) copy-start(pred[4]{0:T(512)(128)(4,1)} %copy-done.20) | copy-start | bytes 16
  212.4 11.8 %copy-start.7 = (f32[4,192]{1,0:T(4,128)S(1)}, f32[4,192]{1,0:T(4,128)}, u32[]{:S(2)}) copy-start(f32[4,192]{1,0:T(4,128)} %reshape.328) | copy-start | bytes 9220
  299.4 3.1 copy-start.1
  299.4 3.1 copy-start.11
  299.4 3.1 copy-start.13
  299.4 3.4 %copy-start.2 = (bf16[1,256,768]{2,1,0:T(8,128)(2,1)S(1)}, bf16[1,256,768]{2,1,0:T(8,128)(2,1)}, u32[]{:S(2)}) copy-start(bf16[1,256,768]{2,1,0:T(8,128)(2,1)} %param.28) | copy-start | bytes 1179652
  299.4 3.4 %copy-start.8 = (f32[768]{0:T(1024)S(1)}, f32[768]{0:T(1024)}, u32[]{:S(2)}) copy-start(f32[768]{0:T(1024)} %add.131) | copy-start | bytes 9220
  299.4 3.4 %copy-start.9 = (f32[768]{0:T(1024)S(1)}, f32[768]{0:T(1024)}, u32[]{:S(2)}) copy-start(f32[768]{0:T(1024)} %add.134) | copy-start | bytes 9220
  302.5 1.7 copy-start.12
  306.1 6.0 %copy-start.16 = (f32[192]{0:T(256)}, f32[192]{0:T(256)S(1)}, u32[]{:S(2)}) copy-start(f32[192]{0:T(256)S(1)} %get-tuple-element.147) | copy-start | bytes 2308

commit v2 on v0

--- a/solution.py
+++ b/solution.py
@@ -1,8 +1,13 @@
+import functools
 import math
+import types
 
 import jax
 import jax.numpy as jnp
+import numpy as np
 from jax import lax
+from jax.experimental import pallas as pl
+from jax.experimental.pallas import tpu as pltpu
 from jax.sharding import PartitionSpec as P
 
 H = 12
@@ -205,7 +210,7 @@
     return (pieces, key_grads, value_grads)
 
 
-def local(
+def whole_parameter_layer(
     hidden_in,
     norm1_gain,
     attention_norm_bias,
@@ -421,6 +426,1180 @@
     )
 
 
+MESH_IDS = pl.DeviceIdType.MESH
+NN = (((1,), (0,)), ((), ()))
+NT = (((1,), (1,)), ((), ()))
+TN = (((0,), (0,)), ((), ()))
+QTILE = 256
+SEMAPHORES = 160
+
+
+def mm(left, right, dims=NN):
+    return lax.dot_general(left, right, dims, preferred_element_type=jnp.float32)
+
+
+def flip(index, bit):
+    return index + bit - 2 * bit * ((index // bit) % 2)
+
+
+def run_when(condition, action):
+    if condition is None:
+        action()
+    else:
+        pl.when(condition)(action)
+
+
+def narrow(values):
+    return values.astype(jnp.bfloat16)
+
+
+def wide(values):
+    return values.astype(jnp.float32)
+
+
+class Copies:
+    def __init__(self, send_sems, recv_sems):
+        self.send_sems, self.recv_sems = send_sems, recv_sems
+        self.count, self.started, self.numbers = 0, [], {}
+
+    def make(self, source, target, device, when=None, like=None):
+        if like is None:
+            number = self.count
+            self.count += 1
+        else:
+            number = self.numbers[id(like)]
+        copy = pltpu.make_async_remote_copy(
+            src_ref=source,
+            dst_ref=target,
+            send_sem=self.send_sems.at[number],
+            recv_sem=self.recv_sems.at[number],
+            device_id=device,
+            device_id_type=MESH_IDS,
+        )
+        self.started.append((copy, when))
+        self.numbers[id(copy)] = number
+        return copy
+
+    def settle(self, chosen):
+        numbers = {id(copy) for copy in chosen}
+        for copy, when in self.started:
+            if id(copy) in numbers:
+                run_when(when, copy.wait_send)
+        self.started = [entry for entry in self.started if id(entry[0]) not in numbers]
+
+    def finish(self):
+        for copy, when in self.started:
+            run_when(when, copy.wait_send)
+
+
+class Place:
+    def __init__(self, nz):
+        self.nz = nz
+        self.c, self.z = lax.axis_index("ctx"), lax.axis_index("fsdp")
+        self.k, self.t = self.c % 2, self.c // 2
+        self.xn, self.yn, self.pn = flip(self.c, 2), flip(self.c, 4), flip(self.c, 1)
+        self.dn = flip(self.xn, 4)
+        self.tx, self.ty = flip(self.t, 1), flip(self.t, 2)
+        self.td = flip(self.tx, 2)
+        self.others = [(self.z + d) % nz for d in range(1, nz)]
+        self.plane = [self.xn, self.yn, self.dn, self.pn] + [
+            flip(peer, 1) for peer in (self.xn, self.yn, self.dn)
+        ]
+        self.above, self.below = jnp.minimum(self.z + 1, nz - 1), jnp.maximum(self.z - 1, 0)
+
+    def on_plane(self, c):
+        return (c, self.z)
+
+    def on_line(self, z):
+        return (self.c, z)
+
+    def greet(self):
+        barrier = pltpu.get_barrier_semaphore()
+        peers = [self.on_plane(peer) for peer in self.plane] + [self.on_line(z) for z in self.others]
+        for peer in peers:
+            pl.semaphore_signal(barrier, inc=1, device_id=peer, device_id_type=MESH_IDS)
+        pl.semaphore_wait(barrier, len(peers))
+
+
+class PlaneShare:
+    def __init__(self, copies, me, source, slot, rows):
+        self.copies, self.me, self.slot = copies, me, slot
+        self.top, self.bottom = pl.ds(0, rows // 2), pl.ds(rows // 2, rows // 2)
+        own = slot(me.k, me.t)
+        self.to_x = copies.make(source, own, me.on_plane(me.xn))
+        self.to_y = copies.make(source, own, me.on_plane(me.yn))
+        self.to_p = copies.make(source, own, me.on_plane(me.pn))
+        self.swaps = [self.to_p]
+        through_x, through_y = slot(me.k, me.tx).at[self.top], slot(me.k, me.ty).at[self.bottom]
+        self.hop_y = copies.make(through_x, through_x, me.on_plane(me.yn))
+        self.hop_x = copies.make(through_y, through_y, me.on_plane(me.xn))
+
+    def start(self):
+        self.to_x.start()
+        self.to_y.start()
+        self.to_p.start()
+
+    def swap(self, place):
+        copy = self.copies.make(place, place, self.me.on_plane(self.me.pn))
+        copy.start()
+        self.swaps.append(copy)
+
+    def on_x(self):
+        self.to_x.wait_recv()
+        self.hop_y.start()
+        self.swap(self.slot(self.me.k, self.me.tx))
+
+    def on_y(self):
+        self.to_y.wait_recv()
+        self.hop_x.start()
+        self.swap(self.slot(self.me.k, self.me.ty))
+
+    def on_diagonal(self):
+        diagonal = self.slot(self.me.k, self.me.td)
+        self.hop_y.wait_recv()
+        self.swap(diagonal.at[self.top])
+        self.hop_x.wait_recv()
+        self.swap(diagonal.at[self.bottom])
+
+    def finish(self):
+        for swap in self.swaps:
+            swap.wait_recv()
+
+
+class LineGather:
+    def __init__(self, copies, me, source, gathered):
+        self.copies, self.me, self.gathered = copies, me, gathered
+        rows = gathered.shape[1] // 2
+        self.mine = pl.ds(me.k * rows, rows)
+        self.moves, self.swaps = {}, []
+        for step in range(me.nz - 1):
+            for sign in (1, -1):
+                shard, target = me.z - sign * step, me.z + sign
+                ok = (shard >= 0) & (shard < me.nz) & (target >= 0) & (target < me.nz)
+                place = self.slot(shard)
+                copy = copies.make(
+                    source.at[self.mine] if step == 0 else place,
+                    place,
+                    me.on_line(jnp.clip(target, 0, me.nz - 1)),
+                    when=ok,
+                )
+                self.moves[step, sign] = (copy, ok)
+
+    def slot(self, shard):
+        return self.gathered.at[jnp.clip(shard, 0, self.me.nz - 1), self.mine]
+
+    def start(self):
+        for sign in (1, -1):
+            copy, ok = self.moves[0, sign]
+            run_when(ok, copy.start)
+
+    def advance(self, step):
+        me = self.me
+        for sign in (1, -1):
+            arrived = me.z - sign * (step + 1)
+            ok = (arrived >= 0) & (arrived < me.nz)
+            run_when(ok, self.moves[step, sign][0].wait_recv)
+            if step + 1 < me.nz - 1:
+                copy, following = self.moves[step + 1, sign]
+                run_when(following, copy.start)
+            place = self.slot(arrived)
+            swap = self.copies.make(place, place, me.on_plane(me.pn), when=ok)
+            run_when(ok, swap.start)
+            self.swaps.append((swap, ok))
+
+    def finish(self):
+        for swap, ok in self.swaps:
+            run_when(ok, swap.wait_recv)
+
+
+class LineSpread:
+    def __init__(self, copies, me, source, target):
+        self.me, self.source, self.target = me, source, target
+        rows = target.shape[0] // 2
+        mine = pl.ds(me.k * rows, rows)
+        here, up, down = me.z == me.t, me.z > me.t, me.z < me.t
+        self.here, self.up, self.down = here, up, down
+        not_last, not_first = me.z < me.nz - 1, me.z > 0
+        to_up, to_down = me.on_line(me.above), me.on_line(me.below)
+        place = target.at[mine]
+        self.first_up = copies.make(source.at[mine], place, to_up, when=here & not_last)
+        self.first_down = copies.make(source.at[mine], place, to_down, when=here & not_first)
+        self.next_up = copies.make(place, place, to_up, when=up & not_last, like=self.first_up)
+        self.next_down = copies.make(place, place, to_down, when=down & not_first, like=self.first_down)
+        self.not_last, self.not_first = not_last, not_first
+        self.swap = copies.make(place, place, me.on_plane(me.pn), when=up | down)
+
+    def start(self):
+        pl.when(self.here & self.not_last)(self.first_up.start)
+        pl.when(self.here & self.not_first)(self.first_down.start)
+
+        @pl.when(self.here)
+        def _():
+            self.target[...] = self.source[...]
+
+    def advance(self):
+        pl.when(self.up)(self.first_up.wait_recv)
+        pl.when(self.down)(self.first_down.wait_recv)
+        pl.when(self.up & self.not_last)(self.next_up.start)
+        pl.when(self.down & self.not_first)(self.next_down.start)
+        pl.when(self.up | self.down)(self.swap.start)
+
+    def finish(self):
+        pl.when(self.up | self.down)(self.swap.wait_recv)
+
+
+def add_narrow(target, index, incoming):
+    target[index] = narrow(wide(target[index]) + wide(incoming[index]))
+
+
+class LineReduce:
+    def __init__(self, copies, me, source, total, up, down):
+        self.me, self.source, self.total, self.up, self.down = me, source, total, up, down
+        half = total.shape[1]
+        self.mine, theirs = pl.ds(me.k * half, half), pl.ds((1 - me.k) * half, half)
+        self.exchange = copies.make(source.at[:, theirs], total, me.on_plane(me.pn))
+        self.sends = {}
+        for owner in range(me.nz):
+            self.sends[owner, 0] = copies.make(
+                total.at[owner], up.at[owner], me.on_line(me.above), when=me.z < owner
+            )
+            self.sends[owner, 1] = copies.make(
+                total.at[owner], down.at[owner], me.on_line(me.below), when=me.z > owner
+            )
+
+    def start(self):
+        self.exchange.start()
+
+    def pair(self):
+        self.exchange.wait_recv()
+        for owner in range(self.me.nz):
+            self.total[owner] = narrow(
+                wide(self.total[owner]) + wide(self.source[owner, self.mine])
+            )
+
+    def events(self, place):
+        nz, found = self.me.nz, []
+        for owner in range(place, nz):
+            if place > 0 or owner > place:
+                found.append((nz - 1 - owner + place, 0, owner))
+        for owner in range(place + 1):
+            if place < nz - 1 or owner < place:
+                found.append((owner + nz - 1 - place, 1, owner))
+        return sorted(found)
+
+    def step(self, place, way, owner):
+        incoming = (self.up, self.down)[way]
+        send = self.sends[owner, way]
+        if (way == 0 and place > 0) or (way == 1 and place < self.me.nz - 1):
+            send.wait_recv()
+            add_narrow(self.total, owner, incoming)
+        if owner != place:
+            send.start()
+
+
+def reduce_along(me, reductions, time):
+    for place in range(me.nz):
+        found = [event for event in reductions[0].events(place) if event[0] == time]
+        if not found:
+            continue
+
+        @pl.when(me.z == place)
+        def _():
+            for _, way, owner in found:
+                for reduction in reductions:
+                    reduction.step(place, way, owner)
+
+
+class LineCollect:
+    def __init__(self, copies, me, source, total, up, down):
+        self.me, self.source, self.total, self.up, self.down = me, source, total, up, down
+        half = total.shape[0]
+        self.mine, theirs = pl.ds(me.k * half, half), pl.ds((1 - me.k) * half, half)
+        self.exchange = copies.make(source.at[theirs], total, me.on_plane(me.pn))
+        self.to_up = copies.make(total, up, me.on_line(me.above), when=me.z < me.t)
+        self.to_down = copies.make(total, down, me.on_line(me.below), when=me.z > me.t)
+
+    def start(self):
+        self.exchange.start()
+
+    def pair(self):
+        self.exchange.wait_recv()
+        self.total[...] = narrow(wide(self.total[...]) + wide(self.source[self.mine]))
+
+    def take(self, incoming):
+        self.total[...] = narrow(wide(self.total[...]) + wide(incoming[...]))
+
+    def along(self, time):
+        me = self.me
+        for place in range(me.nz):
+
+            @pl.when((me.z == place) & (me.t >= place))
+            def _():
+                if place == time:
+                    if place > 0:
+                        self.to_up.wait_recv()
+                        self.take(self.up)
+                    pl.when(me.t > place)(self.to_up.start)
+
+            @pl.when((me.z == place) & (me.t <= place))
+            def _():
+                if me.nz - 1 - place == time:
+                    if place < me.nz - 1:
+                        self.to_down.wait_recv()
+                        self.take(self.down)
+                    pl.when(me.t < place)(self.to_down.start)
+
+
+class PlaneSpread:
+    def __init__(self, copies, me, source, target, rows):
+        self.me, self.source, self.target = me, source, target
+        top, bottom = pl.ds(0, rows // 2), pl.ds(rows // 2, rows // 2)
+        place = target.at[me.k]
+        self.here, self.from_x, self.from_y = me.t == me.z, me.tx == me.z, me.ty == me.z
+        self.from_d = me.td == me.z
+        self.to_x = copies.make(source, place, me.on_plane(me.xn), when=self.here)
+        self.to_y = copies.make(source, place, me.on_plane(me.yn), when=self.here)
+        self.to_p = copies.make(source, place, me.on_plane(me.pn), when=self.here)
+        self.hop_y = copies.make(place.at[top], place.at[top], me.on_plane(me.yn), when=self.from_x)
+        self.hop_x = copies.make(
+            place.at[bottom], place.at[bottom], me.on_plane(me.xn), when=self.from_y
+        )
+        away = self.from_x | self.from_y | self.from_d
+        self.away = away
+        self.swap = copies.make(place, place, me.on_plane(me.pn), when=away, like=self.to_p)
+
+    def start(self):
+        @pl.when(self.here)
+        def _():
+            self.to_x.start()
+            self.to_y.start()
+            self.to_p.start()
+            self.target[self.me.k] = self.source[...]
+
+    def advance(self):
+        @pl.when(self.from_x)
+        def _():
+            self.to_x.wait_recv()
+            self.hop_y.start()
+            self.swap.start()
+
+        @pl.when(self.from_y)
+        def _():
+            self.to_y.wait_recv()
+            self.hop_x.start()
+            self.swap.start()
+
+    def on_diagonal(self):
+        @pl.when(self.from_d)
+        def _():
+            self.hop_y.wait_recv()
+            self.hop_x.wait_recv()
+            self.swap.start()
+
+    def finish(self):
+        self.to_p.wait_recv()
+
+def norm_rows(values_in):
+    centre = jnp.mean(values_in, axis=-1, keepdims=True)
+    mean_removed = values_in - centre
+    inverse_deviation = lax.rsqrt(
+        jnp.mean(mean_removed * mean_removed, axis=-1, keepdims=True) + EPS
+    )
+    return mean_removed * inverse_deviation, inverse_deviation
+
+
+def head_rows(rows, head):
+    lanes = lax.broadcasted_iota(jnp.int32, rows.shape, 1)
+    inside = (lanes >= head * HD) & (lanes < (head + 1) * HD)
+    return jnp.where(inside, rows, jnp.zeros_like(rows))
+
+
+def rope_lanes(r, first, blocks, columns, back):
+    half_rot = ROT // 2
+    tables = [[], [], []]
+    row_cos, row_sin = r.rope_r[:, :128], r.rope_r[:, 128:]
+    lane = lax.broadcasted_iota(jnp.int32, row_cos.shape, 1) % HD
+    for block in range(blocks):
+        both = r.rope_b[pl.ds(first + block, 1), :]
+        block_cos, block_sin = both[:, :128], both[:, 128:]
+        cosine = block_cos * row_cos - block_sin * row_sin
+        sine = block_sin * row_cos + block_cos * row_sin
+        if back:
+            sine = -sine
+        tables[0].append(cosine)
+        tables[1].append(jnp.where(lane < half_rot, -sine, 0.0))
+        tables[2].append(jnp.where(lane >= half_rot, sine, 0.0))
+    stacked = [jnp.concatenate(table, axis=0) for table in tables]
+    return [jnp.concatenate([table] * (columns // 128), axis=1) for table in stacked]
+
+
+def turn(values, tables):
+    columns, half_rot = values.shape[1], ROT // 2
+    return (
+        values * tables[0]
+        + pltpu.roll(values, columns - half_rot, 1) * tables[1]
+        + pltpu.roll(values, half_rot, 1) * tables[2]
+    )
+
+
+def slice_weights(r, me):
+    part = r.wqs.shape[1] // 3
+    chips = r.wqkv.shape[1] // r.wqs.shape[1]
+    for chip in range(chips):
+
+        @pl.when(me.t == chip)
+        def _():
+            for source, target in ((r.wqkv, r.wqs), (r.wup, r.wus)):
+                for piece in range(target.shape[1] // part):
+                    first = (piece * chips + chip) * part
+                    target[:, piece * part : (piece + 1) * part] = source[:, first : first + part]
+
+
+def read_vectors(r, me):
+    nz, part = me.nz, r.vec.shape[1] // me.nz
+    shards = [wide(r.sm4[z]) for z in range(nz)]
+    for row in range(4):
+        for z in range(nz):
+            r.vec[row : row + 1, z * part : (z + 1) * part] = shards[z][
+                0:1, row * part : (row + 1) * part
+            ]
+    for z in range(nz):
+        r.vec[4:5, z * part : (z + 1) * part] = shards[z][1:2, :part] + shards[z][1:2, part : 2 * part]
+    chips = nz
+    for chip in range(chips):
+
+        @pl.when(me.t == chip)
+        def _():
+            for piece in range(3):
+                number = piece * chips + chip
+                first = number % 3 * part
+                r.vec[5:6, piece * part : (piece + 1) * part] = shards[number // 3][
+                    2:3, first : first + part
+                ]
+            for z in range(nz):
+                r.vec[6:7, z * part : (z + 1) * part] = shards[z][3:4, chip * part : (chip + 1) * part]
+
+
+def sorted_rows(r, source, block, blocks):
+    pieces = []
+    for number in range(blocks):
+        pieces.append(source[r.idx[block + number]])
+    return jnp.concatenate(pieces, axis=0)
+
+
+def put_blocks(target, tile, values):
+    blocks = values.shape[0] // BLK
+    target[pl.ds(tile * blocks, blocks)] = values.reshape(blocks, BLK, values.shape[1])
+
+
+def project(r, tile):
+    part = r.q.shape[1]
+    blocks = QTILE // BLK
+    standardized, _ = norm_rows(wide(sorted_rows(r, r.hall, tile * blocks, blocks)))
+    normed = narrow(standardized * r.vec[0:1, :] + r.vec[1:2, :])
+    weight = r.wq4[...].reshape(-1, 3 * part)
+    projected = mm(normed, weight) + r.vec[5:6, : 3 * part]
+    turned = turn(
+        projected[:, : 2 * part], rope_lanes(r, tile * blocks, blocks, 2 * part, False)
+    )
+    place = pl.ds(pl.multiple_of(tile * QTILE, QTILE), QTILE)
+    r.q[place, :] = narrow(wide(narrow(turned[:, :part])) * HD**-0.5)
+    keys, values = turned[:, part:], projected[:, 2 * part :]
+    r.k[place, :] = narrow(keys)
+    r.v[place, :] = narrow(values)
+    r.kt[:, place] = narrow(keys.T)
+    r.vt[:, place] = narrow(values.T)
+
+
+def tile_start(r, me, tile):
+    quarter = r.k.shape[0] // 4
+    low = tile < quarter // QTILE
+    inside = tile * QTILE - jnp.where(low, 0, quarter)
+    return jnp.where(low, quarter * me.k, 3 * quarter - quarter * me.k) + inside
+
+
+def attend(r, me, tile):
+    part = r.k.shape[1]
+    heads = part // HD
+    start = tile_start(r, me, tile)
+    rows = slice(tile * QTILE, (tile + 1) * QTILE)
+    query = r.q[pl.ds(pl.multiple_of(start, QTILE), QTILE), :]
+    per_head = [head_rows(query, head) for head in range(heads)]
+
+    def visit(number, state, masked):
+        place = pl.ds(pl.multiple_of(number * QTILE, QTILE), QTILE)
+        keys = r.k[place, :]
+        result = []
+        for head in range(heads):
+            top, total, acc = state[head]
+            logits = mm(keys, per_head[head], NT)
+            if masked:
+                key_row = lax.broadcasted_iota(jnp.int32, logits.shape, 0)
+                query_row = lax.broadcasted_iota(jnp.int32, logits.shape, 1)
+                logits = jnp.where(key_row <= query_row, logits, NEG)
+            new_top = jnp.maximum(top, jnp.max(logits, axis=0, keepdims=True))
+            fade = jnp.exp(top - new_top)
+            probs = jnp.exp(logits - new_top)
+            total = total * fade + jnp.sum(probs, axis=0, keepdims=True)
+            values = r.vt[head * HD : (head + 1) * HD, place]
+            acc = acc * fade + mm(values, narrow(probs))
+            result.append((new_top, total, acc))
+        return tuple(result)
+
+    state = tuple(
+        (
+            jnp.full((1, QTILE), NEG, jnp.float32),
+            jnp.zeros((1, QTILE), jnp.float32),
+            jnp.zeros((HD, QTILE), jnp.float32),
+        )
+        for _ in range(heads)
+    )
+    last = start // QTILE
+    state = lax.fori_loop(0, last, lambda n, s: visit(n, s, False), state)
+    state = visit(last, state, True)
+    merged = jnp.concatenate([acc / total for _, total, acc in state], axis=0)
+    r.att[rows, :] = narrow(merged.T)
+    for head in range(heads):
+        r.lse[head : head + 1, rows] = state[head][0] + jnp.log(state[head][1])
+
+
+def feed_forward(r, me, tile):
+    place = pl.ds(pl.multiple_of(tile * QTILE, QTILE), QTILE)
+    blocks = QTILE // BLK
+    block = tile_start(r, me, tile) // BLK
+    width = r.hall.shape[2]
+    standardized, _ = norm_rows(wide(sorted_rows(r, r.hall, block, blocks)))
+    cotan = sorted_rows(r, r.gall, block, blocks)
+    gain2 = r.vec[2:3, :]
+    normed = narrow(standardized * gain2 + r.vec[3:4, :])
+    up_weight = r.wu4[...].reshape(width, -1)
+    down_weight = r.wd4[...].reshape(-1, width)
+    up = mm(normed, up_weight) + r.vec[6:7, :]
+    below = 0.5 * (1.0 + lax.erf(up * SQRT_HALF))
+    act = narrow(up * below)
+    slope = below + up * jnp.exp(-0.5 * up * up) * INV_ROOT_TWO_PI
+    d_up = mm(cotan, down_weight, NT) * slope
+    d_up16 = narrow(d_up)
+    attended = r.att[place, :]
+    put_blocks(r.outb, tile, narrow(mm(act, down_weight) + mm(attended, r.wo1[...])))
+    d_normed = mm(d_up16, up_weight, NT)
+    r.sums[2:3, :] += jnp.sum(d_normed * standardized, axis=0, keepdims=True)
+    r.sums[3:4, :] += jnp.sum(d_normed, axis=0, keepdims=True)
+    r.sums[6:7, :] += jnp.sum(d_up, axis=0, keepdims=True)
+    r.e2[place, :] = d_normed * gain2
+    r.n[place, :] = normed
+    r.gl[place, :] = cotan
+    r.act[place, :] = act
+    r.du[place, :] = d_up16
+    d_att = narrow(mm(cotan, r.wo1[...], NT))
+    r.datt[place, :] = d_att
+    product = wide(d_att) * wide(attended)
+    shape = (8, product.shape[1])
+    picked = lax.broadcasted_iota(jnp.int32, shape, 1) // HD == lax.broadcasted_iota(
+        jnp.int32, shape, 0
+    )
+    r.delta[:, place] = lax.dot_general(
+        picked.astype(jnp.float32),
+        product,
+        NT,
+        precision=lax.Precision.HIGHEST,
+        preferred_element_type=jnp.float32,
+    )
+
+
+def weight_grad(target, left, right):
+    rows, columns = left.shape[1], right.shape[1]
+    shard = target.shape[1]
+    values = right[...]
+    for first in range(0, rows, QTILE):
+        result = narrow(mm(left[:, first : first + QTILE], values, TN))
+        at = first
+        while at < first + QTILE:
+            owner, inside = at // shard, at % shard
+            until = min((owner + 1) * shard, first + QTILE)
+            target[owner, inside : inside + until - at, :] = result[at - first : until - first, :]
+            at = until
+
+
+def attend_grad(r, me, tile):
+    part = r.k.shape[1]
+    heads = part // HD
+    kstep = 2 * QTILE
+    start = tile_start(r, me, tile)
+    rows = slice(tile * QTILE, (tile + 1) * QTILE)
+    query = r.q[pl.ds(pl.multiple_of(start, QTILE), QTILE), :]
+    d_out = r.datt[rows, :]
+    queries = jnp.concatenate([head_rows(query, head) for head in range(heads)], axis=0)
+    d_outs = jnp.concatenate([head_rows(d_out, head) for head in range(heads)], axis=0)
+
+    def visit(number, state, masked):
+        place = pl.ds(pl.multiple_of(number * kstep, kstep), kstep)
+        keys, values = r.k[place, :], r.v[place, :]
+        probs_all, d_logits_all, result = [], [], []
+        for head in range(heads):
+            own = slice(head * QTILE, (head + 1) * QTILE)
+            logits = mm(keys, queries[own], NT)
+            probs = jnp.exp(logits - r.lse[head : head + 1, rows])
+            if masked:
+                key_row = number * kstep + lax.broadcasted_iota(jnp.int32, logits.shape, 0)
+                query_row = start + lax.broadcasted_iota(jnp.int32, logits.shape, 1)
+                probs = jnp.where(key_row <= query_row, probs, 0.0)
+            d_probs = mm(values, d_outs[own], NT)
+            d_logits = narrow(probs * (d_probs - r.delta[head : head + 1, rows]))
+            probs_all.append(narrow(probs))
+            d_logits_all.append(d_logits)
+            result.append(state[head] + mm(r.kt[head * HD : (head + 1) * HD, place], d_logits))
+        r.dv[place, :] += mm(jnp.concatenate(probs_all, axis=1), d_outs)
+        r.dk[place, :] += mm(jnp.concatenate(d_logits_all, axis=1), queries)
+        return tuple(result)
+
+    state = tuple(jnp.zeros((HD, QTILE), jnp.float32) for _ in range(heads))
+    last = start // kstep
+    state = lax.fori_loop(0, last, lambda n, s: visit(n, s, False), state)
+    state = visit(last, state, True)
+    r.dqt[:, rows] = jnp.concatenate(state, axis=0)
+
+
+def qkv_grad(r, me, tile):
+    place = pl.ds(pl.multiple_of(tile * QTILE, QTILE), QTILE)
+    part = r.k.shape[1]
+    blocks = QTILE // BLK
+    start = tile_start(r, me, tile)
+    block = start // BLK
+    held = pl.ds(pl.multiple_of(start, QTILE), QTILE)
+    standardized, _ = norm_rows(wide(sorted_rows(r, r.hall, block, blocks)))
+    gain1 = r.vec[0:1, :]
+    r.n[place, :] = narrow(standardized * gain1 + r.vec[1:2, :])
+    d_query = r.dqt[:, place].T * HD**-0.5
+    d_key = r.dk[held, :] + wide(r.kvin[place, :part])
+    d_value = r.dv[held, :] + wide(r.kvin[place, part:])
+    turned = turn(
+        jnp.concatenate([d_query, d_key], axis=1), rope_lanes(r, block, blocks, 2 * part, True)
+    )
+    d_qkv = jnp.concatenate([turned, d_value], axis=1)
+    d_qkv16 = narrow(d_qkv)
+    r.du[place, : 3 * part] = d_qkv16
+    r.sums[5:6, : 3 * part] += jnp.sum(d_qkv, axis=0, keepdims=True)
+    weight = r.wq4[...].reshape(-1, 3 * part)
+    d_normed = mm(d_qkv16, weight, NT)
+    r.sums[0:1, :] += jnp.sum(d_normed * standardized, axis=0, keepdims=True)
+    r.sums[1:2, :] += jnp.sum(d_normed, axis=0, keepdims=True)
+    put_blocks(r.outb, tile, narrow(d_normed * gain1 + r.e2[place, :]))
+
+
+def flat_rows(values):
+    return values.reshape(-1, values.shape[-1])
+
+
+class Scatter:
+    def __init__(self, copies, me, r, source, sent, got, landed):
+        self.me, self.r, self.source, self.sent, self.got, self.landed = me, r, source, sent, got, landed
+        self.chips, self.sides = landed.shape[0], landed.shape[1]
+        self.first = r.k.shape[0] // BLK
+        self.exchanges = [
+            copies.make(self.piece(sent, chip), self.piece(got, chip), me.on_plane(me.pn))
+            for chip in range(self.chips)
+        ]
+        self.moves = [
+            copies.make(self.piece(got, chip), landed.at[me.t], me.on_plane(peer))
+            for chip, peer in ((me.tx, me.xn), (me.ty, me.yn), (me.td, me.dn))
+        ]
+
+    def piece(self, array, chip):
+        return array.at[pl.ds(chip * self.sides, self.sides)]
+
+    def block(self, number):
+        return self.source[self.r.idx[self.first + number]]
+
+    def start(self):
+        count = self.chips * self.sides
+        for number in range(count):
+            self.sent[number] = self.block(count + number)
+        for exchange in self.exchanges:
+            exchange.start()
+
+    def spread(self):
+        count = self.chips * self.sides
+        for exchange in self.exchanges:
+            exchange.wait_recv()
+        for number in range(count):
+            flag = self.r.idx[self.first + 2 * count + number // self.sides]
+            own, other = wide(self.block(number)), wide(self.got[number])
+            here = jnp.full(own.shape, flag, jnp.int32) > 0
+            self.got[number] = narrow(jnp.where(here, own, other))
+        for move in self.moves:
+            move.start()
+
+    def total(self):
+        for move in self.moves:
+            move.wait_recv()
+        me = self.me
+        result = wide(self.got[pl.ds(me.t * self.sides, self.sides)])
+        for chip in (me.tx, me.ty, me.td):
+            result = result + wide(self.landed[chip])
+        return flat_rows(result)
+
+
+def layer_kernel(nz, names, *refs):
+    r = types.SimpleNamespace(**dict(zip(names, refs)))
+    me = Place(nz)
+    copies = Copies(r.send_sems, r.recv_sems)
+    sides = r.h.shape[0]
+    shard = r.wqs.shape[0]
+    tiles = r.att.shape[0] // QTILE
+
+    slice_weights(r, me)
+    me.greet()
+
+    def row_slot(array):
+        return lambda core, chip: array.at[pl.ds((2 * chip + core) * sides, sides)]
+
+    own_rows = pl.ds(me.c * sides, sides)
+    h_share = PlaneShare(copies, me, r.h, row_slot(r.hall), sides)
+    g_share = PlaneShare(copies, me, r.g, row_slot(r.gall), sides)
+    wq = LineGather(copies, me, r.wqs, r.wq4)
+    wu = LineGather(copies, me, r.wus, r.wu4)
+    wd = LineGather(copies, me, r.wdown.at[pl.ds(me.t * shard, shard)], r.wd4)
+    wo = LineSpread(copies, me, r.wout, r.wo1)
+    small = [copies.make(r.sm, r.sm4.at[me.z], me.on_line(other)) for other in me.others]
+
+    h_share.start()
+    wq.start()
+    for copy in small:
+        copy.start()
+    wu.start()
+    r.hall[own_rows] = r.h[...]
+    r.gall[own_rows] = r.g[...]
+    r.wq4[me.z] = r.wqs[...]
+    r.wu4[me.z] = r.wus[...]
+    own_down = pltpu.make_async_copy(
+        r.wdown.at[pl.ds(me.t * shard, shard)], r.wd4.at[me.z], r.local_sem
+    )
+    own_down.start()
+    r.sm4[me.z] = r.sm[...]
+    r.sums[...] = jnp.zeros_like(r.sums)
+    r.vout[...] = jnp.zeros_like(r.vout)
+    r.dk[...] = jnp.zeros_like(r.dk)
+    r.dv[...] = jnp.zeros_like(r.dv)
+    wq.advance(0)
+    h_share.on_x()
+    h_share.on_y()
+    g_share.start()
+    wq.advance(1)
+    wd.start()
+    wo.start()
+    wq.advance(2)
+    for copy in small:
+        copy.wait_recv()
+    read_vectors(r, me)
+    wu.advance(0)
+    h_share.on_diagonal()
+    wq.finish()
+    h_share.finish()
+
+    @pl.loop(0, r.k.shape[0] // QTILE)
+    def _(tile):
+        project(r, tile)
+
+    wd.advance(0)
+    g_share.on_x()
+    g_share.on_y()
+    attend(r, me, 0)
+    wu.advance(1)
+    wd.advance(1)
+    attend(r, me, 1)
+    wo.advance()
+    wu.advance(2)
+    attend(r, me, 2)
+    g_share.on_diagonal()
+    wd.advance(2)
+    for tile in range(3, tiles):
+        attend(r, me, tile)
+    own_down.wait()
+    wu.finish()
+    wd.finish()
+    wo.finish()
+    g_share.finish()
+    copies.settle([g_share.hop_x, g_share.hop_y, *g_share.swaps[1:]])
+
+    @pl.loop(0, tiles)
+    def _(tile):
+        feed_forward(r, me, tile)
+
+    out_scatter = Scatter(copies, me, r, r.outb, r.osent, r.ogot, r.oland)
+    out_scatter.start()
+    up_reduce = LineReduce(copies, me, r.gu, r.tu, r.uu, r.du_in)
+    down_reduce = LineReduce(copies, me, r.gd, r.td, r.ud, r.dd_in)
+    out_reduce = LineCollect(copies, me, r.go, r.to, r.uo, r.do_in)
+    weight_grad(r.gd, r.act, r.gl)
+    down_reduce.start()
+    weight_grad(r.gu, r.n, r.du)
+    up_reduce.start()
+    r.go[...] = narrow(mm(r.att[...], r.gl[...], TN))
+    out_reduce.start()
+    out_scatter.spread()
+    down_reduce.pair()
+    up_reduce.pair()
+    out_reduce.pair()
+    early = [down_reduce, up_reduce]
+    reduce_along(me, early, 0)
+    out_reduce.along(0)
+    attend_grad(r, me, 0)
+    reduce_along(me, early, 1)
+    out_reduce.along(1)
+    attend_grad(r, me, 1)
+    reduce_along(me, early, 2)
+    out_reduce.along(2)
+    attend_grad(r, me, 2)
+    reduce_along(me, early, 3)
+    out_reduce.along(3)
+    half = shard // 2
+    d_share = PlaneShare(copies, me, r.td.at[me.z], lambda core, chip: r.fd.at[core, chip], half)
+    u_share = PlaneShare(copies, me, r.tu.at[me.z], lambda core, chip: r.fu.at[core, chip], half)
+    o_spread = PlaneSpread(copies, me, r.to, r.fo, half)
+    d_share.start()
+    u_share.start()
+    o_spread.start()
+    r.fd[me.k, me.t] = r.td[me.z]
+    r.fu[me.k, me.t] = r.tu[me.z]
+    for tile in range(3, tiles):
+        attend_grad(r, me, tile)
+
+    part = r.k.shape[1]
+    quarter = r.k.shape[0] // 4
+    kv_moves = []
+    for number in range(2):
+        first = quarter * (1 - me.k) if number == 0 else 3 * quarter - quarter * (1 - me.k)
+        theirs = pl.ds(pl.multiple_of(first, quarter), quarter)
+        rows = slice(number * quarter, (number + 1) * quarter)
+        r.act[rows, :part] = narrow(r.dk[theirs, :])
+        r.act[rows, part : 2 * part] = narrow(r.dv[theirs, :])
+        copy = copies.make(r.act.at[rows, : 2 * part], r.kvin.at[rows], me.on_plane(me.pn))
+        copy.start()
+        kv_moves.append(copy)
+    d_share.on_x()
+    d_share.on_y()
+    u_share.on_x()
+    u_share.on_y()
+    o_spread.advance()
+    for copy in kv_moves:
+        copy.wait_recv()
+
+    @pl.loop(0, tiles)
+    def _(tile):
+        qkv_grad(r, me, tile)
+
+    e_scatter = Scatter(
+        copies, me, r, r.outb, r.gall.at[: r.outb.shape[0]], r.gall.at[r.outb.shape[0] :], r.eland
+    )
+    e_scatter.start()
+    weight_grad(r.gq, r.n, r.du.at[:, : 3 * part])
+    qkv_reduce = LineReduce(copies, me, r.gq, r.tq, r.uq, r.dq_in)
+    qkv_reduce.start()
+    e_scatter.spread()
+    qkv_reduce.pair()
+    reduce_along(me, [qkv_reduce], 0)
+
+    vec_part = r.vec.shape[1] // nz
+    r.sums[4:5, :] = jnp.sum(wide(flat_rows(r.g[...])), axis=0, keepdims=True)
+    for z in range(nz):
+        span = slice(z * vec_part, (z + 1) * vec_part)
+        for row in range(4):
+            r.vout[z, 0:1, row * vec_part : (row + 1) * vec_part] = r.sums[row : row + 1, span]
+        r.vout[z, 1:2, :vec_part] = r.sums[4:5, span]
+    for chip in range(nz):
+
+        @pl.when(me.t == chip)
+        def _():
+            for piece in range(3):
+                number = piece * nz + chip
+                first = number % 3 * vec_part
+                r.vout[number // 3, 2:3, first : first + vec_part] = r.sums[
+                    5:6, piece * vec_part : (piece + 1) * vec_part
+                ]
+            for z in range(nz):
+                r.vout[z, 3:4, chip * vec_part : (chip + 1) * vec_part] = r.sums[
+                    6:7, z * vec_part : (z + 1) * vec_part
+                ]
+
+    vec_line = [
+        copies.make(r.vout.at[other], r.vline.at[me.z], me.on_line(other)) for other in me.others
+    ]
+    for copy in vec_line:
+        copy.start()
+    d_share.on_diagonal()
+    u_share.on_diagonal()
+    o_spread.on_diagonal()
+    reduce_along(me, [qkv_reduce], 1)
+    for copy in vec_line:
+        copy.wait_recv()
+    vector = r.vout[me.z]
+    for other in me.others:
+        vector = vector + r.vline[other]
+    r.vsend[...] = vector
+    reduce_along(me, [qkv_reduce], 2)
+    vec_plane = [copies.make(r.vsend, r.vplane.at[me.c], me.on_plane(peer)) for peer in me.plane]
+    for copy in vec_plane:
+        copy.start()
+    reduce_along(me, [qkv_reduce], 3)
+    q_share = PlaneShare(copies, me, r.tq.at[me.z], lambda core, chip: r.fq.at[core, chip], half)
+    q_share.start()
+    r.fq[me.k, me.t] = r.tq[me.z]
+
+    residual = wide(flat_rows(r.h[...]))
+    own_standardized, own_deviation = norm_rows(residual)
+    r.hidden_out[...] = narrow(residual + r.vec[4:5, :] + out_scatter.total())
+    q_share.on_x()
+    q_share.on_y()
+    e_total = e_scatter.total()
+    r.hidden_grad[...] = wide(flat_rows(r.g[...])) + own_deviation * (
+        e_total
+        - jnp.mean(e_total, axis=-1, keepdims=True)
+        - own_standardized * jnp.mean(e_total * own_standardized, axis=-1, keepdims=True)
+    )
+    for copy in vec_plane:
+        copy.wait_recv()
+    vector = r.vsend[...]
+    for peer in me.plane:
+        vector = vector + r.vplane[peer]
+    r.vsum[...] = vector
+    q_share.on_diagonal()
+    d_share.finish()
+    u_share.finish()
+    o_spread.finish()
+    q_share.finish()
+    copies.finish()
+
+
+def assemble_kernel(fq_ref, fu_ref, fd_ref, fo_ref, gq_ref, gu_ref, gd_ref, go_ref):
+    cores, chips, half, _ = fq_ref.shape
+    part = fq_ref.shape[3] // 3
+    for core in range(cores):
+        rows = slice(core * half, (core + 1) * half)
+        go_ref[rows, :] = wide(fo_ref[core])
+        for chip in range(chips):
+            for source, target in ((fq_ref, gq_ref), (fu_ref, gu_ref)):
+                for piece in range(source.shape[3] // part):
+                    first = (piece * chips + chip) * part
+                    target[rows, first : first + part] = wide(
+                        source[core, chip, :, piece * part : (piece + 1) * part]
+                    )
+            first = chip * cores * half + core * half
+            gd_ref[first : first + half, :] = wide(fd_ref[core, chip])
+
+
+def rotary_parts(block_count):
+    half_rot = ROT // 2
+    lane = np.arange(128) % HD
+    rate = np.where(lane < ROT, 10000.0 ** (-2.0 * (lane % half_rot) / ROT), 0.0)
+
+    def table(places):
+        angle = places[:, None].astype(np.float64) * rate[None, :]
+        return np.concatenate([np.cos(angle), np.sin(angle)], axis=1).astype(np.float32)
+
+    return table(np.arange(BLK)), table(np.arange(block_count) * BLK)
+
+
+def block_table(block_order, chips, core):
+    count = block_order.shape[0]
+    quarter = count // 4
+    places = jnp.arange(count, dtype=jnp.int32)
+    gathered = jnp.sum(
+        jnp.where(block_order[:, None] == places[None, :], places[:, None], 0), axis=0
+    )
+    pairs = block_order.reshape(chips, 2, count // (2 * chips))
+    local = jnp.where(
+        (pairs >= quarter * core) & (pairs < quarter * (core + 1)),
+        pairs - quarter * core,
+        jnp.clip(pairs - (3 * quarter - quarter * core) + quarter, 0, 2 * quarter - 1),
+    )
+    outer = (pairs[:, :, 0] < quarter) | (pairs[:, :, 0] >= 3 * quarter)
+    here = outer == (core == 0)
+    mine = jnp.where(core == 0, local[:, 0], local[:, 1])
+    theirs = jnp.where(core == 0, local[:, 1], local[:, 0])
+    flags = jnp.where(core == 0, here[:, 0], here[:, 1])
+    return jnp.concatenate(
+        [gathered, mine.reshape(-1), theirs.reshape(-1), flags.astype(jnp.int32)]
+    ).astype(jnp.int32)
+
+
+VMEM_SPEC = pl.BlockSpec(memory_space=pltpu.VMEM)
+SPECS = {
+    "idx": pl.BlockSpec(memory_space=pltpu.SMEM),
+    "wdown": pl.BlockSpec(memory_space=pl.ANY),
+}
+VMEM_LIMIT = 63 * 1024 * 1024
+
+
+def sliced_layer(
+    nz,
+    hidden_in,
+    norm1_gain,
+    attention_norm_bias,
+    qkv_weight,
+    qkv_bias,
+    out_weight,
+    out_bias,
+    norm2_gain,
+    feedforward_norm_bias,
+    up_weight,
+    up_bias,
+    down_weight,
+    down_bias,
+    cotangent,
+    block_order,
+):
+    f32, b16 = jnp.float32, jnp.bfloat16
+    h, g = hidden_in[0], cotangent[0]
+    local_rows, width = h.shape
+    chips = lax.axis_size("ctx") // 2
+    core = lax.axis_index("ctx") % 2
+    shard = qkv_weight.shape[0]
+    half = shard // 2
+    part = width // chips
+    hidden = up_weight.shape[1] // chips
+    rows = chips * local_rows
+    everyone = 2 * rows
+    sides = local_rows // BLK
+
+    idx = block_table(block_order, chips, core)
+    first = jnp.concatenate([norm1_gain, attention_norm_bias, norm2_gain, feedforward_norm_bias])
+    second = jnp.concatenate([out_bias, down_bias])
+    lines = [
+        jnp.pad(line, (0, width - line.shape[0])) for line in (first, second, qkv_bias, up_bias)
+    ]
+    sm = jnp.pad(jnp.stack(lines), ((0, 12), (0, 0)))
+    rope_r, rope_b = rotary_parts(everyone // BLK)
+
+    inputs = {
+        "idx": idx,
+        "h": h.reshape(sides, BLK, width),
+        "g": g.reshape(sides, BLK, width),
+        "wqkv": qkv_weight,
+        "wup": up_weight,
+        "wdown": down_weight,
+        "wout": out_weight,
+        "sm": sm,
+        "rope_r": jnp.asarray(rope_r),
+        "rope_b": jnp.asarray(rope_b),
+    }
+    outputs = {
+        "hidden_out": ((local_rows, width), b16),
+        "hidden_grad": ((local_rows, width), f32),
+        "fq": ((2, chips, half, 3 * part), b16),
+        "fu": ((2, chips, half, hidden), b16),
+        "fd": ((2, chips, half, width), b16),
+        "fo": ((2, half, width), b16),
+        "vsum": ((8, width), f32),
+    }
+    scratch = {
+        "hall": ((everyone // BLK, BLK, width), b16),
+        "gall": ((everyone // BLK, BLK, width), b16),
+        "wqs": ((shard, 3 * part), b16),
+        "wus": ((shard, hidden), b16),
+        "wq4": ((nz, shard, 3 * part), b16),
+        "wu4": ((nz, shard, hidden), b16),
+        "wd4": ((nz, shard, width), b16),
+        "wo1": ((part, width), b16),
+        "sm4": ((nz, 16, width), b16),
+        "vec": ((8, width), f32),
+        "sums": ((8, width), f32),
+        "q": ((everyone, part), b16),
+        "k": ((everyone, part), b16),
+        "v": ((everyone, part), b16),
+        "kt": ((part, everyone), b16),
+        "vt": ((part, everyone), b16),
+        "att": ((rows, part), b16),
+        "lse": ((8, rows), f32),
+        "delta": ((8, rows), f32),
+        "datt": ((rows, part), b16),
+        "act": ((rows, hidden), b16),
+        "du": ((rows, hidden), b16),
+        "n": ((rows, width), b16),
+        "gl": ((rows, width), b16),
+        "outb": ((rows // BLK, BLK, width), b16),
+        "e2": ((rows, width), f32),
+        "dk": ((everyone, part), f32),
+        "dv": ((everyone, part), f32),
+        "dqt": ((part, rows), f32),
+        "kvin": ((rows, 2 * part), b16),
+        "osent": ((rows // BLK, BLK, width), b16),
+        "ogot": ((rows // BLK, BLK, width), b16),
+        "oland": ((chips, sides, BLK, width), b16),
+        "eland": ((chips, sides, BLK, width), b16),
+        "gq": ((nz, shard, 3 * part), b16),
+        "gu": ((nz, shard, hidden), b16),
+        "gd": ((nz, shard, width), b16),
+        "go": ((part, width), b16),
+        "tq": ((nz, half, 3 * part), b16),
+        "uq": ((nz, half, 3 * part), b16),
+        "dq_in": ((nz, half, 3 * part), b16),
+        "tu": ((nz, half, hidden), b16),
+        "uu": ((nz, half, hidden), b16),
+        "du_in": ((nz, half, hidden), b16),
+        "td": ((nz, half, width), b16),
+        "ud": ((nz, half, width), b16),
+        "dd_in": ((nz, half, width), b16),
+        "to": ((half, width), b16),
+        "uo": ((half, width), b16),
+        "do_in": ((half, width), b16),
+        "vout": ((nz, 8, width), f32),
+        "vline": ((nz, 8, width), f32),
+        "vsend": ((8, width), f32),
+        "vplane": ((2 * chips, 8, width), f32),
+    }
+    names = [*inputs, *outputs, *scratch, "send_sems", "recv_sems", "local_sem"]
+    results = pl.pallas_call(
+        functools.partial(layer_kernel, nz, names),
+        out_shape=tuple(jax.ShapeDtypeStruct(*leaf) for leaf in outputs.values()),
+        in_specs=[SPECS.get(name, VMEM_SPEC) for name in inputs],
+        out_specs=(VMEM_SPEC,) * len(outputs),
+        scratch_shapes=[pltpu.VMEM(*leaf) for leaf in scratch.values()]
+        + [pltpu.SemaphoreType.DMA((SEMAPHORES,))] * 2
+        + [pltpu.SemaphoreType.DMA],
+        compiler_params=pltpu.CompilerParams(
+            collective_id=0, has_side_effects=True, vmem_limit_bytes=VMEM_LIMIT
+        ),
+        name="layer",
+    )(*inputs.values())
+    hidden_out, hidden_grad, fq, fu, fd, fo, vsum = results
+
+    grad_qkv, grad_up, grad_down, grad_out = pl.pallas_call(
+        assemble_kernel,
+        out_shape=tuple(
+            jax.ShapeDtypeStruct(weight.shape, f32)
+            for weight in (qkv_weight, up_weight, down_weight, out_weight)
+        ),
+        in_specs=[VMEM_SPEC] * 4,
+        out_specs=(VMEM_SPEC,) * 4,
+        compiler_params=pltpu.CompilerParams(vmem_limit_bytes=56 * 1024 * 1024),
+        name="assemble",
+    )(fq, fu, fd, fo)
+
+    norms = vsum[0].reshape(nz, shard)
+    bias = vsum[1, :shard]
+    return (
+        hidden_out[None],
+        hidden_grad[None],
+        norms[0],
+        norms[1],
+        grad_qkv,
+        vsum[2, : qkv_bias.shape[0]],
+        grad_out,
+        bias,
+        norms[2],
+        norms[3],
+        grad_up,
+        vsum[3, : up_bias.shape[0]],
+        grad_down,
+        bias,
+    )
+
+
+def sliced_fits(mesh):
+    return mesh.shape["ctx"] == 8 and mesh.shape["fsdp"] == 4
+
+
 def solution(mesh):
     in_specs = (
         P("fsdp", "ctx", None),
@@ -455,4 +1634,7 @@
         P("fsdp", None),
         P("fsdp"),
     )
+    local = whole_parameter_layer
+    if sliced_fits(mesh):
+        local = functools.partial(sliced_layer, mesh.shape["fsdp"])
     return jax.shard_map(local, mesh=mesh, in_specs=in_specs, out_specs=out_specs, check_vma=False)

time: 1130 us -> 166 us (0.15)
  waiting for transfers between devices: 814 us -> 0 us
  Pallas kernels: 0 us -> 152 us
  matrix products: 142 us -> 0 us
  blocking collectives: 71.7 us -> 0 us
  local copies, waits for them, and re-layouts: 37.9 us -> 8.62 us
  other arithmetic: 25.6 us -> 3.87 us
  between operations: 17.8 us -> 0.7 us
  loops' own time: 16.6 us -> 0 us
    reduce_scatter x6 -> x0, waiting for transfers between devices: 605 us -> none  [the longest x1 165 us: local(): lax.psum_scatter(terms[10], 'fsdp', scatter_dimension=0, tiled=True)]
    pallas_call x0 -> x2, Pallas kernels: none -> 152 us  [the longest x1 147 us: sliced_layer(): pl.pallas_call(functools.partial(layer_kernel, nz, names), out_shape=tupl...]
    all_gather x6 -> x0, waiting for transfers between devices: 145 us -> none  [the longest x1 44.2 us: local(): lax.all_gather(qkv_weight, 'fsdp', axis=0, tiled=True)]
    dot_general x40 -> x0, matrix products: 142 us -> none  [the longest x8 18 us: masked_logits(): jnp.einsum('qhd,khd->hqk', query_block, key_block, preferred_element_type...]
    psum x1 -> x0, waiting for transfers between devices: 60.8 us -> none  [local(): lax.psum((shares[0], shares[1], shares[2], shares[3], shares[4], shares[5...]
    unnamed x2 -> x0, blocking collectives: 34.4 us -> none
    psum x1 -> x0, blocking collectives: 23.7 us -> none  [local(): lax.psum((shares[0], shares[1], shares[2], shares[3], shares[4], shares[5...]
    unnamed x94 -> x9, local copies, waits for them, and re-layouts: 19.1 us -> 2.2 us
  transfers between devices with their start and end apart: 13 -> 0, of which waited for: 12 -> 0; matrix products, arithmetic and copies ran while one was open for 17% -> 0% of each run, Pallas kernels for 0% -> 0%
where the time goes in v2:
time: 166 us
  Pallas kernels  152 us (92%)
  local copies, waits for them, and re-layouts  8.62 us (5%)
  other arithmetic  3.87 us (2%)
    pallas_call x1, Pallas kernels, sliced_layer(): pl.pallas_call(functools.partial(layer_kernel, nz, names), out_shape=tupl...  147 us
    pallas_call x1, Pallas kernels, sliced_layer(): pl.pallas_call(assemble_kernel, out_shape=tuple((jax.ShapeDtypeStruct(wei...  5.45 us

profile of v2, /device:TPU:1, one launch (start us, length us, event | category | flops | bytes accessed | tf_op | source)
XLA Modules:
  0.0 165.6 jit_solution(10916044817032884611)
XLA Ops:
  0.7 0.7 select_reduce_fusion
  1.4 0.8 pad_maximum_fusion
  2.2 0.7 pad.13
  2.9 0.7 fusion.11
  3.6 0.7 stack.18
  4.3 0.7 reshape.61
  5.1 0.2 compare_reduce_fusion
  5.3 0.2 convert_reduce_fusion
  5.5 0.1 select_n.51
  5.5 0.1 select_n.53
  5.6 0.6 pad_add_fusion.refs_0_
  6.2 0.6 fusion.6.refs_7_
  6.9 147.0 %layer.1 = (bf16[256,768]{1,0:T(8,128)(2,1)}, f32[256,768]{1,0:T(8,128)}, bf16[2,4,96,576]{3,2,1,0:T(8,128)(2,1)}, bf16[2,4,96,768]{3,2,1,0:T(8,128)(2,1)}, bf16...) custom-call(s32[36]{0:T(128)} %pad_add_fusion.refs_0_, bf16[2,128,768]{2,1,0:T(8,128)(2,1)} %bitcast.10, ...), custom_call_target="tpu_custom_call" | custom-call | tf_op jit(solution)/shard_map/layer/pallas_call | solution.py:1552
  153.8 1.3 slice_reduce_fusion.1
  155.2 1.3 slice_reduce_fusion
  156.5 1.4 fusion.12
  157.9 0.0 copy-start.2
  157.9 0.0 copy-start.1
  158.0 5.5 %assemble.1 = (f32[192,2304]{1,0:T(8,128)}, f32[192,3072]{1,0:T(8,128)}, f32[768,768]{1,0:T(8,128)}, f32[192,768]{1,0:T(8,128)}) custom-call(bf16[2,4,96,576]{3,2,1,0:T(8,128)(2,1)} %get-tuple-element.28.fq_ref, bf16[2,4,96,768]{3,2,1,0:T(8,128)(2,1)} %get-tuple-element.29.fu_ref, bf16[2,4,96,768]{3,2,1,0:T(8,128)(2,1)} %get-tuple-element.30.fd_ref, ...), custom_call_target="tpu_custom_call" | custom-call | tf_op jit(solution)/shard_map/assemble/pallas_call | solution.py:1567
  163.4 0.0 copy-start
  163.4 0.0 copy-done.2
  163.4 0.6 copy.34
  164.0 0.0 copy-done.1
  164.0 0.7 copy.35
  164.7 0.0 copy-done
  164.7 0.9 copy.36
  (5 shorter events, 0.1 us)
Async XLA Ops:
  157.9 5.5 %copy-start.2 = (f32[1,192]{1,0:T(1,128)}, f32[1,192]{1,0:T(1,128)S(1)}, u32[]{:S(2)}) copy-start(f32[1,192]{1,0:T(1,128)S(1)} %get-tuple-element.40) | copy-start | bytes 2308
  157.9 6.0 %copy-start.1 = (bf16[256,768]{1,0:T(8,128)(2,1)S(1)}, bf16[256,768]{1,0:T(8,128)(2,1)}, u32[]{:S(2)}) copy-start(bf16[256,768]{1,0:T(8,128)(2,1)} %get-tuple-element.25) | copy-start | bytes 1179652
  163.4 1.3 copy-start

commit v3 on v2

--- a/solution.py
+++ b/solution.py
@@ -524,46 +524,46 @@
 class PlaneShare:
     def __init__(self, copies, me, source, slot, rows):
         self.copies, self.me, self.slot = copies, me, slot
-        self.top, self.bottom = pl.ds(0, rows // 2), pl.ds(rows // 2, rows // 2)
+        top, bottom = pl.ds(0, rows // 2), pl.ds(rows // 2, rows // 2)
         own = slot(me.k, me.t)
-        self.to_x = copies.make(source, own, me.on_plane(me.xn))
-        self.to_y = copies.make(source, own, me.on_plane(me.yn))
+        to_x, to_y = me.on_plane(me.xn), me.on_plane(me.yn)
+        self.x_first = copies.make(source.at[top], own.at[top], to_x)
+        self.y_first = copies.make(source.at[bottom], own.at[bottom], to_y)
+        self.x_second = copies.make(source.at[bottom], own.at[bottom], to_x)
+        self.y_second = copies.make(source.at[top], own.at[top], to_y)
         self.to_p = copies.make(source, own, me.on_plane(me.pn))
-        self.swaps = [self.to_p]
-        through_x, through_y = slot(me.k, me.tx).at[self.top], slot(me.k, me.ty).at[self.bottom]
-        self.hop_y = copies.make(through_x, through_x, me.on_plane(me.yn))
-        self.hop_x = copies.make(through_y, through_y, me.on_plane(me.xn))
+        through_x, through_y = slot(me.k, me.tx).at[top], slot(me.k, me.ty).at[bottom]
+        self.hop_y = copies.make(through_x, through_x, to_y)
+        self.hop_x = copies.make(through_y, through_y, to_x)
+        self.swaps = []
+        for chip in (me.tx, me.ty, me.td):
+            place = slot(me.k, chip)
+            self.swaps.append(copies.make(place, place, me.on_plane(me.pn)))
 
     def start(self):
-        self.to_x.start()
-        self.to_y.start()
-        self.to_p.start()
-
-    def swap(self, place):
-        copy = self.copies.make(place, place, self.me.on_plane(self.me.pn))
-        copy.start()
-        self.swaps.append(copy)
-
-    def on_x(self):
-        self.to_x.wait_recv()
+        for copy in (self.x_first, self.y_first, self.x_second, self.y_second, self.to_p):
+            copy.start()
+
+    def relay(self):
+        self.x_first.wait_recv()
         self.hop_y.start()
-        self.swap(self.slot(self.me.k, self.me.tx))
-
-    def on_y(self):
-        self.to_y.wait_recv()
+        self.y_first.wait_recv()
         self.hop_x.start()
-        self.swap(self.slot(self.me.k, self.me.ty))
+
+    def swap(self):
+        self.x_second.wait_recv()
+        self.swaps[0].start()
+        self.y_second.wait_recv()
+        self.swaps[1].start()
 
     def on_diagonal(self):
-        diagonal = self.slot(self.me.k, self.me.td)
         self.hop_y.wait_recv()
-        self.swap(diagonal.at[self.top])
         self.hop_x.wait_recv()
-        self.swap(diagonal.at[self.bottom])
+        self.swaps[2].start()
 
     def finish(self):
-        for swap in self.swaps:
-            swap.wait_recv()
+        for copy in (self.to_p, *self.swaps):
+            copy.wait_recv()
 
 
 class LineGather:
@@ -617,55 +617,41 @@
         self.me, self.source, self.target = me, source, target
         rows = target.shape[0] // 2
         mine = pl.ds(me.k * rows, rows)
-        here, up, down = me.z == me.t, me.z > me.t, me.z < me.t
-        self.here, self.up, self.down = here, up, down
-        not_last, not_first = me.z < me.nz - 1, me.z > 0
-        to_up, to_down = me.on_line(me.above), me.on_line(me.below)
+        self.here, self.away = me.z == me.t, me.z != me.t
         place = target.at[mine]
-        self.first_up = copies.make(source.at[mine], place, to_up, when=here & not_last)
-        self.first_down = copies.make(source.at[mine], place, to_down, when=here & not_first)
-        self.next_up = copies.make(place, place, to_up, when=up & not_last, like=self.first_up)
-        self.next_down = copies.make(place, place, to_down, when=down & not_first, like=self.first_down)
-        self.not_last, self.not_first = not_last, not_first
-        self.swap = copies.make(place, place, me.on_plane(me.pn), when=up | down)
+        self.sends, self.arrivals = [], []
+        for distance in range(1, me.nz):
+            target_z = (me.t + distance) % me.nz
+            copy = copies.make(source.at[mine], place, me.on_line(target_z), when=self.here)
+            self.sends.append(copy)
+            self.arrivals.append(me.z == target_z)
+        self.swap = copies.make(place, place, me.on_plane(me.pn), when=self.away)
 
     def start(self):
-        pl.when(self.here & self.not_last)(self.first_up.start)
-        pl.when(self.here & self.not_first)(self.first_down.start)
-
         @pl.when(self.here)
         def _():
+            for copy in self.sends:
+                copy.start()
             self.target[...] = self.source[...]
 
     def advance(self):
-        pl.when(self.up)(self.first_up.wait_recv)
-        pl.when(self.down)(self.first_down.wait_recv)
-        pl.when(self.up & self.not_last)(self.next_up.start)
-        pl.when(self.down & self.not_first)(self.next_down.start)
-        pl.when(self.up | self.down)(self.swap.start)
+        for copy, arrives in zip(self.sends, self.arrivals):
+            pl.when(arrives)(copy.wait_recv)
+        pl.when(self.away)(self.swap.start)
 
     def finish(self):
-        pl.when(self.up | self.down)(self.swap.wait_recv)
-
-
-def add_narrow(target, index, incoming):
-    target[index] = narrow(wide(target[index]) + wide(incoming[index]))
+        pl.when(self.away)(self.swap.wait_recv)
 
 
 class LineReduce:
-    def __init__(self, copies, me, source, total, up, down):
-        self.me, self.source, self.total, self.up, self.down = me, source, total, up, down
+    def __init__(self, copies, me, source, total, landed):
+        self.me, self.source, self.total, self.landed = me, source, total, landed
         half = total.shape[1]
         self.mine, theirs = pl.ds(me.k * half, half), pl.ds((1 - me.k) * half, half)
         self.exchange = copies.make(source.at[:, theirs], total, me.on_plane(me.pn))
-        self.sends = {}
-        for owner in range(me.nz):
-            self.sends[owner, 0] = copies.make(
-                total.at[owner], up.at[owner], me.on_line(me.above), when=me.z < owner
-            )
-            self.sends[owner, 1] = copies.make(
-                total.at[owner], down.at[owner], me.on_line(me.below), when=me.z > owner
-            )
+        self.sends = [
+            copies.make(total.at[other], landed.at[me.z], me.on_line(other)) for other in me.others
+        ]
 
     def start(self):
         self.exchange.start()
@@ -676,48 +662,30 @@
             self.total[owner] = narrow(
                 wide(self.total[owner]) + wide(self.source[owner, self.mine])
             )
-
-    def events(self, place):
-        nz, found = self.me.nz, []
-        for owner in range(place, nz):
-            if place > 0 or owner > place:
-                found.append((nz - 1 - owner + place, 0, owner))
-        for owner in range(place + 1):
-            if place < nz - 1 or owner < place:
-                found.append((owner + nz - 1 - place, 1, owner))
-        return sorted(found)
-
-    def step(self, place, way, owner):
-        incoming = (self.up, self.down)[way]
-        send = self.sends[owner, way]
-        if (way == 0 and place > 0) or (way == 1 and place < self.me.nz - 1):
+        for send in self.sends:
+            send.start()
+
+    def collect(self):
+        me = self.me
+        result = wide(self.total[me.z])
+        for send in self.sends:
             send.wait_recv()
-            add_narrow(self.total, owner, incoming)
-        if owner != place:
-            send.start()
-
-
-def reduce_along(me, reductions, time):
-    for place in range(me.nz):
-        found = [event for event in reductions[0].events(place) if event[0] == time]
-        if not found:
-            continue
-
-        @pl.when(me.z == place)
-        def _():
-            for _, way, owner in found:
-                for reduction in reductions:
-                    reduction.step(place, way, owner)
+        for other in me.others:
+            result = result + wide(self.landed[other])
+        self.total[me.z] = narrow(result)
 
 
 class LineCollect:
-    def __init__(self, copies, me, source, total, up, down):
-        self.me, self.source, self.total, self.up, self.down = me, source, total, up, down
+    def __init__(self, copies, me, source, total, landed):
+        self.me, self.source, self.total, self.landed = me, source, total, landed
         half = total.shape[0]
         self.mine, theirs = pl.ds(me.k * half, half), pl.ds((1 - me.k) * half, half)
         self.exchange = copies.make(source.at[theirs], total, me.on_plane(me.pn))
-        self.to_up = copies.make(total, up, me.on_line(me.above), when=me.z < me.t)
-        self.to_down = copies.make(total, down, me.on_line(me.below), when=me.z > me.t)
+        self.sends = []
+        for distance in range(1, me.nz):
+            leaves = (me.z + distance) % me.nz == me.t
+            copy = copies.make(total, landed.at[me.z], me.on_line(me.t), when=leaves)
+            self.sends.append((copy, leaves))
 
     def start(self):
         self.exchange.start()
@@ -725,29 +693,20 @@
     def pair(self):
         self.exchange.wait_recv()
         self.total[...] = narrow(wide(self.total[...]) + wide(self.source[self.mine]))
-
-    def take(self, incoming):
-        self.total[...] = narrow(wide(self.total[...]) + wide(incoming[...]))
-
-    def along(self, time):
+        for copy, leaves in self.sends:
+            pl.when(leaves)(copy.start)
+
+    def collect(self):
         me = self.me
-        for place in range(me.nz):
-
-            @pl.when((me.z == place) & (me.t >= place))
-            def _():
-                if place == time:
-                    if place > 0:
-                        self.to_up.wait_recv()
-                        self.take(self.up)
-                    pl.when(me.t > place)(self.to_up.start)
-
-            @pl.when((me.z == place) & (me.t <= place))
-            def _():
-                if me.nz - 1 - place == time:
-                    if place < me.nz - 1:
-                        self.to_down.wait_recv()
-                        self.take(self.down)
-                    pl.when(me.t < place)(self.to_down.start)
+
+        @pl.when(me.z == me.t)
+        def _():
+            result = wide(self.total[...])
+            for copy, _ in self.sends:
+                copy.wait_recv()
+            for other in me.others:
+                result = result + wide(self.landed[other])
+            self.total[...] = narrow(result)
 
 
 class PlaneSpread:
@@ -855,29 +814,63 @@
                     target[:, piece * part : (piece + 1) * part] = source[:, first : first + part]
 
 
+VECTORS = ("gain1", "shift1", "gain2", "shift2", "bout", "bdown", "bqkv", "bup")
+
+
+def pack_vectors(r):
+    first = 0
+    for name in VECTORS:
+        values = wide(getattr(r, name)[...])
+        count = values.shape[0]
+        r.sm[0:1, first : first + count] = values.reshape(1, count)
+        first += count
+
+
 def read_vectors(r, me):
     nz, part = me.nz, r.vec.shape[1] // me.nz
-    shards = [wide(r.sm4[z]) for z in range(nz)]
-    for row in range(4):
-        for z in range(nz):
-            r.vec[row : row + 1, z * part : (z + 1) * part] = shards[z][
-                0:1, row * part : (row + 1) * part
-            ]
+
+    def piece(z, number):
+        return r.sm4[z, 0:1, number * part : (number + 1) * part]
+
     for z in range(nz):
-        r.vec[4:5, z * part : (z + 1) * part] = shards[z][1:2, :part] + shards[z][1:2, part : 2 * part]
+        span = slice(z * part, (z + 1) * part)
+        for row in range(4):
+            r.vec[row : row + 1, span] = piece(z, row)
+        r.vec[4:5, span] = piece(z, 4) + piece(z, 5)
     chips = nz
     for chip in range(chips):
 
         @pl.when(me.t == chip)
         def _():
-            for piece in range(3):
-                number = piece * chips + chip
-                first = number % 3 * part
-                r.vec[5:6, piece * part : (piece + 1) * part] = shards[number // 3][
-                    2:3, first : first + part
-                ]
+            for number in range(3):
+                held = number * chips + chip
+                r.vec[5:6, number * part : (number + 1) * part] = piece(held // 3, 6 + held % 3)
             for z in range(nz):
-                r.vec[6:7, z * part : (z + 1) * part] = shards[z][3:4, chip * part : (chip + 1) * part]
+                r.vec[6:7, z * part : (z + 1) * part] = piece(z, 9 + chip)
+
+
+def block_table(r, me):
+    count = r.order.shape[0]
+    chips, quarter = me.nz, count // 4
+    sides = count // (2 * chips)
+    held = [r.order[number] for number in range(count)]
+    for position in range(count):
+        found = 0
+        for number in range(1, count):
+            found = jnp.where(held[number] == position, number, found)
+        r.idx[position] = found
+    for chip in range(chips):
+        for owner, first in ((me.k, count), (1 - me.k, count + chips * sides)):
+            for side in range(sides):
+                position = r.order[(2 * chip + owner) * sides + side]
+                low = (position >= quarter * me.k) & (position < quarter * (me.k + 1))
+                high = position - 2 * quarter + quarter * me.k
+                r.idx[first + chip * sides + side] = jnp.where(
+                    low, position - quarter * me.k, jnp.clip(high, 0, 2 * quarter - 1)
+                )
+        position = r.order[(2 * chip + me.k) * sides]
+        outer = jnp.where((position < quarter) | (position >= 3 * quarter), 0, 1)
+        r.idx[count + 2 * chips * sides + chip] = jnp.where(outer == me.k, 1, 0)
 
 
 def sorted_rows(r, source, block, blocks):
@@ -885,6 +878,10 @@
     for number in range(blocks):
         pieces.append(source[r.idx[block + number]])
     return jnp.concatenate(pieces, axis=0)
+
+
+def flat_rows(values):
+    return values.reshape(-1, values.shape[-1])
 
 
 def put_blocks(target, tile, values):
@@ -959,6 +956,7 @@
     state = visit(last, state, True)
     merged = jnp.concatenate([acc / total for _, total, acc in state], axis=0)
     r.att[rows, :] = narrow(merged.T)
+    r.attt[:, rows] = narrow(merged)
     for head in range(heads):
         r.lse[head : head + 1, rows] = state[head][0] + jnp.log(state[head][1])
 
@@ -980,8 +978,7 @@
     slope = below + up * jnp.exp(-0.5 * up * up) * INV_ROOT_TWO_PI
     d_up = mm(cotan, down_weight, NT) * slope
     d_up16 = narrow(d_up)
-    attended = r.att[place, :]
-    put_blocks(r.outb, tile, narrow(mm(act, down_weight) + mm(attended, r.wo1[...])))
+    put_blocks(r.outb, tile, narrow(mm(act, down_weight)))
     d_normed = mm(d_up16, up_weight, NT)
     r.sums[2:3, :] += jnp.sum(d_normed * standardized, axis=0, keepdims=True)
     r.sums[3:4, :] += jnp.sum(d_normed, axis=0, keepdims=True)
@@ -991,20 +988,21 @@
     r.gl[place, :] = cotan
     r.act[place, :] = act
     r.du[place, :] = d_up16
-    d_att = narrow(mm(cotan, r.wo1[...], NT))
-    r.datt[place, :] = d_att
-    product = wide(d_att) * wide(attended)
-    shape = (8, product.shape[1])
-    picked = lax.broadcasted_iota(jnp.int32, shape, 1) // HD == lax.broadcasted_iota(
-        jnp.int32, shape, 0
-    )
-    r.delta[:, place] = lax.dot_general(
-        picked.astype(jnp.float32),
-        product,
-        NT,
-        precision=lax.Precision.HIGHEST,
-        preferred_element_type=jnp.float32,
-    )
+
+
+def out_project(r, me, tile):
+    place = pl.ds(pl.multiple_of(tile * QTILE, QTILE), QTILE)
+    blocks = QTILE // BLK
+    attended = r.att[place, :]
+    mlp = flat_rows(r.outb[pl.ds(tile * blocks, blocks)])
+    put_blocks(r.outb, tile, narrow(wide(mlp) + mm(attended, r.wo1[...])))
+    cotan = r.gl[place, :]
+    r.datt[place, :] = narrow(mm(cotan, r.wo1[...], NT))
+    product = wide(narrow(mm(r.wo1[...], cotan, NT))) * wide(r.attt[:, place])
+    for head in range(product.shape[0] // HD):
+        r.delta[head : head + 1, place] = jnp.sum(
+            product[head * HD : (head + 1) * HD], axis=0, keepdims=True
+        )
 
 
 def weight_grad(target, left, right):
@@ -1087,23 +1085,33 @@
     put_blocks(r.outb, tile, narrow(d_normed * gain1 + r.e2[place, :]))
 
 
-def flat_rows(values):
-    return values.reshape(-1, values.shape[-1])
-
-
 class Scatter:
     def __init__(self, copies, me, r, source, sent, got, landed):
         self.me, self.r, self.source, self.sent, self.got, self.landed = me, r, source, sent, got, landed
-        self.chips, self.sides = landed.shape[0], landed.shape[1]
+        self.chips = me.nz
+        self.sides = sent.shape[0] // self.chips
         self.first = r.k.shape[0] // BLK
         self.exchanges = [
             copies.make(self.piece(sent, chip), self.piece(got, chip), me.on_plane(me.pn))
             for chip in range(self.chips)
         ]
-        self.moves = [
-            copies.make(self.piece(got, chip), landed.at[me.t], me.on_plane(peer))
-            for chip, peer in ((me.tx, me.xn), (me.ty, me.yn), (me.td, me.dn))
-        ]
+        self.steps = []
+        for side, near, far, to_near, to_far in (
+            (0, me.tx, me.ty, me.xn, me.yn),
+            (1, me.ty, me.tx, me.yn, me.xn),
+        ):
+            first, last = self.place(near, side), self.place(far, side)
+            self.steps.append(
+                (
+                    copies.make(got.at[self.place(me.td, side)], landed.at[3 * side], me.on_plane(to_near)),
+                    copies.make(got.at[first], landed.at[3 * side + 1], me.on_plane(to_near)),
+                    copies.make(got.at[last], landed.at[3 * side + 2], me.on_plane(to_far)),
+                    last,
+                )
+            )
+
+    def place(self, chip, side):
+        return chip * self.sides + side
 
     def piece(self, array, chip):
         return array.at[pl.ds(chip * self.sides, self.sides)]
@@ -1127,17 +1135,28 @@
             own, other = wide(self.block(number)), wide(self.got[number])
             here = jnp.full(own.shape, flag, jnp.int32) > 0
             self.got[number] = narrow(jnp.where(here, own, other))
-        for move in self.moves:
-            move.start()
+        for far, _, _, _ in self.steps:
+            far.start()
+        for _, near, _, _ in self.steps:
+            near.start()
+
+    def middle(self):
+        for side, (far, _, on, last) in enumerate(self.steps):
+            far.wait_recv()
+            self.got[last] = narrow(wide(self.got[last]) + wide(self.landed[3 * side]))
+            on.start()
 
     def total(self):
-        for move in self.moves:
-            move.wait_recv()
-        me = self.me
-        result = wide(self.got[pl.ds(me.t * self.sides, self.sides)])
-        for chip in (me.tx, me.ty, me.td):
-            result = result + wide(self.landed[chip])
-        return flat_rows(result)
+        pieces = []
+        for side, (_, near, on, _) in enumerate(self.steps):
+            near.wait_recv()
+            on.wait_recv()
+            pieces.append(
+                wide(self.got[self.place(self.me.t, side)])
+                + wide(self.landed[3 * side + 1])
+                + wide(self.landed[3 * side + 2])
+            )
+        return jnp.concatenate(pieces, axis=0)
 
 
 def layer_kernel(nz, names, *refs):
@@ -1149,6 +1168,7 @@
     tiles = r.att.shape[0] // QTILE
 
     slice_weights(r, me)
+    pack_vectors(r)
     me.greet()
 
     def row_slot(array):
@@ -1168,102 +1188,109 @@
     for copy in small:
         copy.start()
     wu.start()
+    own_down = pltpu.make_async_copy(
+        r.wdown.at[pl.ds(me.t * shard, shard)], r.wd4.at[me.z], r.local_sem
+    )
+    own_down.start()
     r.hall[own_rows] = r.h[...]
     r.gall[own_rows] = r.g[...]
     r.wq4[me.z] = r.wqs[...]
     r.wu4[me.z] = r.wus[...]
-    own_down = pltpu.make_async_copy(
-        r.wdown.at[pl.ds(me.t * shard, shard)], r.wd4.at[me.z], r.local_sem
-    )
-    own_down.start()
     r.sm4[me.z] = r.sm[...]
+    block_table(r, me)
     r.sums[...] = jnp.zeros_like(r.sums)
     r.vout[...] = jnp.zeros_like(r.vout)
     r.dk[...] = jnp.zeros_like(r.dk)
     r.dv[...] = jnp.zeros_like(r.dv)
     wq.advance(0)
-    h_share.on_x()
-    h_share.on_y()
-    g_share.start()
+    h_share.relay()
+    wu.advance(0)
     wq.advance(1)
     wd.start()
-    wo.start()
-    wq.advance(2)
+    h_share.swap()
+    g_share.start()
     for copy in small:
         copy.wait_recv()
     read_vectors(r, me)
-    wu.advance(0)
+    wq.advance(2)
+    wu.advance(1)
     h_share.on_diagonal()
     wq.finish()
     h_share.finish()
 
-    @pl.loop(0, r.k.shape[0] // QTILE)
-    def _(tile):
-        project(r, tile)
-
-    wd.advance(0)
-    g_share.on_x()
-    g_share.on_y()
+    count = r.k.shape[0] // QTILE
+    for first in (0, count // 2):
+
+        @pl.loop(first, first + count // 2)
+        def _(tile):
+            project(r, tile)
+
+        if first == 0:
+            wd.advance(0)
+
+    wu.advance(2)
+    wd.advance(1)
     attend(r, me, 0)
-    wu.advance(1)
-    wd.advance(1)
+    g_share.relay()
     attend(r, me, 1)
-    wo.advance()
-    wu.advance(2)
+    wd.advance(2)
+    wo.start()
+    g_share.swap()
     attend(r, me, 2)
     g_share.on_diagonal()
-    wd.advance(2)
-    for tile in range(3, tiles):
-        attend(r, me, tile)
     own_down.wait()
     wu.finish()
     wd.finish()
-    wo.finish()
     g_share.finish()
-    copies.settle([g_share.hop_x, g_share.hop_y, *g_share.swaps[1:]])
+    copies.settle([g_share.hop_x, g_share.hop_y, *g_share.swaps])
 
     @pl.loop(0, tiles)
     def _(tile):
         feed_forward(r, me, tile)
 
+    half = shard // 2
     out_scatter = Scatter(copies, me, r, r.outb, r.osent, r.ogot, r.oland)
-    out_scatter.start()
-    up_reduce = LineReduce(copies, me, r.gu, r.tu, r.uu, r.du_in)
-    down_reduce = LineReduce(copies, me, r.gd, r.td, r.ud, r.dd_in)
-    out_reduce = LineCollect(copies, me, r.go, r.to, r.uo, r.do_in)
+    up_reduce = LineReduce(copies, me, r.gu, r.tu, r.uu)
+    down_reduce = LineReduce(copies, me, r.gd, r.td, r.ud)
+    out_reduce = LineCollect(copies, me, r.go, r.to, r.uo)
+    d_share = PlaneShare(copies, me, r.td.at[me.z], lambda core, chip: r.fd.at[core, chip], half)
+    u_share = PlaneShare(copies, me, r.tu.at[me.z], lambda core, chip: r.fu.at[core, chip], half)
+    o_spread = PlaneSpread(copies, me, r.to, r.fo, half)
+
+    def share_down():
+        d_share.start()
+        r.fd[me.k, me.t] = r.td[me.z]
+
+    def share_up():
+        u_share.start()
+        r.fu[me.k, me.t] = r.tu[me.z]
+
     weight_grad(r.gd, r.act, r.gl)
     down_reduce.start()
     weight_grad(r.gu, r.n, r.du)
     up_reduce.start()
+    down_reduce.pair()
+    wo.advance()
+    up_reduce.pair()
+    attend(r, me, 3)
+    wo.finish()
+
+    @pl.loop(0, tiles)
+    def _(tile):
+        out_project(r, me, tile)
+
+    out_scatter.start()
     r.go[...] = narrow(mm(r.att[...], r.gl[...], TN))
     out_reduce.start()
+    attend_grad(r, me, 0)
     out_scatter.spread()
-    down_reduce.pair()
-    up_reduce.pair()
     out_reduce.pair()
-    early = [down_reduce, up_reduce]
-    reduce_along(me, early, 0)
-    out_reduce.along(0)
-    attend_grad(r, me, 0)
-    reduce_along(me, early, 1)
-    out_reduce.along(1)
     attend_grad(r, me, 1)
-    reduce_along(me, early, 2)
-    out_reduce.along(2)
     attend_grad(r, me, 2)
-    reduce_along(me, early, 3)
-    out_reduce.along(3)
-    half = shard // 2
-    d_share = PlaneShare(copies, me, r.td.at[me.z], lambda core, chip: r.fd.at[core, chip], half)
-    u_share = PlaneShare(copies, me, r.tu.at[me.z], lambda core, chip: r.fu.at[core, chip], half)
-    o_spread = PlaneSpread(copies, me, r.to, r.fo, half)
-    d_share.start()
-    u_share.start()
-    o_spread.start()
-    r.fd[me.k, me.t] = r.td[me.z]
-    r.fu[me.k, me.t] = r.tu[me.z]
-    for tile in range(3, tiles):
-        attend_grad(r, me, tile)
+    down_reduce.collect()
+    share_down()
+    out_scatter.middle()
+    attend_grad(r, me, 3)
 
     part = r.k.shape[1]
     quarter = r.k.shape[0] // 4
@@ -1277,11 +1304,12 @@
         copy = copies.make(r.act.at[rows, : 2 * part], r.kvin.at[rows], me.on_plane(me.pn))
         copy.start()
         kv_moves.append(copy)
-    d_share.on_x()
-    d_share.on_y()
-    u_share.on_x()
-    u_share.on_y()
-    o_spread.advance()
+    d_share.relay()
+    up_reduce.collect()
+    share_up()
+    d_share.swap()
+    out_reduce.collect()
+    o_spread.start()
     for copy in kv_moves:
         copy.wait_recv()
 
@@ -1293,12 +1321,14 @@
         copies, me, r, r.outb, r.gall.at[: r.outb.shape[0]], r.gall.at[r.outb.shape[0] :], r.eland
     )
     e_scatter.start()
+    u_share.relay()
     weight_grad(r.gq, r.n, r.du.at[:, : 3 * part])
-    qkv_reduce = LineReduce(copies, me, r.gq, r.tq, r.uq, r.dq_in)
+    qkv_reduce = LineReduce(copies, me, r.gq, r.tq, r.uq)
     qkv_reduce.start()
     e_scatter.spread()
     qkv_reduce.pair()
-    reduce_along(me, [qkv_reduce], 0)
+    u_share.swap()
+    o_spread.advance()
 
     vec_part = r.vec.shape[1] // nz
     r.sums[4:5, :] = jnp.sum(wide(flat_rows(r.g[...])), axis=0, keepdims=True)
@@ -1328,20 +1358,19 @@
     for copy in vec_line:
         copy.start()
     d_share.on_diagonal()
-    u_share.on_diagonal()
-    o_spread.on_diagonal()
-    reduce_along(me, [qkv_reduce], 1)
     for copy in vec_line:
         copy.wait_recv()
     vector = r.vout[me.z]
     for other in me.others:
         vector = vector + r.vline[other]
     r.vsend[...] = vector
-    reduce_along(me, [qkv_reduce], 2)
+    e_scatter.middle()
     vec_plane = [copies.make(r.vsend, r.vplane.at[me.c], me.on_plane(peer)) for peer in me.plane]
     for copy in vec_plane:
         copy.start()
-    reduce_along(me, [qkv_reduce], 3)
+    u_share.on_diagonal()
+    o_spread.on_diagonal()
+    qkv_reduce.collect()
     q_share = PlaneShare(copies, me, r.tq.at[me.z], lambda core, chip: r.fq.at[core, chip], half)
     q_share.start()
     r.fq[me.k, me.t] = r.tq[me.z]
@@ -1349,14 +1378,14 @@
     residual = wide(flat_rows(r.h[...]))
     own_standardized, own_deviation = norm_rows(residual)
     r.hidden_out[...] = narrow(residual + r.vec[4:5, :] + out_scatter.total())
-    q_share.on_x()
-    q_share.on_y()
+    q_share.relay()
     e_total = e_scatter.total()
     r.hidden_grad[...] = wide(flat_rows(r.g[...])) + own_deviation * (
         e_total
         - jnp.mean(e_total, axis=-1, keepdims=True)
         - own_standardized * jnp.mean(e_total * own_standardized, axis=-1, keepdims=True)
     )
+    q_share.swap()
     for copy in vec_plane:
         copy.wait_recv()
     vector = r.vsend[...]
@@ -1371,21 +1400,30 @@
     copies.finish()
 
 
-def assemble_kernel(fq_ref, fu_ref, fd_ref, fo_ref, gq_ref, gu_ref, gd_ref, go_ref):
-    cores, chips, half, _ = fq_ref.shape
+def assemble_kernel(
+    fq_ref, fu_ref, fd_ref, fo_ref, out_ref, grad_ref, vsum_ref,
+    gq_ref, gu_ref, gd_ref, go_ref, hidden_out_ref, hidden_grad_ref, *vector_refs,
+):
+    _, chips, _, _ = fq_ref.shape
     part = fq_ref.shape[3] // 3
-    for core in range(cores):
-        rows = slice(core * half, (core + 1) * half)
-        go_ref[rows, :] = wide(fo_ref[core])
-        for chip in range(chips):
-            for source, target in ((fq_ref, gq_ref), (fu_ref, gu_ref)):
-                for piece in range(source.shape[3] // part):
-                    first = (piece * chips + chip) * part
-                    target[rows, first : first + part] = wide(
-                        source[core, chip, :, piece * part : (piece + 1) * part]
-                    )
-            first = chip * cores * half + core * half
-            gd_ref[first : first + half, :] = wide(fd_ref[core, chip])
+    hidden_out_ref[...] = out_ref[...]
+    hidden_grad_ref[...] = grad_ref[...]
+    go_ref[...] = wide(fo_ref[0])
+    for chip in range(chips):
+        for source, target in ((fq_ref, gq_ref), (fu_ref, gu_ref)):
+            for piece in range(source.shape[3] // part):
+                first = (piece * chips + chip) * part
+                target[:, first : first + part] = wide(
+                    source[0, chip, :, piece * part : (piece + 1) * part]
+                )
+        gd_ref[chip, 0] = wide(fd_ref[0, chip])
+
+    @pl.when(pl.program_id(0) == 0)
+    def _():
+        places = [(0, n) for n in range(4)] + [(1, 0), (1, 0), (2, 0), (3, 0)]
+        for target, (row, number) in zip(vector_refs, places):
+            count = target.shape[0]
+            target[...] = vsum_ref[row : row + 1, number * count : (number + 1) * count].reshape(count)
 
 
 def rotary_parts(block_count):
@@ -1400,32 +1438,9 @@
     return table(np.arange(BLK)), table(np.arange(block_count) * BLK)
 
 
-def block_table(block_order, chips, core):
-    count = block_order.shape[0]
-    quarter = count // 4
-    places = jnp.arange(count, dtype=jnp.int32)
-    gathered = jnp.sum(
-        jnp.where(block_order[:, None] == places[None, :], places[:, None], 0), axis=0
-    )
-    pairs = block_order.reshape(chips, 2, count // (2 * chips))
-    local = jnp.where(
-        (pairs >= quarter * core) & (pairs < quarter * (core + 1)),
-        pairs - quarter * core,
-        jnp.clip(pairs - (3 * quarter - quarter * core) + quarter, 0, 2 * quarter - 1),
-    )
-    outer = (pairs[:, :, 0] < quarter) | (pairs[:, :, 0] >= 3 * quarter)
-    here = outer == (core == 0)
-    mine = jnp.where(core == 0, local[:, 0], local[:, 1])
-    theirs = jnp.where(core == 0, local[:, 1], local[:, 0])
-    flags = jnp.where(core == 0, here[:, 0], here[:, 1])
-    return jnp.concatenate(
-        [gathered, mine.reshape(-1), theirs.reshape(-1), flags.astype(jnp.int32)]
-    ).astype(jnp.int32)
-
-
 VMEM_SPEC = pl.BlockSpec(memory_space=pltpu.VMEM)
 SPECS = {
-    "idx": pl.BlockSpec(memory_space=pltpu.SMEM),
+    "order": pl.BlockSpec(memory_space=pltpu.SMEM),
     "wdown": pl.BlockSpec(memory_space=pl.ANY),
 }
 VMEM_LIMIT = 63 * 1024 * 1024
@@ -1453,7 +1468,6 @@
     h, g = hidden_in[0], cotangent[0]
     local_rows, width = h.shape
     chips = lax.axis_size("ctx") // 2
-    core = lax.axis_index("ctx") % 2
     shard = qkv_weight.shape[0]
     half = shard // 2
     part = width // chips
@@ -1462,24 +1476,24 @@
     everyone = 2 * rows
     sides = local_rows // BLK
 
-    idx = block_table(block_order, chips, core)
-    first = jnp.concatenate([norm1_gain, attention_norm_bias, norm2_gain, feedforward_norm_bias])
-    second = jnp.concatenate([out_bias, down_bias])
-    lines = [
-        jnp.pad(line, (0, width - line.shape[0])) for line in (first, second, qkv_bias, up_bias)
-    ]
-    sm = jnp.pad(jnp.stack(lines), ((0, 12), (0, 0)))
+    small = 6 * shard + qkv_bias.shape[0] + up_bias.shape[0]
     rope_r, rope_b = rotary_parts(everyone // BLK)
 
     inputs = {
-        "idx": idx,
+        "order": block_order,
         "h": h.reshape(sides, BLK, width),
         "g": g.reshape(sides, BLK, width),
         "wqkv": qkv_weight,
         "wup": up_weight,
         "wdown": down_weight,
         "wout": out_weight,
-        "sm": sm,
+        **dict(
+            zip(
+                VECTORS,
+                (norm1_gain, attention_norm_bias, norm2_gain, feedforward_norm_bias)
+                + (out_bias, down_bias, qkv_bias, up_bias),
+            )
+        ),
         "rope_r": jnp.asarray(rope_r),
         "rope_b": jnp.asarray(rope_b),
     }
@@ -1501,7 +1515,8 @@
         "wu4": ((nz, shard, hidden), b16),
         "wd4": ((nz, shard, width), b16),
         "wo1": ((part, width), b16),
-        "sm4": ((nz, 16, width), b16),
+        "sm": ((1, small), f32),
+        "sm4": ((nz, 1, small), f32),
         "vec": ((8, width), f32),
         "sums": ((8, width), f32),
         "q": ((everyone, part), b16),
@@ -1510,6 +1525,7 @@
         "kt": ((part, everyone), b16),
         "vt": ((part, everyone), b16),
         "att": ((rows, part), b16),
+        "attt": ((part, rows), b16),
         "lse": ((8, rows), f32),
         "delta": ((8, rows), f32),
         "datt": ((rows, part), b16),
@@ -1525,36 +1541,33 @@
         "kvin": ((rows, 2 * part), b16),
         "osent": ((rows // BLK, BLK, width), b16),
         "ogot": ((rows // BLK, BLK, width), b16),
-        "oland": ((chips, sides, BLK, width), b16),
-        "eland": ((chips, sides, BLK, width), b16),
+        "oland": ((6, BLK, width), b16),
+        "eland": ((6, BLK, width), b16),
         "gq": ((nz, shard, 3 * part), b16),
         "gu": ((nz, shard, hidden), b16),
         "gd": ((nz, shard, width), b16),
         "go": ((part, width), b16),
         "tq": ((nz, half, 3 * part), b16),
         "uq": ((nz, half, 3 * part), b16),
-        "dq_in": ((nz, half, 3 * part), b16),
         "tu": ((nz, half, hidden), b16),
         "uu": ((nz, half, hidden), b16),
-        "du_in": ((nz, half, hidden), b16),
         "td": ((nz, half, width), b16),
         "ud": ((nz, half, width), b16),
-        "dd_in": ((nz, half, width), b16),
         "to": ((half, width), b16),
-        "uo": ((half, width), b16),
-        "do_in": ((half, width), b16),
+        "uo": ((nz, half, width), b16),
         "vout": ((nz, 8, width), f32),
         "vline": ((nz, 8, width), f32),
         "vsend": ((8, width), f32),
         "vplane": ((2 * chips, 8, width), f32),
     }
-    names = [*inputs, *outputs, *scratch, "send_sems", "recv_sems", "local_sem"]
+    names = [*inputs, *outputs, *scratch, "idx", "send_sems", "recv_sems", "local_sem"]
     results = pl.pallas_call(
         functools.partial(layer_kernel, nz, names),
         out_shape=tuple(jax.ShapeDtypeStruct(*leaf) for leaf in outputs.values()),
         in_specs=[SPECS.get(name, VMEM_SPEC) for name in inputs],
         out_specs=(VMEM_SPEC,) * len(outputs),
         scratch_shapes=[pltpu.VMEM(*leaf) for leaf in scratch.values()]
+        + [pltpu.SMEM((64,), jnp.int32)]
         + [pltpu.SemaphoreType.DMA((SEMAPHORES,))] * 2
         + [pltpu.SemaphoreType.DMA],
         compiler_params=pltpu.CompilerParams(
@@ -1564,35 +1577,69 @@
     )(*inputs.values())
     hidden_out, hidden_grad, fq, fu, fd, fo, vsum = results
 
-    grad_qkv, grad_up, grad_down, grad_out = pl.pallas_call(
+    steps = 4
+    some, few = shard // steps, local_rows // steps
+    inner = half // some
+
+    def pieces(cols):
+        return pl.BlockSpec((1, chips, some, cols), lambda i: (i // inner, 0, i % inner, 0))
+
+    def lines(count, cols):
+        return pl.BlockSpec((count, cols), lambda i: (i, 0))
+
+    def vector(count):
+        return pl.BlockSpec((count,), lambda i: (0,))
+
+    sizes = [shard] * 6 + [qkv_bias.shape[0], up_bias.shape[0]]
+    grad_qkv, grad_up, grad_down, grad_out, hidden_out, hidden_grad, *vectors = pl.pallas_call(
         assemble_kernel,
-        out_shape=tuple(
-            jax.ShapeDtypeStruct(weight.shape, f32)
-            for weight in (qkv_weight, up_weight, down_weight, out_weight)
-        ),
-        in_specs=[VMEM_SPEC] * 4,
-        out_specs=(VMEM_SPEC,) * 4,
+        grid=(steps,),
+        out_shape=(
+            jax.ShapeDtypeStruct(qkv_weight.shape, f32),
+            jax.ShapeDtypeStruct(up_weight.shape, f32),
+            jax.ShapeDtypeStruct((chips, steps, some, width), f32),
+            jax.ShapeDtypeStruct(out_weight.shape, f32),
+            jax.ShapeDtypeStruct(h.shape, b16),
+            jax.ShapeDtypeStruct(h.shape, f32),
+        )
+        + tuple(jax.ShapeDtypeStruct((size,), f32) for size in sizes),
+        in_specs=[
+            pieces(3 * part),
+            pieces(hidden),
+            pieces(width),
+            pl.BlockSpec((1, some, width), lambda i: (i // inner, i % inner, 0)),
+            lines(few, width),
+            lines(few, width),
+            pl.BlockSpec((8, width), lambda i: (0, 0)),
+        ],
+        out_specs=(
+            lines(some, qkv_weight.shape[1]),
+            lines(some, up_weight.shape[1]),
+            pl.BlockSpec((chips, 1, some, width), lambda i: (0, i, 0, 0)),
+            lines(some, width),
+            lines(few, width),
+            lines(few, width),
+        )
+        + tuple(vector(size) for size in sizes),
         compiler_params=pltpu.CompilerParams(vmem_limit_bytes=56 * 1024 * 1024),
         name="assemble",
-    )(fq, fu, fd, fo)
-
-    norms = vsum[0].reshape(nz, shard)
-    bias = vsum[1, :shard]
+    )(fq, fu, fd, fo, hidden_out, hidden_grad, vsum)
+    g_gain1, g_shift1, g_gain2, g_shift2, g_bout, g_bdown, g_bqkv, g_bup = vectors
     return (
         hidden_out[None],
         hidden_grad[None],
-        norms[0],
-        norms[1],
+        g_gain1,
+        g_shift1,
         grad_qkv,
-        vsum[2, : qkv_bias.shape[0]],
+        g_bqkv,
         grad_out,
-        bias,
-        norms[2],
-        norms[3],
+        g_bout,
+        g_gain2,
+        g_shift2,
         grad_up,
-        vsum[3, : up_bias.shape[0]],
-        grad_down,
-        bias,
+        g_bup,
+        grad_down.reshape(down_weight.shape),
+        g_bdown,
     )
 
 

time: 166 us -> 133 us (0.80)
  Pallas kernels: 152 us -> 132 us
  local copies, waits for them, and re-layouts: 8.62 us -> 0 us
  other arithmetic: 3.87 us -> 0 us
    pallas_call x1, Pallas kernels: 147 us -> 125 us  [sliced_layer(): pl.pallas_call(functools.partial(layer_kernel, nz, names), out_shape=tupl...]
    slice x3 -> x0, local copies, waits for them, and re-layouts: 4.12 us -> none  [the longest x1 1.45 us: sliced_layer(): norms[3]]
    unnamed x9 -> x0, local copies, waits for them, and re-layouts: 2.2 us -> none
    concatenate x3 -> x0, other arithmetic: 2.12 us -> none  [the longest x1 0.78 us: sliced_layer(): jnp.concatenate([norm1_gain, attention_norm_bias, norm2_gain, feedforward...]
where the time goes in v3:
time: 133 us; the launch traced here: 132 us
  Pallas kernels  132 us (99%)
    pallas_call x1, Pallas kernels, sliced_layer(): pl.pallas_call(functools.partial(layer_kernel, nz, names), out_shape=tupl...  125 us
    pallas_call x1, Pallas kernels, sliced_layer(): pl.pallas_call(assemble_kernel, grid=(steps,), out_shape=(jax.ShapeDtypeS...  6.37 us

profile of v3, /device:TPU:1, one launch (start us, length us, event | category | flops | bytes accessed | tf_op | source)
XLA Modules:
  0.0 132.4 jit_solution(13523333963758118019)
XLA Ops:
  0.7 125.2 %layer.1 = (bf16[256,768]{1,0:T(8,128)(2,1)}, f32[256,768]{1,0:T(8,128)}, bf16[2,4,96,576]{3,2,1,0:T(8,128)(2,1)}, bf16[2,4,96,768]{3,2,1,0:T(8,128)(2,1)}, bf16...) custom-call(s32[16]{0:T(128)} %refs_0_.1, bf16[2,128,768]{2,1,0:T(8,128)(2,1)} %bitcast.5, ...), custom_call_target="tpu_custom_call" | custom-call | tf_op jit(solution)/shard_map/layer/pallas_call | solution.py:1564
  125.9 6.4 %assemble.1 = (f32[192,2304]{1,0:T(8,128)}, f32[192,3072]{1,0:T(8,128)}, f32[4,4,48,768]{3,2,1,0:T(8,128)}, f32[192,768]{1,0:T(8,128)}, bf16[256,768]{1,0:T(8,12...) custom-call(bf16[2,4,96,576]{3,2,1,0:T(8,128)(2,1)} %get-tuple-eleme, ...), custom_call_target="tpu_custom_call" | custom-call | tf_op jit(solution)/shard_map/assemble/pallas_call | solution.py:1594

commit v4 on v3

--- a/solution.py
+++ b/solution.py
@@ -612,6 +612,33 @@
             run_when(ok, swap.wait_recv)
 
 
+class LineSend:
+    def __init__(self, copies, me, source, gathered):
+        self.me = me
+        rows = gathered.shape[1] // 2
+        mine = pl.ds(me.k * rows, rows)
+        self.sends, self.swaps = [], []
+        for distance, other in enumerate(me.others, 1):
+            self.sends.append(
+                copies.make(source.at[mine], gathered.at[me.z, mine], me.on_line(other))
+            )
+            place = gathered.at[(me.z - distance) % me.nz, mine]
+            self.swaps.append(copies.make(place, place, me.on_plane(me.pn)))
+
+    def start(self):
+        for send in self.sends:
+            send.start()
+
+    def advance(self):
+        for send, swap in zip(self.sends, self.swaps):
+            send.wait_recv()
+            swap.start()
+
+    def finish(self):
+        for swap in self.swaps:
+            swap.wait_recv()
+
+
 class LineSpread:
     def __init__(self, copies, me, source, target):
         self.me, self.source, self.target = me, source, target
@@ -773,13 +800,13 @@
     return jnp.where(inside, rows, jnp.zeros_like(rows))
 
 
-def rope_lanes(r, first, blocks, columns, back):
+def rope_lanes(r, blocks, columns, back):
     half_rot = ROT // 2
     tables = [[], [], []]
     row_cos, row_sin = r.rope_r[:, :128], r.rope_r[:, 128:]
     lane = lax.broadcasted_iota(jnp.int32, row_cos.shape, 1) % HD
-    for block in range(blocks):
-        both = r.rope_b[pl.ds(first + block, 1), :]
+    for block in blocks:
+        both = r.rope_b[block]
         block_cos, block_sin = both[:, :128], both[:, 128:]
         cosine = block_cos * row_cos - block_sin * row_sin
         sine = block_sin * row_cos + block_cos * row_sin
@@ -889,43 +916,56 @@
     target[pl.ds(tile * blocks, blocks)] = values.reshape(blocks, BLK, values.shape[1])
 
 
-def project(r, tile):
-    part = r.q.shape[1]
-    blocks = QTILE // BLK
-    standardized, _ = norm_rows(wide(sorted_rows(r, r.hall, tile * blocks, blocks)))
-    normed = narrow(standardized * r.vec[0:1, :] + r.vec[1:2, :])
-    weight = r.wq4[...].reshape(-1, 3 * part)
-    projected = mm(normed, weight) + r.vec[5:6, : 3 * part]
-    turned = turn(
-        projected[:, : 2 * part], rope_lanes(r, tile * blocks, blocks, 2 * part, False)
-    )
-    place = pl.ds(pl.multiple_of(tile * QTILE, QTILE), QTILE)
-    r.q[place, :] = narrow(wide(narrow(turned[:, :part])) * HD**-0.5)
-    keys, values = turned[:, part:], projected[:, 2 * part :]
-    r.k[place, :] = narrow(keys)
-    r.v[place, :] = narrow(values)
-    r.kt[:, place] = narrow(keys.T)
-    r.vt[:, place] = narrow(values.T)
+def project(r, me, chip):
+    part = r.wqs.shape[1] // 3
+    sides = r.h.shape[0]
+
+    @pl.loop(0, 2)
+    def _(number):
+        first = (2 * chip + (me.k + number) % 2) * sides
+        rows = flat_rows(r.hall[pl.ds(first, sides)])
+        standardized, _ = norm_rows(wide(rows))
+        normed = narrow(standardized * r.vec[0:1, :] + r.vec[1:2, :])
+        weight = r.wq4[...].reshape(-1, 3 * part)
+        projected = mm(normed, weight) + r.vec[5:6, : 3 * part]
+        positions = [r.order[first + side] for side in range(sides)]
+        turned = turn(projected[:, : 2 * part], rope_lanes(r, positions, 2 * part, False))
+        keys, values = turned[:, part:], projected[:, 2 * part :]
+        query = narrow(wide(narrow(turned[:, :part])) * HD**-0.5)
+        for side in range(sides):
+            own = slice(side * BLK, (side + 1) * BLK)
+            r.q[first + side] = query[own]
+            r.k[first + side] = narrow(keys[own])
+            r.v[first + side] = narrow(values[own])
+            r.kt[first + side] = narrow(keys[own].T)
+            r.vt[first + side] = narrow(values[own].T)
+
+
+def sorted_columns(r, source, head, block, blocks):
+    lanes = slice(head * HD, (head + 1) * HD)
+    return jnp.concatenate(
+        [source[r.idx[block + number], lanes, :] for number in range(blocks)], axis=1
+    )
 
 
 def tile_start(r, me, tile):
-    quarter = r.k.shape[0] // 4
+    quarter = r.k.shape[0] * BLK // 4
     low = tile < quarter // QTILE
     inside = tile * QTILE - jnp.where(low, 0, quarter)
     return jnp.where(low, quarter * me.k, 3 * quarter - quarter * me.k) + inside
 
 
 def attend(r, me, tile):
-    part = r.k.shape[1]
+    part = r.k.shape[2]
+    blocks = QTILE // BLK
     heads = part // HD
     start = tile_start(r, me, tile)
     rows = slice(tile * QTILE, (tile + 1) * QTILE)
-    query = r.q[pl.ds(pl.multiple_of(start, QTILE), QTILE), :]
+    query = sorted_rows(r, r.q, start // BLK, blocks)
     per_head = [head_rows(query, head) for head in range(heads)]
 
     def visit(number, state, masked):
-        place = pl.ds(pl.multiple_of(number * QTILE, QTILE), QTILE)
-        keys = r.k[place, :]
+        keys = sorted_rows(r, r.k, number * blocks, blocks)
         result = []
         for head in range(heads):
             top, total, acc = state[head]
@@ -938,7 +978,7 @@
             fade = jnp.exp(top - new_top)
             probs = jnp.exp(logits - new_top)
             total = total * fade + jnp.sum(probs, axis=0, keepdims=True)
-            values = r.vt[head * HD : (head + 1) * HD, place]
+            values = sorted_columns(r, r.vt, head, number * blocks, blocks)
             acc = acc * fade + mm(values, narrow(probs))
             result.append((new_top, total, acc))
         return tuple(result)
@@ -1020,19 +1060,21 @@
 
 
 def attend_grad(r, me, tile):
-    part = r.k.shape[1]
+    part = r.k.shape[2]
     heads = part // HD
     kstep = 2 * QTILE
     start = tile_start(r, me, tile)
     rows = slice(tile * QTILE, (tile + 1) * QTILE)
-    query = r.q[pl.ds(pl.multiple_of(start, QTILE), QTILE), :]
+    blocks = kstep // BLK
+    query = sorted_rows(r, r.q, start // BLK, QTILE // BLK)
     d_out = r.datt[rows, :]
     queries = jnp.concatenate([head_rows(query, head) for head in range(heads)], axis=0)
     d_outs = jnp.concatenate([head_rows(d_out, head) for head in range(heads)], axis=0)
 
     def visit(number, state, masked):
         place = pl.ds(pl.multiple_of(number * kstep, kstep), kstep)
-        keys, values = r.k[place, :], r.v[place, :]
+        keys = sorted_rows(r, r.k, number * blocks, blocks)
+        values = sorted_rows(r, r.v, number * blocks, blocks)
         probs_all, d_logits_all, result = [], [], []
         for head in range(heads):
             own = slice(head * QTILE, (head + 1) * QTILE)
@@ -1046,7 +1088,8 @@
             d_logits = narrow(probs * (d_probs - r.delta[head : head + 1, rows]))
             probs_all.append(narrow(probs))
             d_logits_all.append(d_logits)
-            result.append(state[head] + mm(r.kt[head * HD : (head + 1) * HD, place], d_logits))
+            columns = sorted_columns(r, r.kt, head, number * blocks, blocks)
+            result.append(state[head] + mm(columns, d_logits))
         r.dv[place, :] += mm(jnp.concatenate(probs_all, axis=1), d_outs)
         r.dk[place, :] += mm(jnp.concatenate(d_logits_all, axis=1), queries)
         return tuple(result)
@@ -1060,7 +1103,7 @@
 
 def qkv_grad(r, me, tile):
     place = pl.ds(pl.multiple_of(tile * QTILE, QTILE), QTILE)
-    part = r.k.shape[1]
+    part = r.k.shape[2]
     blocks = QTILE // BLK
     start = tile_start(r, me, tile)
     block = start // BLK
@@ -1072,7 +1115,8 @@
     d_key = r.dk[held, :] + wide(r.kvin[place, :part])
     d_value = r.dv[held, :] + wide(r.kvin[place, part:])
     turned = turn(
-        jnp.concatenate([d_query, d_key], axis=1), rope_lanes(r, block, blocks, 2 * part, True)
+        jnp.concatenate([d_query, d_key], axis=1),
+        rope_lanes(r, [block + n for n in range(blocks)], 2 * part, True),
     )
     d_qkv = jnp.concatenate([turned, d_value], axis=1)
     d_qkv16 = narrow(d_qkv)
@@ -1085,12 +1129,33 @@
     put_blocks(r.outb, tile, narrow(d_normed * gain1 + r.e2[place, :]))
 
 
+def gather_sums(r, me):
+    nz, part = me.nz, r.vec.shape[1] // me.nz
+    r.sums[4:5, :] = jnp.sum(wide(flat_rows(r.g[...])), axis=0, keepdims=True)
+
+    def put(z, number, values):
+        r.vout[z, 0:1, number * part : (number + 1) * part] = values
+
+    for z in range(nz):
+        for row in range(5):
+            put(z, row, r.sums[row : row + 1, z * part : (z + 1) * part])
+    for chip in range(nz):
+
+        @pl.when(me.t == chip)
+        def _():
+            for number in range(3):
+                held = number * nz + chip
+                put(held // 3, 5 + held % 3, r.sums[5:6, number * part : (number + 1) * part])
+            for z in range(nz):
+                put(z, 8 + chip, r.sums[6:7, z * part : (z + 1) * part])
+
+
 class Scatter:
     def __init__(self, copies, me, r, source, sent, got, landed):
         self.me, self.r, self.source, self.sent, self.got, self.landed = me, r, source, sent, got, landed
         self.chips = me.nz
         self.sides = sent.shape[0] // self.chips
-        self.first = r.k.shape[0] // BLK
+        self.first = r.k.shape[0]
         self.exchanges = [
             copies.make(self.piece(sent, chip), self.piece(got, chip), me.on_plane(me.pn))
             for chip in range(self.chips)
@@ -1177,7 +1242,7 @@
     own_rows = pl.ds(me.c * sides, sides)
     h_share = PlaneShare(copies, me, r.h, row_slot(r.hall), sides)
     g_share = PlaneShare(copies, me, r.g, row_slot(r.gall), sides)
-    wq = LineGather(copies, me, r.wqs, r.wq4)
+    wq = LineSend(copies, me, r.wqs, r.wq4)
     wu = LineGather(copies, me, r.wus, r.wu4)
     wd = LineGather(copies, me, r.wdown.at[pl.ds(me.t * shard, shard)], r.wd4)
     wo = LineSpread(copies, me, r.wout, r.wo1)
@@ -1188,6 +1253,7 @@
     for copy in small:
         copy.start()
     wu.start()
+    wd.start()
     own_down = pltpu.make_async_copy(
         r.wdown.at[pl.ds(me.t * shard, shard)], r.wd4.at[me.z], r.local_sem
     )
@@ -1202,47 +1268,40 @@
     r.vout[...] = jnp.zeros_like(r.vout)
     r.dk[...] = jnp.zeros_like(r.dk)
     r.dv[...] = jnp.zeros_like(r.dv)
-    wq.advance(0)
     h_share.relay()
-    wu.advance(0)
-    wq.advance(1)
-    wd.start()
     h_share.swap()
     g_share.start()
+    wq.advance()
     for copy in small:
         copy.wait_recv()
     read_vectors(r, me)
-    wq.advance(2)
+    wq.finish()
+    h_share.to_p.wait_recv()
+    project(r, me, me.t)
+    wu.advance(0)
+    h_share.swaps[0].wait_recv()
+    h_share.on_diagonal()
+    project(r, me, me.tx)
+    wd.advance(0)
+    h_share.swaps[1].wait_recv()
+    project(r, me, me.ty)
+    g_share.relay()
     wu.advance(1)
-    h_share.on_diagonal()
-    wq.finish()
-    h_share.finish()
-
-    count = r.k.shape[0] // QTILE
-    for first in (0, count // 2):
-
-        @pl.loop(first, first + count // 2)
-        def _(tile):
-            project(r, tile)
-
-        if first == 0:
-            wd.advance(0)
-
+    h_share.swaps[2].wait_recv()
+    project(r, me, me.td)
+    attend(r, me, 1)
+    wd.advance(1)
+    g_share.swap()
+    attend(r, me, 2)
     wu.advance(2)
-    wd.advance(1)
+    g_share.on_diagonal()
     attend(r, me, 0)
-    g_share.relay()
-    attend(r, me, 1)
     wd.advance(2)
     wo.start()
-    g_share.swap()
-    attend(r, me, 2)
-    g_share.on_diagonal()
     own_down.wait()
     wu.finish()
     wd.finish()
     g_share.finish()
-    copies.settle([g_share.hop_x, g_share.hop_y, *g_share.swaps])
 
     @pl.loop(0, tiles)
     def _(tile):
@@ -1269,10 +1328,10 @@
     down_reduce.start()
     weight_grad(r.gu, r.n, r.du)
     up_reduce.start()
+    wo.advance()
     down_reduce.pair()
-    wo.advance()
+    attend(r, me, 3)
     up_reduce.pair()
-    attend(r, me, 3)
     wo.finish()
 
     @pl.loop(0, tiles)
@@ -1283,17 +1342,18 @@
     r.go[...] = narrow(mm(r.att[...], r.gl[...], TN))
     out_reduce.start()
     attend_grad(r, me, 0)
+    out_reduce.pair()
     out_scatter.spread()
-    out_reduce.pair()
+    attend_grad(r, me, 3)
+    out_scatter.middle()
     attend_grad(r, me, 1)
-    attend_grad(r, me, 2)
     down_reduce.collect()
     share_down()
-    out_scatter.middle()
-    attend_grad(r, me, 3)
-
-    part = r.k.shape[1]
-    quarter = r.k.shape[0] // 4
+    copies.settle([g_share.hop_x, g_share.hop_y, *g_share.swaps])
+    attend_grad(r, me, 2)
+
+    part = r.k.shape[2]
+    quarter = r.k.shape[0] * BLK // 4
     kv_moves = []
     for number in range(2):
         first = quarter * (1 - me.k) if number == 0 else 3 * quarter - quarter * (1 - me.k)
@@ -1307,57 +1367,35 @@
     d_share.relay()
     up_reduce.collect()
     share_up()
+    for copy in kv_moves:
+        copy.wait_recv()
+
+    @pl.loop(0, tiles)
+    def _(tile):
+        qkv_grad(r, me, tile)
+
+    e_scatter = Scatter(
+        copies, me, r, r.outb, r.gall.at[: r.outb.shape[0]], r.gall.at[r.outb.shape[0] :], r.eland
+    )
+    e_scatter.start()
+    u_share.relay()
     d_share.swap()
     out_reduce.collect()
     o_spread.start()
-    for copy in kv_moves:
-        copy.wait_recv()
-
-    @pl.loop(0, tiles)
-    def _(tile):
-        qkv_grad(r, me, tile)
-
-    e_scatter = Scatter(
-        copies, me, r, r.outb, r.gall.at[: r.outb.shape[0]], r.gall.at[r.outb.shape[0] :], r.eland
-    )
-    e_scatter.start()
-    u_share.relay()
+    gather_sums(r, me)
+    vec_line = [
+        copies.make(r.vout.at[other], r.vline.at[me.z], me.on_line(other)) for other in me.others
+    ]
+    for copy in vec_line:
+        copy.start()
     weight_grad(r.gq, r.n, r.du.at[:, : 3 * part])
     qkv_reduce = LineReduce(copies, me, r.gq, r.tq, r.uq)
     qkv_reduce.start()
     e_scatter.spread()
     qkv_reduce.pair()
+    d_share.on_diagonal()
     u_share.swap()
     o_spread.advance()
-
-    vec_part = r.vec.shape[1] // nz
-    r.sums[4:5, :] = jnp.sum(wide(flat_rows(r.g[...])), axis=0, keepdims=True)
-    for z in range(nz):
-        span = slice(z * vec_part, (z + 1) * vec_part)
-        for row in range(4):
-            r.vout[z, 0:1, row * vec_part : (row + 1) * vec_part] = r.sums[row : row + 1, span]
-        r.vout[z, 1:2, :vec_part] = r.sums[4:5, span]
-    for chip in range(nz):
-
-        @pl.when(me.t == chip)
-        def _():
-            for piece in range(3):
-                number = piece * nz + chip
-                first = number % 3 * vec_part
-                r.vout[number // 3, 2:3, first : first + vec_part] = r.sums[
-                    5:6, piece * vec_part : (piece + 1) * vec_part
-                ]
-            for z in range(nz):
-                r.vout[z, 3:4, chip * vec_part : (chip + 1) * vec_part] = r.sums[
-                    6:7, z * vec_part : (z + 1) * vec_part
-                ]
-
-    vec_line = [
-        copies.make(r.vout.at[other], r.vline.at[me.z], me.on_line(other)) for other in me.others
-    ]
-    for copy in vec_line:
-        copy.start()
-    d_share.on_diagonal()
     for copy in vec_line:
         copy.wait_recv()
     vector = r.vout[me.z]
@@ -1378,13 +1416,13 @@
     residual = wide(flat_rows(r.h[...]))
     own_standardized, own_deviation = norm_rows(residual)
     r.hidden_out[...] = narrow(residual + r.vec[4:5, :] + out_scatter.total())
-    q_share.relay()
     e_total = e_scatter.total()
     r.hidden_grad[...] = wide(flat_rows(r.g[...])) + own_deviation * (
         e_total
         - jnp.mean(e_total, axis=-1, keepdims=True)
         - own_standardized * jnp.mean(e_total * own_standardized, axis=-1, keepdims=True)
     )
+    q_share.relay()
     q_share.swap()
     for copy in vec_plane:
         copy.wait_recv()
@@ -1393,10 +1431,8 @@
         vector = vector + r.vplane[peer]
     r.vsum[...] = vector
     q_share.on_diagonal()
-    d_share.finish()
-    u_share.finish()
-    o_spread.finish()
-    q_share.finish()
+    for share in (d_share, u_share, o_spread, q_share):
+        share.finish()
     copies.finish()
 
 
@@ -1420,10 +1456,13 @@
 
     @pl.when(pl.program_id(0) == 0)
     def _():
-        places = [(0, n) for n in range(4)] + [(1, 0), (1, 0), (2, 0), (3, 0)]
-        for target, (row, number) in zip(vector_refs, places):
+        first = 0
+        for number, target in enumerate(vector_refs):
             count = target.shape[0]
-            target[...] = vsum_ref[row : row + 1, number * count : (number + 1) * count].reshape(count)
+            if number == 5:
+                first -= count
+            target[...] = vsum_ref[0:1, first : first + count].reshape(count)
+            first += count
 
 
 def rotary_parts(block_count):
@@ -1476,6 +1515,7 @@
     everyone = 2 * rows
     sides = local_rows // BLK
 
+    sums = 5 * shard + qkv_bias.shape[0] + up_bias.shape[0]
     small = 6 * shard + qkv_bias.shape[0] + up_bias.shape[0]
     rope_r, rope_b = rotary_parts(everyone // BLK)
 
@@ -1495,7 +1535,7 @@
             )
         ),
         "rope_r": jnp.asarray(rope_r),
-        "rope_b": jnp.asarray(rope_b),
+        "rope_b": jnp.asarray(rope_b[:, None, :]),
     }
     outputs = {
         "hidden_out": ((local_rows, width), b16),
@@ -1504,7 +1544,7 @@
         "fu": ((2, chips, half, hidden), b16),
         "fd": ((2, chips, half, width), b16),
         "fo": ((2, half, width), b16),
-        "vsum": ((8, width), f32),
+        "vsum": ((1, sums), f32),
     }
     scratch = {
         "hall": ((everyone // BLK, BLK, width), b16),
@@ -1519,11 +1559,11 @@
         "sm4": ((nz, 1, small), f32),
         "vec": ((8, width), f32),
         "sums": ((8, width), f32),
-        "q": ((everyone, part), b16),
-        "k": ((everyone, part), b16),
-        "v": ((everyone, part), b16),
-        "kt": ((part, everyone), b16),
-        "vt": ((part, everyone), b16),
+        "q": ((everyone // BLK, BLK, part), b16),
+        "k": ((everyone // BLK, BLK, part), b16),
+        "v": ((everyone // BLK, BLK, part), b16),
+        "kt": ((everyone // BLK, part, BLK), b16),
+        "vt": ((everyone // BLK, part, BLK), b16),
         "att": ((rows, part), b16),
         "attt": ((part, rows), b16),
         "lse": ((8, rows), f32),
@@ -1555,10 +1595,10 @@
         "ud": ((nz, half, width), b16),
         "to": ((half, width), b16),
         "uo": ((nz, half, width), b16),
-        "vout": ((nz, 8, width), f32),
-        "vline": ((nz, 8, width), f32),
-        "vsend": ((8, width), f32),
-        "vplane": ((2 * chips, 8, width), f32),
+        "vout": ((nz, 1, sums), f32),
+        "vline": ((nz, 1, sums), f32),
+        "vsend": ((1, sums), f32),
+        "vplane": ((2 * chips, 1, sums), f32),
     }
     names = [*inputs, *outputs, *scratch, "idx", "send_sems", "recv_sems", "local_sem"]
     results = pl.pallas_call(
@@ -1610,7 +1650,7 @@
             pl.BlockSpec((1, some, width), lambda i: (i // inner, i % inner, 0)),
             lines(few, width),
             lines(few, width),
-            pl.BlockSpec((8, width), lambda i: (0, 0)),
+            pl.BlockSpec((1, sums), lambda i: (0, 0)),
         ],
         out_specs=(
             lines(some, qkv_weight.shape[1]),

time: 133 us -> 123 us (0.925); the launches traced: 132 us -> 121 us
  Pallas kernels: 132 us -> 120 us
    pallas_call x1, Pallas kernels: 125 us -> 114 us  [sliced_layer(): pl.pallas_call(functools.partial(layer_kernel, nz, names), out_shape=tupl...]
where the time goes in v4:
time: 123 us; the launch traced here: 121 us
  Pallas kernels  120 us (98%)
    pallas_call x1, Pallas kernels, sliced_layer(): pl.pallas_call(functools.partial(layer_kernel, nz, names), out_shape=tupl...  114 us
    pallas_call x1, Pallas kernels, sliced_layer(): pl.pallas_call(assemble_kernel, grid=(steps,), out_shape=(jax.ShapeDtypeS...  6.37 us

profile of v4, /device:TPU:1, one launch (start us, length us, event | category | flops | bytes accessed | tf_op | source)
XLA Modules:
  0.0 121.0 jit_solution(5582880122919876879)
XLA Ops:
  0.7 113.7 %layer.1 = (bf16[256,768]{1,0:T(8,128)(2,1)}, f32[256,768]{1,0:T(8,128)}, bf16[2,4,96,576]{3,2,1,0:T(8,128)(2,1)}, bf16[2,4,96,768]{3,2,1,0:T(8,128)(2,1)}, bf16...) custom-call(s32[16]{0:T(128)} %refs_0_.1, bf16[2,128,768]{2,1,0:T(8,128)(2,1)} %bitcast.5, ...), custom_call_target="tpu_custom_call" | custom-call | tf_op jit(solution)/shard_map/layer/pallas_call | solution.py:1604
  114.4 6.4 %assemble.1 = (f32[192,2304]{1,0:T(8,128)}, f32[192,3072]{1,0:T(8,128)}, f32[4,4,48,768]{3,2,1,0:T(8,128)}, f32[192,768]{1,0:T(8,128)}, bf16[256,768]{1,0:T(8,12...) custom-call(bf16[2,4,96,576]{3,2,1,0:T(8,128)(2,1)} %get-tuple-eleme, ...), custom_call_target="tpu_custom_call" | custom-call | tf_op jit(solution)/shard_map/assemble/pallas_call | solution.py:1634

commit v5 on v4

--- a/solution.py
+++ b/solution.py
@@ -431,7 +431,7 @@
 NT = (((1,), (1,)), ((), ()))
 TN = (((0,), (0,)), ((), ()))
 QTILE = 256
-SEMAPHORES = 160
+SEMAPHORES = 192
 
 
 def mm(left, right, dims=NN):
@@ -640,8 +640,9 @@
 
 
 class LineSpread:
-    def __init__(self, copies, me, source, target):
-        self.me, self.source, self.target = me, source, target
+    def __init__(self, copies, me, source, target, sem):
+        self.me = me
+        self.keep = pltpu.make_async_copy(source, target, sem)
         rows = target.shape[0] // 2
         mine = pl.ds(me.k * rows, rows)
         self.here, self.away = me.z == me.t, me.z != me.t
@@ -659,7 +660,7 @@
         def _():
             for copy in self.sends:
                 copy.start()
-            self.target[...] = self.source[...]
+            self.keep.start()
 
     def advance(self):
         for copy, arrives in zip(self.sends, self.arrivals):
@@ -667,6 +668,7 @@
         pl.when(self.away)(self.swap.start)
 
     def finish(self):
+        pl.when(self.here)(self.keep.wait)
         pl.when(self.away)(self.swap.wait_recv)
 
 
@@ -737,8 +739,9 @@
 
 
 class PlaneSpread:
-    def __init__(self, copies, me, source, target, rows):
-        self.me, self.source, self.target = me, source, target
+    def __init__(self, copies, me, source, target, rows, sem):
+        self.me = me
+        self.keep = pltpu.make_async_copy(source, target.at[me.k], sem)
         top, bottom = pl.ds(0, rows // 2), pl.ds(rows // 2, rows // 2)
         place = target.at[me.k]
         self.here, self.from_x, self.from_y = me.t == me.z, me.tx == me.z, me.ty == me.z
@@ -760,7 +763,7 @@
             self.to_x.start()
             self.to_y.start()
             self.to_p.start()
-            self.target[self.me.k] = self.source[...]
+            self.keep.start()
 
     def advance(self):
         @pl.when(self.from_x)
@@ -783,6 +786,7 @@
             self.swap.start()
 
     def finish(self):
+        pl.when(self.here)(self.keep.wait)
         self.to_p.wait_recv()
 
 def norm_rows(values_in):
@@ -828,17 +832,38 @@
     )
 
 
+def windows(r, me):
+    part = r.wqs.shape[1] // 3
+    chips, columns = me.nz, r.win.shape[2]
+    copies = []
+    for source, pieces in ((r.wqkv, 3), (r.wup, r.wus.shape[1] // part)):
+        for piece in range(pieces):
+            first = (piece * chips + me.t) * part // 128 * 128
+            number = len(copies)
+            copies.append(
+                pltpu.make_async_copy(
+                    source.at[:, pl.ds(pl.multiple_of(first, 128), columns)],
+                    r.win.at[number],
+                    r.window_sems.at[number],
+                )
+            )
+    return copies
+
+
 def slice_weights(r, me):
     part = r.wqs.shape[1] // 3
-    chips = r.wqkv.shape[1] // r.wqs.shape[1]
-    for chip in range(chips):
+    for chip in range(me.nz):
 
         @pl.when(me.t == chip)
         def _():
-            for source, target in ((r.wqkv, r.wqs), (r.wup, r.wus)):
+            first = chip * part % 128
+            number = 0
+            for target in (r.wqs, r.wus):
                 for piece in range(target.shape[1] // part):
-                    first = (piece * chips + chip) * part
-                    target[:, piece * part : (piece + 1) * part] = source[:, first : first + part]
+                    target[:, piece * part : (piece + 1) * part] = r.win[
+                        number, :, first : first + part
+                    ]
+                    number += 1
 
 
 VECTORS = ("gain1", "shift1", "gain2", "shift2", "bout", "bdown", "bqkv", "bup")
@@ -887,13 +912,14 @@
             found = jnp.where(held[number] == position, number, found)
         r.idx[position] = found
     for chip in range(chips):
-        for owner, first in ((me.k, count), (1 - me.k, count + chips * sides)):
+        for holder, first in ((me.k, count), (1 - me.k, count + chips * sides)):
             for side in range(sides):
-                position = r.order[(2 * chip + owner) * sides + side]
-                low = (position >= quarter * me.k) & (position < quarter * (me.k + 1))
-                high = position - 2 * quarter + quarter * me.k
-                r.idx[first + chip * sides + side] = jnp.where(
-                    low, position - quarter * me.k, jnp.clip(high, 0, 2 * quarter - 1)
+                position = r.order[(2 * chip + me.k) * sides + side]
+                low = (position >= quarter * holder) & (position < quarter * (holder + 1))
+                near = position - quarter * holder
+                high = position - 2 * quarter + quarter * holder
+                r.idx[first + chip * sides + side] = jnp.clip(
+                    jnp.where(low, near, high), 0, 2 * quarter - 1
                 )
         position = r.order[(2 * chip + me.k) * sides]
         outer = jnp.where((position < quarter) | (position >= 3 * quarter), 0, 1)
@@ -916,29 +942,35 @@
     target[pl.ds(tile * blocks, blocks)] = values.reshape(blocks, BLK, values.shape[1])
 
 
-def project(r, me, chip):
+def prepare(r, chip, target, at):
+    sides = r.h.shape[0]
+    rows = sides * BLK
+
+    @pl.loop(0, 2)
+    def _(core):
+        values = flat_rows(r.hall[pl.ds((2 * chip + core) * sides, sides)])
+        standardized, _ = norm_rows(wide(values))
+        place = pl.ds(pl.multiple_of(at + core * rows, rows), rows)
+        target[place, :] = narrow(standardized * r.vec[0:1, :] + r.vec[1:2, :])
+
+
+def project(r, chip, source, at):
     part = r.wqs.shape[1] // 3
-    sides = r.h.shape[0]
-
-    @pl.loop(0, 2)
-    def _(number):
-        first = (2 * chip + (me.k + number) % 2) * sides
-        rows = flat_rows(r.hall[pl.ds(first, sides)])
-        standardized, _ = norm_rows(wide(rows))
-        normed = narrow(standardized * r.vec[0:1, :] + r.vec[1:2, :])
-        weight = r.wq4[...].reshape(-1, 3 * part)
-        projected = mm(normed, weight) + r.vec[5:6, : 3 * part]
-        positions = [r.order[first + side] for side in range(sides)]
-        turned = turn(projected[:, : 2 * part], rope_lanes(r, positions, 2 * part, False))
-        keys, values = turned[:, part:], projected[:, 2 * part :]
-        query = narrow(wide(narrow(turned[:, :part])) * HD**-0.5)
-        for side in range(sides):
-            own = slice(side * BLK, (side + 1) * BLK)
-            r.q[first + side] = query[own]
-            r.k[first + side] = narrow(keys[own])
-            r.v[first + side] = narrow(values[own])
-            r.kt[first + side] = narrow(keys[own].T)
-            r.vt[first + side] = narrow(values[own].T)
+    blocks = 2 * r.h.shape[0]
+    first = chip * blocks
+    weight = r.wq4[...].reshape(-1, 3 * part)
+    projected = mm(source[at : at + blocks * BLK, :], weight) + r.vec[5:6, : 3 * part]
+    positions = [r.order[first + number] for number in range(blocks)]
+    turned = turn(projected[:, : 2 * part], rope_lanes(r, positions, 2 * part, False))
+    keys, values = turned[:, part:], projected[:, 2 * part :]
+    query = narrow(wide(narrow(turned[:, :part])) * HD**-0.5)
+    for number in range(blocks):
+        own = slice(number * BLK, (number + 1) * BLK)
+        r.q[first + number] = query[own]
+        r.k[first + number] = narrow(keys[own])
+        r.v[first + number] = narrow(values[own])
+        r.kt[first + number] = narrow(keys[own].T)
+        r.vt[first + number] = narrow(values[own].T)
 
 
 def sorted_columns(r, source, head, block, blocks):
@@ -1131,7 +1163,7 @@
 
 def gather_sums(r, me):
     nz, part = me.nz, r.vec.shape[1] // me.nz
-    r.sums[4:5, :] = jnp.sum(wide(flat_rows(r.g[...])), axis=0, keepdims=True)
+    r.sums[4:5, :] = jnp.sum(wide(flat_rows(r.gown[...])), axis=0, keepdims=True)
 
     def put(z, number, values):
         r.vout[z, 0:1, number * part : (number + 1) * part] = values
@@ -1151,14 +1183,16 @@
 
 
 class Scatter:
-    def __init__(self, copies, me, r, source, sent, got, landed):
-        self.me, self.r, self.source, self.sent, self.got, self.landed = me, r, source, sent, got, landed
+    def __init__(self, copies, me, r, source, theirs, got, landed):
+        self.me, self.r, self.source, self.theirs, self.got, self.landed = me, r, source, theirs, got, landed
         self.chips = me.nz
-        self.sides = sent.shape[0] // self.chips
+        self.sides = got.shape[0] // self.chips
         self.first = r.k.shape[0]
+        self.tiles = source.shape[0] * BLK // QTILE
+        self.number = copies.count
+        self.send_sems, self.recv_sems = copies.send_sems, copies.recv_sems
         self.exchanges = [
-            copies.make(self.piece(sent, chip), self.piece(got, chip), me.on_plane(me.pn))
-            for chip in range(self.chips)
+            copies.make(*self.rows(tile), me.on_plane(me.pn)) for tile in range(self.tiles)
         ]
         self.steps = []
         for side, near, far, to_near, to_far in (
@@ -1178,18 +1212,21 @@
     def place(self, chip, side):
         return chip * self.sides + side
 
-    def piece(self, array, chip):
-        return array.at[pl.ds(chip * self.sides, self.sides)]
-
-    def block(self, number):
-        return self.source[self.r.idx[self.first + number]]
-
-    def start(self):
-        count = self.chips * self.sides
-        for number in range(count):
-            self.sent[number] = self.block(count + number)
-        for exchange in self.exchanges:
-            exchange.start()
+    def rows(self, tile):
+        blocks = QTILE // BLK
+        place = pl.ds(tile * blocks, blocks)
+        return self.source.at[place], self.theirs.at[place]
+
+    def exchange(self, tile):
+        source, target = self.rows(tile)
+        pltpu.make_async_remote_copy(
+            src_ref=source,
+            dst_ref=target,
+            send_sem=self.send_sems.at[self.number + tile],
+            recv_sem=self.recv_sems.at[self.number + tile],
+            device_id=self.me.on_plane(self.me.pn),
+            device_id_type=MESH_IDS,
+        ).start()
 
     def spread(self):
         count = self.chips * self.sides
@@ -1197,7 +1234,8 @@
             exchange.wait_recv()
         for number in range(count):
             flag = self.r.idx[self.first + 2 * count + number // self.sides]
-            own, other = wide(self.block(number)), wide(self.got[number])
+            own = wide(self.source[self.r.idx[self.first + number]])
+            other = wide(self.theirs[self.r.idx[self.first + count + number]])
             here = jnp.full(own.shape, flag, jnp.int32) > 0
             self.got[number] = narrow(jnp.where(here, own, other))
         for far, _, _, _ in self.steps:
@@ -1232,63 +1270,80 @@
     shard = r.wqs.shape[0]
     tiles = r.att.shape[0] // QTILE
 
-    slice_weights(r, me)
+    kept = []
+
+    def keep(source, target):
+        copy = pltpu.make_async_copy(source, target, r.local_sems.at[len(kept)])
+        copy.start()
+        kept.append(copy)
+        return copy
+
+    own_rows = pl.ds(me.c * sides, sides)
+    loads = windows(r, me)
+    for copy in loads:
+        copy.start()
+    h_own = keep(r.h, r.hall.at[own_rows])
+    keep(r.g, r.gall.at[own_rows])
+    keep(r.g, r.gown)
+    own_down = keep(r.wdown.at[pl.ds(me.t * shard, shard)], r.wd4.at[me.z])
     pack_vectors(r)
     me.greet()
 
     def row_slot(array):
         return lambda core, chip: array.at[pl.ds((2 * chip + core) * sides, sides)]
 
-    own_rows = pl.ds(me.c * sides, sides)
     h_share = PlaneShare(copies, me, r.h, row_slot(r.hall), sides)
     g_share = PlaneShare(copies, me, r.g, row_slot(r.gall), sides)
     wq = LineSend(copies, me, r.wqs, r.wq4)
     wu = LineGather(copies, me, r.wus, r.wu4)
     wd = LineGather(copies, me, r.wdown.at[pl.ds(me.t * shard, shard)], r.wd4)
-    wo = LineSpread(copies, me, r.wout, r.wo1)
+    wo = LineSpread(copies, me, r.wout, r.wo1, r.window_sems.at[len(loads)])
     small = [copies.make(r.sm, r.sm4.at[me.z], me.on_line(other)) for other in me.others]
 
-    h_share.start()
-    wq.start()
     for copy in small:
         copy.start()
+    h_share.start()
+    for copy in loads:
+        copy.wait()
+    slice_weights(r, me)
+    r.wq4[me.z] = r.wqs[...]
+    r.wu4[me.z] = r.wus[...]
+    wq.start()
     wu.start()
     wd.start()
-    own_down = pltpu.make_async_copy(
-        r.wdown.at[pl.ds(me.t * shard, shard)], r.wd4.at[me.z], r.local_sem
-    )
-    own_down.start()
-    r.hall[own_rows] = r.h[...]
-    r.gall[own_rows] = r.g[...]
-    r.wq4[me.z] = r.wqs[...]
-    r.wu4[me.z] = r.wus[...]
     r.sm4[me.z] = r.sm[...]
     block_table(r, me)
     r.sums[...] = jnp.zeros_like(r.sums)
     r.vout[...] = jnp.zeros_like(r.vout)
     r.dk[...] = jnp.zeros_like(r.dk)
     r.dv[...] = jnp.zeros_like(r.dv)
+    for copy in small:
+        copy.wait_recv()
+    read_vectors(r, me)
+    h_own.wait()
+    h_share.to_p.wait_recv()
+    pair = 2 * sides * BLK
+    prepare(r, me.t, r.n, 0)
     h_share.relay()
     h_share.swap()
     g_share.start()
+    h_share.swaps[0].wait_recv()
+    prepare(r, me.tx, r.n, pair)
+    h_share.swaps[1].wait_recv()
     wq.advance()
-    for copy in small:
-        copy.wait_recv()
-    read_vectors(r, me)
+    prepare(r, me.ty, r.gl, 0)
     wq.finish()
-    h_share.to_p.wait_recv()
-    project(r, me, me.t)
+    project(r, me.t, r.n, 0)
     wu.advance(0)
-    h_share.swaps[0].wait_recv()
     h_share.on_diagonal()
-    project(r, me, me.tx)
+    project(r, me.tx, r.n, pair)
     wd.advance(0)
-    h_share.swaps[1].wait_recv()
-    project(r, me, me.ty)
+    project(r, me.ty, r.gl, 0)
     g_share.relay()
     wu.advance(1)
     h_share.swaps[2].wait_recv()
-    project(r, me, me.td)
+    prepare(r, me.td, r.gl, pair)
+    project(r, me.td, r.gl, pair)
     attend(r, me, 1)
     wd.advance(1)
     g_share.swap()
@@ -1298,7 +1353,9 @@
     attend(r, me, 0)
     wd.advance(2)
     wo.start()
-    own_down.wait()
+    for copy in kept[1:]:
+        copy.wait()
+    settled = len(kept)
     wu.finish()
     wd.finish()
     g_share.finish()
@@ -1308,21 +1365,21 @@
         feed_forward(r, me, tile)
 
     half = shard // 2
-    out_scatter = Scatter(copies, me, r, r.outb, r.osent, r.ogot, r.oland)
+    out_scatter = Scatter(copies, me, r, r.outb, r.otheirs, r.ogot, r.oland)
     up_reduce = LineReduce(copies, me, r.gu, r.tu, r.uu)
     down_reduce = LineReduce(copies, me, r.gd, r.td, r.ud)
     out_reduce = LineCollect(copies, me, r.go, r.to, r.uo)
     d_share = PlaneShare(copies, me, r.td.at[me.z], lambda core, chip: r.fd.at[core, chip], half)
     u_share = PlaneShare(copies, me, r.tu.at[me.z], lambda core, chip: r.fu.at[core, chip], half)
-    o_spread = PlaneSpread(copies, me, r.to, r.fo, half)
+    o_spread = PlaneSpread(copies, me, r.to, r.fo, half, r.window_sems.at[len(loads) + 1])
 
     def share_down():
         d_share.start()
-        r.fd[me.k, me.t] = r.td[me.z]
+        keep(r.td.at[me.z], r.fd.at[me.k, me.t])
 
     def share_up():
         u_share.start()
-        r.fu[me.k, me.t] = r.tu[me.z]
+        keep(r.tu.at[me.z], r.fu.at[me.k, me.t])
 
     weight_grad(r.gd, r.act, r.gl)
     down_reduce.start()
@@ -1337,8 +1394,9 @@
     @pl.loop(0, tiles)
     def _(tile):
         out_project(r, me, tile)
-
-    out_scatter.start()
+        pl.when(tile > 0)(functools.partial(out_scatter.exchange, tile - 1))
+
+    out_scatter.exchange(tiles - 1)
     r.go[...] = narrow(mm(r.att[...], r.gl[...], TN))
     out_reduce.start()
     attend_grad(r, me, 0)
@@ -1346,16 +1404,16 @@
     out_scatter.spread()
     attend_grad(r, me, 3)
     out_scatter.middle()
-    attend_grad(r, me, 1)
+    attend_grad(r, me, 2)
     down_reduce.collect()
     share_down()
     copies.settle([g_share.hop_x, g_share.hop_y, *g_share.swaps])
-    attend_grad(r, me, 2)
+    copies.settle(out_scatter.exchanges)
 
     part = r.k.shape[2]
     quarter = r.k.shape[0] * BLK // 4
-    kv_moves = []
-    for number in range(2):
+
+    def send_keys(number):
         first = quarter * (1 - me.k) if number == 0 else 3 * quarter - quarter * (1 - me.k)
         theirs = pl.ds(pl.multiple_of(first, quarter), quarter)
         rows = slice(number * quarter, (number + 1) * quarter)
@@ -1363,76 +1421,89 @@
         r.act[rows, part : 2 * part] = narrow(r.dv[theirs, :])
         copy = copies.make(r.act.at[rows, : 2 * part], r.kvin.at[rows], me.on_plane(me.pn))
         copy.start()
-        kv_moves.append(copy)
+        return copy
+
+    later = send_keys(1)
+    attend_grad(r, me, 1)
+    sooner = send_keys(0)
     d_share.relay()
+    later.wait_recv()
+    e_scatter = Scatter(
+        copies, me, r, r.outb, r.gall.at[: r.outb.shape[0]], r.gall.at[r.outb.shape[0] :], r.eland
+    )
+
+    @pl.loop(0, tiles)
+    def _(number):
+        pl.when(number == tiles // 2)(sooner.wait_recv)
+        qkv_grad(r, me, (number + tiles // 2) % tiles)
+        pl.when(number > 0)(
+            functools.partial(e_scatter.exchange, (number + tiles // 2 - 1) % tiles)
+        )
+
     up_reduce.collect()
     share_up()
-    for copy in kv_moves:
-        copy.wait_recv()
-
-    @pl.loop(0, tiles)
-    def _(tile):
-        qkv_grad(r, me, tile)
-
-    e_scatter = Scatter(
-        copies, me, r, r.outb, r.gall.at[: r.outb.shape[0]], r.gall.at[r.outb.shape[0] :], r.eland
-    )
-    e_scatter.start()
-    u_share.relay()
-    d_share.swap()
-    out_reduce.collect()
-    o_spread.start()
     gather_sums(r, me)
+    e_scatter.exchange(tiles // 2 - 1)
     vec_line = [
         copies.make(r.vout.at[other], r.vline.at[me.z], me.on_line(other)) for other in me.others
     ]
     for copy in vec_line:
         copy.start()
+    d_share.swap()
     weight_grad(r.gq, r.n, r.du.at[:, : 3 * part])
     qkv_reduce = LineReduce(copies, me, r.gq, r.tq, r.uq)
     qkv_reduce.start()
     e_scatter.spread()
     qkv_reduce.pair()
+    u_share.relay()
+    out_reduce.collect()
+    o_spread.start()
     d_share.on_diagonal()
     u_share.swap()
-    o_spread.advance()
+    e_scatter.middle()
     for copy in vec_line:
         copy.wait_recv()
     vector = r.vout[me.z]
     for other in me.others:
         vector = vector + r.vline[other]
     r.vsend[...] = vector
-    e_scatter.middle()
     vec_plane = [copies.make(r.vsend, r.vplane.at[me.c], me.on_plane(peer)) for peer in me.plane]
     for copy in vec_plane:
         copy.start()
-    u_share.on_diagonal()
-    o_spread.on_diagonal()
     qkv_reduce.collect()
     q_share = PlaneShare(copies, me, r.tq.at[me.z], lambda core, chip: r.fq.at[core, chip], half)
     q_share.start()
-    r.fq[me.k, me.t] = r.tq[me.z]
-
-    residual = wide(flat_rows(r.h[...]))
+    keep(r.tq.at[me.z], r.fq.at[me.k, me.t])
+
+    residual = wide(flat_rows(r.hall[own_rows]))
     own_standardized, own_deviation = norm_rows(residual)
-    r.hidden_out[...] = narrow(residual + r.vec[4:5, :] + out_scatter.total())
+    rows = sides * BLK
+    r.n[:rows, :] = narrow(residual + r.vec[4:5, :] + out_scatter.total())
+    keep(r.n.at[:rows], r.hidden_out)
+    o_spread.advance()
+    u_share.on_diagonal()
+    q_share.relay()
     e_total = e_scatter.total()
-    r.hidden_grad[...] = wide(flat_rows(r.g[...])) + own_deviation * (
+    r.e2[:rows, :] = wide(flat_rows(r.gown[...])) + own_deviation * (
         e_total
         - jnp.mean(e_total, axis=-1, keepdims=True)
         - own_standardized * jnp.mean(e_total * own_standardized, axis=-1, keepdims=True)
     )
-    q_share.relay()
+    keep(r.e2.at[:rows], r.hidden_grad)
     q_share.swap()
+    o_spread.on_diagonal()
     for copy in vec_plane:
         copy.wait_recv()
     vector = r.vsend[...]
     for peer in me.plane:
         vector = vector + r.vplane[peer]
-    r.vsum[...] = vector
+    r.vlast[...] = vector
+    keep(r.vlast, r.vsum)
     q_share.on_diagonal()
     for share in (d_share, u_share, o_spread, q_share):
         share.finish()
+    for copy in kept[settled:]:
+        copy.wait()
     copies.finish()
 
 
@@ -1480,7 +1551,11 @@
 VMEM_SPEC = pl.BlockSpec(memory_space=pltpu.VMEM)
 SPECS = {
     "order": pl.BlockSpec(memory_space=pltpu.SMEM),
-    "wdown": pl.BlockSpec(memory_space=pl.ANY),
+    **{
+        name: pl.BlockSpec(memory_space=pl.ANY)
+        for name in ("h", "g", "wqkv", "wup", "wdown", "wout")
+        + ("hidden_out", "hidden_grad", "fq", "fu", "fd", "fo", "vsum")
+    },
 }
 VMEM_LIMIT = 63 * 1024 * 1024
 
@@ -1516,6 +1591,8 @@
     sides = local_rows // BLK
 
     sums = 5 * shard + qkv_bias.shape[0] + up_bias.shape[0]
+    slices = 3 + hidden // part
+    columns = max(-(-(chip * part % 128 + part) // 128) * 128 for chip in range(chips))
     small = 6 * shard + qkv_bias.shape[0] + up_bias.shape[0]
     rope_r, rope_b = rotary_parts(everyone // BLK)
 
@@ -1579,7 +1656,7 @@
         "dv": ((everyone, part), f32),
         "dqt": ((part, rows), f32),
         "kvin": ((rows, 2 * part), b16),
-        "osent": ((rows // BLK, BLK, width), b16),
+        "otheirs": ((rows // BLK, BLK, width), b16),
         "ogot": ((rows // BLK, BLK, width), b16),
         "oland": ((6, BLK, width), b16),
         "eland": ((6, BLK, width), b16),
@@ -1598,18 +1675,21 @@
         "vout": ((nz, 1, sums), f32),
         "vline": ((nz, 1, sums), f32),
         "vsend": ((1, sums), f32),
+        "vlast": ((1, sums), f32),
+        "gown": ((sides, BLK, width), b16),
+        "win": ((slices, shard, columns), b16),
         "vplane": ((2 * chips, 1, sums), f32),
     }
-    names = [*inputs, *outputs, *scratch, "idx", "send_sems", "recv_sems", "local_sem"]
+    names = [*inputs, *outputs, *scratch, "idx", "send_sems", "recv_sems", "local_sems", "window_sems"]
     results = pl.pallas_call(
         functools.partial(layer_kernel, nz, names),
         out_shape=tuple(jax.ShapeDtypeStruct(*leaf) for leaf in outputs.values()),
         in_specs=[SPECS.get(name, VMEM_SPEC) for name in inputs],
-        out_specs=(VMEM_SPEC,) * len(outputs),
+        out_specs=tuple(SPECS.get(name, VMEM_SPEC) for name in outputs),
         scratch_shapes=[pltpu.VMEM(*leaf) for leaf in scratch.values()]
         + [pltpu.SMEM((64,), jnp.int32)]
         + [pltpu.SemaphoreType.DMA((SEMAPHORES,))] * 2
-        + [pltpu.SemaphoreType.DMA],
+        + [pltpu.SemaphoreType.DMA((16,))] * 2,
         compiler_params=pltpu.CompilerParams(
             collective_id=0, has_side_effects=True, vmem_limit_bytes=VMEM_LIMIT
         ),
@@ -1617,7 +1697,7 @@
     )(*inputs.values())
     hidden_out, hidden_grad, fq, fu, fd, fo, vsum = results
 
-    steps = 4
+    steps = 2
     some, few = shard // steps, local_rows // steps
     inner = half // some
 

time: 123 us -> 120 us (0.976); the launches traced: 121 us -> 120 us
  no operation moved by 1% of the time
where the time goes in v5:
time: 120 us
  Pallas kernels  119 us (99%)
    pallas_call x1, Pallas kernels, sliced_layer(): pl.pallas_call(functools.partial(layer_kernel, nz, names), out_shape=tupl...  113 us
    pallas_call x1, Pallas kernels, sliced_layer(): pl.pallas_call(assemble_kernel, grid=(steps,), out_shape=(jax.ShapeDtypeS...  5.53 us

profile of v5, /device:TPU:1, one launch (start us, length us, event | category | flops | bytes accessed | tf_op | source)
XLA Modules:
  0.0 119.8 jit_solution(2728227245574858077)
XLA Ops:
  0.7 113.4 %layer.1 = (bf16[256,768]{1,0:T(8,128)(2,1)}, f32[256,768]{1,0:T(8,128)}, bf16[2,4,96,576]{3,2,1,0:T(8,128)(2,1)}, bf16[2,4,96,768]{3,2,1,0:T(8,128)(2,1)}, bf16...) custom-call(s32[16]{0:T(128)} %refs_0_.1, bf16[2,128,768]{2,1,0:T(8,128)(2,1)} %bitcast.5, ...), custom_call_target="tpu_custom_call" | custom-call | tf_op jit(solution)/shard_map/layer/pallas_call | solution.py:1684
  114.1 5.5 %assemble.1 = (f32[192,2304]{1,0:T(8,128)}, f32[192,3072]{1,0:T(8,128)}, f32[4,2,96,768]{3,2,1,0:T(8,128)}, f32[192,768]{1,0:T(8,128)}, bf16[256,768]{1,0:T(8,12...) custom-call(bf16[2,4,96,576]{3,2,1,0:T(8,128)(2,1)} %get-tuple-eleme, ...), custom_call_target="tpu_custom_call" | custom-call | tf_op jit(solution)/shard_map/assemble/pallas_call | solution.py:1714

commit v6 on v5

--- a/solution.py
+++ b/solution.py
@@ -1350,7 +1350,6 @@
     attend(r, me, 2)
     wu.advance(2)
     g_share.on_diagonal()
-    attend(r, me, 0)
     wd.advance(2)
     wo.start()
     for copy in kept[1:]:
@@ -1387,6 +1386,7 @@
     up_reduce.start()
     wo.advance()
     down_reduce.pair()
+    attend(r, me, 0)
     attend(r, me, 3)
     up_reduce.pair()
     wo.finish()
@@ -1426,7 +1426,6 @@
     later = send_keys(1)
     attend_grad(r, me, 1)
     sooner = send_keys(0)
-    d_share.relay()
     later.wait_recv()
     e_scatter = Scatter(
         copies, me, r, r.outb, r.gall.at[: r.outb.shape[0]], r.gall.at[r.outb.shape[0] :], r.eland
@@ -1435,6 +1434,7 @@
     @pl.loop(0, tiles)
     def _(number):
         pl.when(number == tiles // 2)(sooner.wait_recv)
+        pl.when(number == tiles // 2)(d_share.relay)
         qkv_grad(r, me, (number + tiles // 2) % tiles)
         pl.when(number > 0)(
             functools.partial(e_scatter.exchange, (number + tiles // 2 - 1) % tiles)

time: 120 us -> 120 us (level)
  no operation moved by 1% of the time
where the time goes in v6:
time: 120 us
  Pallas kernels  119 us (99%)
    pallas_call x1, Pallas kernels, sliced_layer(): pl.pallas_call(functools.partial(layer_kernel, nz, names), out_shape=tupl...  113 us
    pallas_call x1, Pallas kernels, sliced_layer(): pl.pallas_call(assemble_kernel, grid=(steps,), out_shape=(jax.ShapeDtypeS...  5.53 us

profile of v6, /device:TPU:1, one launch (start us, length us, event | category | flops | bytes accessed | tf_op | source)
XLA Modules:
  0.0 119.5 jit_solution(17782847815152944684)
XLA Ops:
  0.7 113.2 %layer.1 = (bf16[256,768]{1,0:T(8,128)(2,1)}, f32[256,768]{1,0:T(8,128)}, bf16[2,4,96,576]{3,2,1,0:T(8,128)(2,1)}, bf16[2,4,96,768]{3,2,1,0:T(8,128)(2,1)}, bf16...) custom-call(s32[16]{0:T(128)} %refs_0_.1, bf16[2,128,768]{2,1,0:T(8,128)(2,1)} %bitcast.5, ...), custom_call_target="tpu_custom_call" | custom-call | tf_op jit(solution)/shard_map/layer/pallas_call | solution.py:1684
  113.8 5.5 %assemble.1 = (f32[192,2304]{1,0:T(8,128)}, f32[192,3072]{1,0:T(8,128)}, f32[4,2,96,768]{3,2,1,0:T(8,128)}, f32[192,768]{1,0:T(8,128)}, bf16[256,768]{1,0:T(8,12...) custom-call(bf16[2,4,96,576]{3,2,1,0:T(8,128)(2,1)} %get-tuple-eleme, ...), custom_call_target="tpu_custom_call" | custom-call | tf_op jit(solution)/shard_map/assemble/pallas_call | solution.py:1714

commit v7 on v6

--- a/solution.py
+++ b/solution.py
@@ -1376,10 +1376,6 @@
         d_share.start()
         keep(r.td.at[me.z], r.fd.at[me.k, me.t])
 
-    def share_up():
-        u_share.start()
-        keep(r.tu.at[me.z], r.fu.at[me.k, me.t])
-
     weight_grad(r.gd, r.act, r.gl)
     down_reduce.start()
     weight_grad(r.gu, r.n, r.du)
@@ -1400,11 +1396,11 @@
     r.go[...] = narrow(mm(r.att[...], r.gl[...], TN))
     out_reduce.start()
     attend_grad(r, me, 0)
-    out_reduce.pair()
     out_scatter.spread()
     attend_grad(r, me, 3)
     out_scatter.middle()
     attend_grad(r, me, 2)
+    out_reduce.pair()
     down_reduce.collect()
     share_down()
     copies.settle([g_share.hop_x, g_share.hop_y, *g_share.swaps])
@@ -1435,13 +1431,14 @@
     def _(number):
         pl.when(number == tiles // 2)(sooner.wait_recv)
         pl.when(number == tiles // 2)(d_share.relay)
+        pl.when(number == tiles - 1)(up_reduce.collect)
+        pl.when(number == tiles - 1)(u_share.start)
         qkv_grad(r, me, (number + tiles // 2) % tiles)
         pl.when(number > 0)(
             functools.partial(e_scatter.exchange, (number + tiles // 2 - 1) % tiles)
         )
 
-    up_reduce.collect()
-    share_up()
+    keep(r.tu.at[me.z], r.fu.at[me.k, me.t])
     gather_sums(r, me)
     e_scatter.exchange(tiles // 2 - 1)
     vec_line = [

time: 120 us -> 120 us (level)
  no operation moved by 1% of the time
where the time goes in v7:
time: 120 us; the launch traced here: 119 us
  Pallas kernels  119 us (99%)
    pallas_call x1, Pallas kernels, sliced_layer(): pl.pallas_call(functools.partial(layer_kernel, nz, names), out_shape=tupl...  113 us
    pallas_call x1, Pallas kernels, sliced_layer(): pl.pallas_call(assemble_kernel, grid=(steps,), out_shape=(jax.ShapeDtypeS...  5.53 us

profile of v7, /device:TPU:1, one launch (start us, length us, event | category | flops | bytes accessed | tf_op | source)
XLA Modules:
  0.0 119.4 jit_solution(3923167029152044020)
XLA Ops:
  0.7 113.1 %layer.1 = (bf16[256,768]{1,0:T(8,128)(2,1)}, f32[256,768]{1,0:T(8,128)}, bf16[2,4,96,576]{3,2,1,0:T(8,128)(2,1)}, bf16[2,4,96,768]{3,2,1,0:T(8,128)(2,1)}, bf16...) custom-call(s32[16]{0:T(128)} %refs_0_.1, bf16[2,128,768]{2,1,0:T(8,128)(2,1)} %bitcast.5, ...), custom_call_target="tpu_custom_call" | custom-call | tf_op jit(solution)/shard_map/layer/pallas_call | solution.py:1681
  113.7 5.5 %assemble.1 = (f32[192,2304]{1,0:T(8,128)}, f32[192,3072]{1,0:T(8,128)}, f32[4,2,96,768]{3,2,1,0:T(8,128)}, f32[192,768]{1,0:T(8,128)}, bf16[256,768]{1,0:T(8,12...) custom-call(bf16[2,4,96,576]{3,2,1,0:T(8,128)(2,1)} %get-tuple-eleme, ...), custom_call_target="tpu_custom_call" | custom-call | tf_op jit(solution)/shard_map/assemble/pallas_call | solution.py:1711
